TPU v7x, 32 devices: a whole 2x2x4 slice. The times are simulated.
32 devices in a mesh: groups: 2 (over y), space: 16 (over z, x, core).
Axes of the slice: x: 2, y: 2, z: 4, core: 2. Of those that a mesh axis runs over, the one named last changes fastest.
Arguments:
- wavefield: bfloat16 [8192, 1024], P(('groups', 'space')), parts along dimension 0, may hold values from -6 to 6
- redatum_taps: float32 [512, 65], P('groups'), parts along dimension 0, may hold values from -0.75 to 0.75
- cell_x: int32 [5, 16384], replicated, may hold values from 0 to 4095
- cell_depth: int32 [16384], replicated, may hold values from 1 to 511
- slowness: float32 [4], replicated, may hold values from 0.02 to 0.2
- illumination: float32 [32768], P('groups'), parts along dimension 0, may hold values from 0.3 to 3
- aperture: int32 [8192, 1024], P(('groups', 'space')), parts along dimension 0, may hold values 0 or 1
Outputs:
- image: float32 [32, 1024], P(('groups', 'space')), parts along dimension 0
There are 2 independent parts, one for each index of `groups`. A program takes and returns all parts, laid end to end along the dimension named above; an argument that names none is the same for every part. Nothing has to cross between parts.
All inputs are finite; a program needn't handle non-finite values. No bound on the sum of `aperture` on one device may be relied on, other than what follows from the above.
Results may differ from a plain program's by a relative error of at most 0.0075.
Values may be sent and summed in bfloat16 or wider, within the bound.
No kernel may reach another device: no remote copies, remote signals or barrier semaphores. Data moves between devices by JAX's collectives and lax.ppermute only.
A program may use at most 64 MiB of HBM per device.

v0:
```python
import jax
import jax.numpy as jnp
from jax import lax
from jax.sharding import PartitionSpec as P

LEVELS = 4
BOXES = 16


column_block = 256


def passed_along(shard, axis, by):
    devices = lax.axis_size(axis)
    pairs = [(i, i + by) for i in range(devices) if 0 <= i + by < devices]
    return lax.ppermute(shard, axis, pairs)


def partner(shard, axis, bit):
    return lax.ppermute(shard, axis, [(i, i ^ 1 << bit) for i in range(lax.axis_size(axis))])


def translator(rows_x, cols_x, cols_depth, slow, width):
    across = (rows_x[:, None] - cols_x[None, :]).astype(jnp.float32)
    depth = cols_depth.astype(jnp.float32)[None, :]
    travel = jnp.sqrt(across * across + depth * depth)
    return (jnp.cos(slow * travel) / jnp.sqrt(jnp.float32(width))).astype(jnp.bfloat16)


def redatum(padded, taps, width):
    total = taps[..., 0:1] * padded[..., 0:width]
    for shift in range(1, taps.shape[-1]):
        total = total + taps[..., shift : shift + 1] * padded[..., shift : shift + width]
    return total


def translate(left, rows_x, cols_x, cols_depth, slow, width):
    step = min(column_block, cols_x.shape[0])
    pieces = []
    for start in range(0, cols_x.shape[0], step):
        table = translator(
            rows_x, cols_x[start : start + step], cols_depth[start : start + step], slow, width
        )
        pieces.append(jnp.dot(left, table, preferred_element_type=jnp.float32))
    return jnp.concatenate(pieces, 1)


def on_device(wavefield, redatum_taps, cell_x, cell_depth, slowness, illumination, aperture):
    index = lax.axis_index("space")
    devices = lax.axis_size("space")
    blocks = devices // BOXES
    block_bits = blocks.bit_length() - 1
    box = index // blocks
    block = index % blocks
    count = wavefield.shape[0]
    width = wavefield.shape[1]
    reach = (redatum_taps.shape[1] - 1) // 2
    below = passed_along(wavefield[:, width - reach :], "space", blocks)
    above = passed_along(wavefield[:, :reach], "space", -blocks)
    padded = jnp.concatenate([below, wavefield, above], 1).astype(jnp.float32)
    taps = lax.dynamic_slice_in_dim(redatum_taps, block * count, count, 0)
    state = redatum(padded, taps, width).astype(jnp.bfloat16)
    for level in range(LEVELS):
        bit = 1 << level
        upper = box // bit % 2 == 1
        lower_box = box - jnp.where(upper, bit, 0)
        rows_low = lax.dynamic_slice_in_dim(cell_x[level], lower_box * width, width)
        rows_high = lax.dynamic_slice_in_dim(cell_x[level], (lower_box + bit) * width, width)
        cols_x = lax.dynamic_slice_in_dim(cell_x[level + 1], box * width, width)
        cols_depth = lax.dynamic_slice_in_dim(cell_depth, box * width, width)
        slow = slowness[level]
        paired_box = box + jnp.where(upper, -bit, bit)
        own_rows = jnp.where(upper, rows_high, rows_low)
        far_x = lax.dynamic_slice_in_dim(cell_x[level + 1], paired_box * width, width)
        far_depth = lax.dynamic_slice_in_dim(cell_depth, paired_box * width, width)
        far_term = translate(state, own_rows, far_x, far_depth, slow, width)
        own_term = translate(state, own_rows, cols_x, cols_depth, slow, width)
        mixed = own_term + partner(far_term, "space", level + block_bits)
        state = mixed.astype(jnp.bfloat16) if level + 1 < LEVELS else mixed
    summed = jnp.sum(jnp.where(aperture > 0, state, jnp.zeros_like(state)), 0)
    weights = lax.dynamic_slice_in_dim(illumination, box * width, width)
    partial_image = summed * weights / jnp.sqrt(jnp.float32(count * blocks))
    for level in range(block_bits):
        partial_image = partial_image + partner(partial_image, "space", level)
    share = width // blocks
    image = lax.dynamic_slice_in_dim(partial_image, block * share, share)
    return image[None, :]


def solution(mesh):
    placed = (
        P(("groups", "space"), None),
        P("groups", None),
        P(),
        P(),
        P(),
        P("groups"),
        P(("groups", "space"), None),
    )
    return jax.shard_map(
        on_device,
        mesh=mesh,
        in_specs=placed,
        out_specs=P(("groups", "space"), None),
        check_vma=False,
    )
```

profile of v0, /device:TPU:0, one launch (start us, length us, event | category | flops | bytes accessed | tf_op | source)
XLA Modules:
  0.0 239.7 jit_solution(9726554810114574971)
XLA Ops:
  13.7 23.1 %fusion.1 = bf16[256,1024]{1,0:T(8,128)(2,1)S(1)} fusion(f32[256,1088]{1,0:T(8,128)S(1)} %convert_element_type.279, f32[256]{0:T(256)S(1)} %bitcast.176, f32[256]{0:T(256)S(1)} %bitcast.177, f32[256]{0:T(256)S(1)} %bitcast.179, f32[256]{0:T(256)S(1)} %bitcast.180, f32[256]{0:T(256)S(1)} %bitcast.181, f32[256]{0:T(256)S(1)} %bitcast.182, f32[256]{0:T(256)S(1)} %bitcast.183, ...), kind=kLoop, calls=%fused_computation.2 | loop fusion | flops 34078720 | bytes 68748288 | tf_op jit(solution)/shard_map/convert_element_type | solution.py:62
  36.8 4.7 %fusion.77 = f32[256,256]{0,1:T(8,128)S(1)} fusion(bf16[256,1024]{1,0:T(8,128)(2,1)S(1)} %fusion.1, f32[256]{0:T(256)S(1)} %get-tuple-element.131, s32[256]{0:T(256)S(1)} %bitcast.266, s32[1024]{0:T(1024)S(1)} %bitcast.138, f32[]{:T(128)} %bitcast.65), kind=kOutput, calls=%fused_computation.182 | convolution fusion | flops 136052736 | bytes 792580 | tf_op jit(solution)/shard_map/dot_general | solution.py:44
  41.5 4.7 %fusion.76 = f32[256,256]{0,1:T(8,128)S(1)} fusion(bf16[256,1024]{1,0:T(8,128)(2,1)S(1)} %fusion.1, f32[256]{0:T(256)S(1)} %get-tuple-element.132, s32[256]{0:T(256)S(1)} %bitcast.265, s32[1024]{0:T(1024)S(1)} %bitcast.139, f32[]{:T(128)} %bitcast.65), kind=kOutput, calls=%fused_computation.181 | convolution fusion | flops 136052736 | bytes 792580 | tf_op jit(solution)/shard_map/dot_general | solution.py:44
  46.2 5.2 %fusion.75 = f32[256,256]{0,1:T(8,128)S(1)} fusion(bf16[256,1024]{1,0:T(8,128)(2,1)S(1)} %fusion.1, f32[256]{0:T(256)S(1)} %get-tuple-element.133, s32[256]{0:T(256)S(1)} %bitcast.264, s32[1024]{0:T(1024)S(1)} %bitcast.140, f32[]{:T(128)} %bitcast.65), kind=kOutput, calls=%fused_computation.180 | convolution fusion | flops 136052736 | bytes 792580 | tf_op jit(solution)/shard_map/dot_general | solution.py:44
  51.5 4.7 %fusion.74 = f32[256,256]{0,1:T(8,128)S(1)} fusion(bf16[256,1024]{1,0:T(8,128)(2,1)S(1)} %fusion.1, f32[256]{0:T(256)S(1)} %get-tuple-element.130, s32[256]{0:T(256)S(1)} %bitcast.263, s32[1024]{0:T(1024)S(1)} %bitcast.141, f32[]{:T(128)} %bitcast.65), kind=kOutput, calls=%fused_computation.179 | convolution fusion | flops 136052736 | bytes 792580 | tf_op jit(solution)/shard_map/dot_general | solution.py:44
  59.6 4.7 %fusion.73 = f32[256,256]{0,1:T(8,128)S(1)} fusion(bf16[256,1024]{1,0:T(8,128)(2,1)S(1)} %fusion.1, f32[256]{0:T(256)S(1)} %get-tuple-element.127, s32[256]{0:T(256)S(1)} %bitcast.262, s32[1024]{0:T(1024)S(1)} %bitcast.142, f32[]{:T(128)} %bitcast.65), kind=kOutput, calls=%fused_computation.178 | convolution fusion | flops 136052736 | bytes 792580 | tf_op jit(solution)/shard_map/dot_general | solution.py:44
  64.3 4.9 %fusion.72 = f32[256,256]{0,1:T(8,128)S(1)} fusion(bf16[256,1024]{1,0:T(8,128)(2,1)S(1)} %fusion.1, f32[256]{0:T(256)S(1)} %get-tuple-element.128, s32[256]{0:T(256)S(1)} %bitcast.261, s32[1024]{0:T(1024)S(1)} %bitcast.143, f32[]{:T(128)} %bitcast.65), kind=kOutput, calls=%fused_computation.177 | convolution fusion | flops 136052736 | bytes 792580 | tf_op jit(solution)/shard_map/dot_general | solution.py:44
  69.2 4.7 %fusion.71 = f32[256,256]{0,1:T(8,128)S(1)} fusion(bf16[256,1024]{1,0:T(8,128)(2,1)S(1)} %fusion.1, f32[256]{0:T(256)S(1)} %get-tuple-element.129, s32[256]{0:T(256)S(1)} %bitcast.260, s32[1024]{0:T(1024)S(1)} %bitcast.144, f32[]{:T(128)} %bitcast.65), kind=kOutput, calls=%fused_computation.176 | convolution fusion | flops 136052736 | bytes 792580 | tf_op jit(solution)/shard_map/dot_general | solution.py:44
  73.9 4.7 %fusion.70 = f32[256,256]{0,1:T(8,128)S(1)} fusion(bf16[256,1024]{1,0:T(8,128)(2,1)S(1)} %fusion.1, f32[256]{0:T(256)S(1)} %get-tuple-element.126, s32[256]{0:T(256)S(1)} %bitcast.259, s32[1024]{0:T(1024)S(1)} %bitcast.145, f32[]{:T(128)} %bitcast.65), kind=kOutput, calls=%fused_computation.175 | convolution fusion | flops 136052736 | bytes 792580 | tf_op jit(solution)/shard_map/dot_general | solution.py:44
  78.8 4.9 %fusion.85 = f32[256,256]{0,1:T(8,128)S(1)} fusion(bf16[256,1024]{0,1:T(8,128)(2,1)S(1)} %fusion.65, f32[256]{0:T(256)S(1)} %get-tuple-element.123, s32[256]{0:T(256)S(1)} %bitcast.258, s32[1024]{0:T(1024)S(1)} %bitcast.146, f32[]{:T(128)} %bitcast.75), kind=kOutput, calls=%fused_computation.190 | convolution fusion | flops 136052736 | bytes 792580 | tf_op jit(solution)/shard_map/dot_general | solution.py:44
  83.8 4.7 %fusion.84 = f32[256,256]{0,1:T(8,128)S(1)} fusion(bf16[256,1024]{0,1:T(8,128)(2,1)S(1)} %fusion.65, f32[256]{0:T(256)S(1)} %get-tuple-element.124, s32[256]{0:T(256)S(1)} %bitcast.257, s32[1024]{0:T(1024)S(1)} %bitcast.147, f32[]{:T(128)} %bitcast.75), kind=kOutput, calls=%fused_computation.189 | convolution fusion | flops 136052736 | bytes 792580 | tf_op jit(solution)/shard_map/dot_general | solution.py:44
  93.2 5.1 %fusion.82 = f32[256,256]{0,1:T(8,128)S(1)} fusion(bf16[256,1024]{0,1:T(8,128)(2,1)S(1)} %fusion.65, f32[256]{0:T(256)S(1)} %get-tuple-element.122, s32[256]{0:T(256)S(1)} %bitcast.255, s32[1024]{0:T(1024)S(1)} %bitcast.149, f32[]{:T(128)} %bitcast.75), kind=kOutput, calls=%fused_computation.187 | convolution fusion | flops 136052736 | bytes 792580 | tf_op jit(solution)/shard_map/dot_general | solution.py:44
  104.8 4.7 %fusion.80 = f32[256,256]{0,1:T(8,128)S(1)} fusion(bf16[256,1024]{0,1:T(8,128)(2,1)S(1)} %fusion.65, s32[256]{0:T(256)S(1)} %bitcast.253, s32[1024]{0:T(1024)S(1)} %bitcast.151, f32[]{:T(128)} %bitcast.75, f32[256]{0:T(256)S(1)} %get-tuple-element.128), kind=kOutput, calls=%fused_computation.185 | convolution fusion | flops 136052736 | bytes 792580 | tf_op jit(solution)/shard_map/dot_general | solution.py:44
  109.5 4.9 %fusion.79 = f32[256,256]{0,1:T(8,128)S(1)} fusion(bf16[256,1024]{0,1:T(8,128)(2,1)S(1)} %fusion.65, s32[256]{0:T(256)S(1)} %bitcast.252, s32[1024]{0:T(1024)S(1)} %bitcast.152, f32[]{:T(128)} %bitcast.75, f32[256]{0:T(256)S(1)} %get-tuple-element.129), kind=kOutput, calls=%fused_computation.184 | convolution fusion | flops 136052736 | bytes 792580 | tf_op jit(solution)/shard_map/dot_general | solution.py:44
  119.1 4.8 %collective-permute-done.3 = f32[256,1024]{0,1:T(8,128)S(1)} collective-permute-done((f32[256,1024]{0,1:T(8,128)S(1)}, f32[256,1024]{0,1:T(8,128)S(1)}, u32[]{:S(2)}, u32[]{:S(2)}) %collective-permute-start.3) | collective-permute-done | bytes 1048608 | tf_op jit(solution)/shard_map/ppermute | solution.py:20
  124.1 4.8 %fusion.93 = f32[256,256]{0,1:T(8,128)S(1)} fusion(bf16[256,1024]{0,1:T(8,128)(2,1)S(1)} %fusion.66, f32[256]{0:T(256)S(1)} %get-tuple-element.119, s32[256]{0:T(256)S(1)} %bitcast.250, s32[1024]{0:T(1024)S(1)} %bitcast.162, f32[]{:T(128)} %bitcast.85), kind=kOutput, calls=%fused_computation.198 | convolution fusion | flops 136052736 | bytes 792580 | tf_op jit(solution)/shard_map/dot_general | solution.py:44
  128.8 5.0 %fusion.92 = f32[256,256]{0,1:T(8,128)S(1)} fusion(bf16[256,1024]{0,1:T(8,128)(2,1)S(1)} %fusion.66, f32[256]{0:T(256)S(1)} %get-tuple-element.120, s32[256]{0:T(256)S(1)} %bitcast.249, s32[1024]{0:T(1024)S(1)} %bitcast.163, f32[]{:T(128)} %bitcast.85), kind=kOutput, calls=%fused_computation.197 | convolution fusion | flops 136052736 | bytes 792580 | tf_op jit(solution)/shard_map/dot_general | solution.py:44
  133.8 4.8 %fusion.91 = f32[256,256]{0,1:T(8,128)S(1)} fusion(bf16[256,1024]{0,1:T(8,128)(2,1)S(1)} %fusion.66, f32[256]{0:T(256)S(1)} %get-tuple-element.121, s32[256]{0:T(256)S(1)} %bitcast.248, s32[1024]{0:T(1024)S(1)} %bitcast.164, f32[]{:T(128)} %bitcast.85), kind=kOutput, calls=%fused_computation.196 | convolution fusion | flops 136052736 | bytes 792580 | tf_op jit(solution)/shard_map/dot_general | solution.py:44
  138.6 5.2 %fusion.90 = f32[256,256]{0,1:T(8,128)S(1)} fusion(bf16[256,1024]{0,1:T(8,128)(2,1)S(1)} %fusion.66, f32[256]{0:T(256)S(1)} %get-tuple-element.118, s32[256]{0:T(256)S(1)} %bitcast.247, s32[1024]{0:T(1024)S(1)} %bitcast.165, f32[]{:T(128)} %bitcast.85), kind=kOutput, calls=%fused_computation.195 | convolution fusion | flops 136052736 | bytes 792580 | tf_op jit(solution)/shard_map/dot_general | solution.py:44
  146.6 4.8 %fusion.89 = f32[256,256]{0,1:T(8,128)S(1)} fusion(bf16[256,1024]{0,1:T(8,128)(2,1)S(1)} %fusion.66, s32[256]{0:T(256)S(1)} %bitcast.246, s32[1024]{0:T(1024)S(1)} %bitcast.166, f32[]{:T(128)} %bitcast.85, f32[256]{0:T(256)S(1)} %get-tuple-element.127), kind=kOutput, calls=%fused_computation.194 | convolution fusion | flops 136052736 | bytes 792580 | tf_op jit(solution)/shard_map/dot_general | solution.py:44
  151.4 4.8 %fusion.88 = f32[256,256]{0,1:T(8,128)S(1)} fusion(bf16[256,1024]{0,1:T(8,128)(2,1)S(1)} %fusion.66, s32[256]{0:T(256)S(1)} %bitcast.245, s32[1024]{0:T(1024)S(1)} %bitcast.167, f32[]{:T(128)} %bitcast.85, f32[256]{0:T(256)S(1)} %get-tuple-element.128), kind=kOutput, calls=%fused_computation.193 | convolution fusion | flops 136052736 | bytes 792580 | tf_op jit(solution)/shard_map/dot_general | solution.py:44
  156.2 4.9 %fusion.87 = f32[256,256]{0,1:T(8,128)S(1)} fusion(bf16[256,1024]{0,1:T(8,128)(2,1)S(1)} %fusion.66, s32[256]{0:T(256)S(1)} %bitcast.244, s32[1024]{0:T(1024)S(1)} %bitcast.168, f32[]{:T(128)} %bitcast.85, f32[256]{0:T(256)S(1)} %get-tuple-element.129), kind=kOutput, calls=%fused_computation.192 | convolution fusion | flops 136052736 | bytes 792580 | tf_op jit(solution)/shard_map/dot_general | solution.py:44
  161.1 4.8 %fusion.86 = f32[256,256]{0,1:T(8,128)S(1)} fusion(bf16[256,1024]{0,1:T(8,128)(2,1)S(1)} %fusion.66, s32[256]{0:T(256)S(1)} %bitcast.243, s32[1024]{0:T(1024)S(1)} %bitcast.169, f32[]{:T(128)} %bitcast.85, f32[256]{0:T(256)S(1)} %get-tuple-element.126), kind=kOutput, calls=%fused_computation.191 | convolution fusion | flops 136052736 | bytes 792580 | tf_op jit(solution)/shard_map/dot_general | solution.py:44
  169.8 4.8 %fusion.101 = f32[256,256]{0,1:T(8,128)S(1)} fusion(bf16[256,1024]{0,1:T(8,128)(2,1)S(1)} %fusion.67, f32[256]{0:T(256)S(1)} %get-tuple-element.115, s32[256]{0:T(256)S(1)} %bitcast.242, s32[1024]{0:T(1024)S(1)} %bitcast.154, f32[]{:T(128)} %bitcast.95), kind=kOutput, calls=%fused_computation.206 | convolution fusion | flops 136052736 | bytes 792580 | tf_op jit(solution)/shard_map/dot_general | solution.py:44
  174.5 4.9 %fusion.100 = f32[256,256]{0,1:T(8,128)S(1)} fusion(bf16[256,1024]{0,1:T(8,128)(2,1)S(1)} %fusion.67, f32[256]{0:T(256)S(1)} %get-tuple-element.116, s32[256]{0:T(256)S(1)} %bitcast.241, s32[1024]{0:T(1024)S(1)} %bitcast.155, f32[]{:T(128)} %bitcast.95), kind=kOutput, calls=%fused_computation.205 | convolution fusion | flops 136052736 | bytes 792580 | tf_op jit(solution)/shard_map/dot_general | solution.py:44
  179.5 4.7 %fusion.99 = f32[256,256]{0,1:T(8,128)S(1)} fusion(bf16[256,1024]{0,1:T(8,128)(2,1)S(1)} %fusion.67, f32[256]{0:T(256)S(1)} %get-tuple-element.117, s32[256]{0:T(256)S(1)} %bitcast.240, s32[1024]{0:T(1024)S(1)} %bitcast.156, f32[]{:T(128)} %bitcast.95), kind=kOutput, calls=%fused_computation.204 | convolution fusion | flops 136052736 | bytes 792580 | tf_op jit(solution)/shard_map/dot_general | solution.py:44
  184.2 4.7 %fusion.98 = f32[256,256]{0,1:T(8,128)S(1)} fusion(bf16[256,1024]{0,1:T(8,128)(2,1)S(1)} %fusion.67, f32[256]{0:T(256)S(1)} %get-tuple-element.114, s32[256]{0:T(256)S(1)} %bitcast.239, s32[1024]{0:T(1024)S(1)} %bitcast.157, f32[]{:T(128)} %bitcast.95), kind=kOutput, calls=%fused_computation.203 | convolution fusion | flops 136052736 | bytes 792580 | tf_op jit(solution)/shard_map/dot_general | solution.py:44
  192.2 6.2 %fusion.97 = f32[256,256]{0,1:T(8,128)S(1)} fusion(bf16[256,1024]{0,1:T(8,128)(2,1)} %copy-done.2, s32[256]{0:T(256)S(1)} %bitcast.238, s32[1024]{0:T(1024)S(1)} %bitcast.158, f32[]{:T(128)} %bitcast.95, f32[256]{0:T(256)S(1)} %get-tuple-element.127), kind=kOutput, calls=%fused_computation.202 | convolution fusion | flops 136052736 | bytes 792580 | tf_op jit(solution)/shard_map/dot_general | solution.py:44
  198.4 4.7 %fusion.96 = f32[256,256]{0,1:T(8,128)S(1)} fusion(bf16[256,1024]{0,1:T(8,128)(2,1)S(1)} %copy-done.3, s32[256]{0:T(256)S(1)} %bitcast.237, s32[1024]{0:T(1024)S(1)} %bitcast.159, f32[]{:T(128)} %bitcast.95, f32[256]{0:T(256)S(1)} %get-tuple-element.128), kind=kOutput, calls=%fused_computation.201 | convolution fusion | flops 136052736 | bytes 792580 | tf_op jit(solution)/shard_map/dot_general | solution.py:44
  203.2 4.7 %fusion.95 = f32[256,256]{0,1:T(8,128)S(1)} fusion(bf16[256,1024]{0,1:T(8,128)(2,1)S(1)} %copy-done.3, s32[256]{0:T(256)S(1)} %bitcast.236, s32[1024]{0:T(1024)S(1)} %bitcast.160, f32[]{:T(128)} %bitcast.95, f32[256]{0:T(256)S(1)} %get-tuple-element.129), kind=kOutput, calls=%fused_computation.200 | convolution fusion | flops 136052736 | bytes 792580 | tf_op jit(solution)/shard_map/dot_general | solution.py:44
  207.9 4.9 %fusion.94 = f32[256,256]{0,1:T(8,128)S(1)} fusion(bf16[256,1024]{0,1:T(8,128)(2,1)S(1)} %copy-done.3, s32[256]{0:T(256)S(1)} %bitcast.235, s32[1024]{0:T(1024)S(1)} %bitcast.161, f32[]{:T(128)} %bitcast.95, f32[256]{0:T(256)S(1)} %get-tuple-element.126), kind=kOutput, calls=%fused_computation.199 | convolution fusion | flops 136052736 | bytes 792580 | tf_op jit(solution)/shard_map/dot_general | solution.py:44
  212.8 23.9 %collective-permute-done.5 = f32[256,1024]{0,1:T(8,128)} collective-permute-done((f32[256,1024]{0,1:T(8,128)S(1)}, f32[256,1024]{0,1:T(8,128)}, u32[]{:S(2)}, u32[]{:S(2)}) %collective-permute-start.5) | collective-permute-done | bytes 1048608 | tf_op jit(solution)/shard_map/ppermute | solution.py:20
  (54 shorter events, 45.7 us)
Async XLA Ops:
  0.0 12.9 %copy-start.1 = (bf16[256,1024]{1,0:T(8,128)(2,1)S(1)}, bf16[256,1024]{1,0:T(8,128)(2,1)}, u32[]{:S(2)}) copy-start(bf16[256,1024]{1,0:T(8,128)(2,1)} %param.7) | copy-start | bytes 1572868
  0.0 11.9 %copy-start.4 = (f32[4]{0:T(128)S(1)}, f32[4]{0:T(128)}, u32[]{:S(2)}) copy-start(f32[4]{0:T(128)} %param.11) | copy-start | bytes 52
  1.0 11.9 %collective-permute-start = (bf16[256,32]{1,0:T(8,128)(2,1)S(1)}, bf16[256,32]{1,0:T(8,128)(2,1)S(1)}, u32[]{:S(2)}, u32[]{:S(2)}) collective-permute-start(bf16[256,32]{1,0:T(8,128)(2,1)S(1)} %get-tuple-element.11), channel_id=1, source_target_pairs={{0,1},{1,2},{2,3},{3,4},{4,5},{5,6},{6,7},{7,8},{8,9},{9,10},{10,1... | collective-permute-start | bytes 49160 | tf_op jit(solution)/shard_map/ppermute | solution.py:16
  3.4 9.5 %collective-permute-start.1 = (bf16[256,32]{1,0:T(8,128)(2,1)S(1)}, bf16[256,32]{1,0:T(8,128)(2,1)S(1)}, u32[]{:S(2)}, u32[]{:S(2)}) collective-permute-start(bf16[256,32]{1,0:T(8,128)(2,1)S(1)} %get-tuple-element.10), channel_id=1, source_target_pairs={{1,0},{2,1},{3,2},{4,3},{5,4},{6,5},{7,6},{8,7},{9,8},{10,9},{11,1... | collective-permute-start | bytes 49160 | tf_op jit(solution)/shard_map/ppermute | solution.py:16
  56.3 22.4 %collective-permute-start.2 = (f32[256,1024]{0,1:T(8,128)S(1)}, f32[256,1024]{0,1:T(8,128)S(1)}, u32[]{:S(2)}, u32[]{:S(2)}) collective-permute-start(f32[256,1024]{0,1:T(8,128)S(1)} %pad_maximum_fusion), channel_id=1, source_target_pairs={{0,1},{1,0},{2,3},{3,2},{4,5},{5,4},{6,7},{7,6},{8,9},{9,8},{10,11... | collective-permute-start | bytes 3145736 | tf_op jit(solution)/shard_map/ppermute | solution.py:20
  98.4 25.5 %collective-permute-start.3 = (f32[256,1024]{0,1:T(8,128)S(1)}, f32[256,1024]{0,1:T(8,128)S(1)}, u32[]{:S(2)}, u32[]{:S(2)}) collective-permute-start(f32[256,1024]{0,1:T(8,128)S(1)} %pad_maximum_fusion.1), channel_id=1, source_target_pairs={{0,2},{1,3},{2,0},{3,1},{4,6},{5,7},{6,4},{7,5},{8,10},{9,11},{10,... | collective-permute-start | bytes 3145736 | tf_op jit(solution)/shard_map/ppermute | solution.py:20
  143.8 25.7 %collective-permute-start.4 = (f32[256,1024]{0,1:T(8,128)S(1)}, f32[256,1024]{0,1:T(8,128)S(1)}, u32[]{:S(2)}, u32[]{:S(2)}) collective-permute-start(f32[256,1024]{0,1:T(8,128)S(1)} %pad_maximum_fusion.2), channel_id=1, source_target_pairs={{0,4},{1,5},{2,6},{3,7},{4,0},{5,1},{6,2},{7,3},{8,12},{9,13},{10,... | collective-permute-start | bytes 3145736 | tf_op jit(solution)/shard_map/ppermute | solution.py:20
  169.8 14.4 %copy-start.2 = (bf16[256,1024]{0,1:T(8,128)(2,1)}, bf16[256,1024]{0,1:T(8,128)(2,1)S(1)}, u32[]{:S(2)}) copy-start(bf16[256,1024]{0,1:T(8,128)(2,1)S(1)} %fusion.67) | copy-start | bytes 1572868
  189.0 2.9 %copy-start = (s32[256,1024]{1,0:T(8,128)S(1)}, s32[256,1024]{1,0:T(8,128)}, u32[]{:S(2)}) copy-start(s32[256,1024]{1,0:T(8,128)} %param.13) | copy-start | bytes 3145732
  189.0 47.6 %collective-permute-start.5 = (f32[256,1024]{0,1:T(8,128)S(1)}, f32[256,1024]{0,1:T(8,128)}, u32[]{:S(2)}, u32[]{:S(2)}) collective-permute-start(f32[256,1024]{0,1:T(8,128)S(1)} %pad_maximum_fusion.3), channel_id=1, source_target_pairs={{0,8},{1,9},{2,10},{3,11},{4,12},{5,13},{6,14},{7,15},{8,0},{9,1},... | collective-permute-start | bytes 3145736 | tf_op jit(solution)/shard_map/ppermute | solution.py:20
  192.2 6.2 %copy-start.3 = (bf16[256,1024]{0,1:T(8,128)(2,1)S(1)}, bf16[256,1024]{0,1:T(8,128)(2,1)}, u32[]{:S(2)}) copy-start(bf16[256,1024]{0,1:T(8,128)(2,1)} %copy-done.2) | copy-start | bytes 1572868
where the time goes:
time: 244 us; the launch traced here: 240 us
  matrix products  155 us (64%)
  waiting for transfers between devices  32.3 us (13%)
  other arithmetic  26.8 us (11%)
  starting transfers between devices  14.3 us (6%)
  local copies, waits for them, and re-layouts  9.83 us (4%)
    dot_general x32, matrix products, translate(): pieces.append(jnp.dot(left, table, preferred_element_type=jnp.float32))  155 us
    ppermute x4, waiting for transfers between devices, partner(): lax.ppermute(shard, axis, [(i, i ^ 1 << bit) for i in range(lax.axis_size...  32.3 us
    convert_element_type x1, other arithmetic, on_device(): state = redatum(padded, taps, width).astype(jnp.bfloat16)  23.1 us
    ppermute x4, starting transfers between devices, partner(): lax.ppermute(shard, axis, [(i, i ^ 1 << bit) for i in range(lax.axis_size...  10.6 us
  transfers between devices with their start and end apart: 6, of which 3 were waited for; matrix products, arithmetic and copies ran while one was open for 36% of the time, Pallas kernels for 0%

commit v1 on v0

v1 whole, which is shorter than its diff:
```python
import functools
import math

import jax
import jax.numpy as jnp
from jax import lax
from jax.experimental import pallas as pl
from jax.experimental.pallas import tpu as pltpu
from jax.sharding import PartitionSpec as P

LEVELS = 4
BOXES = 16
LANES = 128
SUBLANES = 8

POLY_A = -0.55846636
POLY_B = 0.08535978
SCALE = -73.58594804
PIECES = 16
VMEM = pl.BlockSpec(memory_space=pltpu.VMEM)
SMEM = pl.BlockSpec(memory_space=pltpu.SMEM)


def params(mib):
    return pltpu.CompilerParams(vmem_limit_bytes=mib << 20)


def cost(flops, moved, transcendentals=0):
    return pl.CostEstimate(flops=flops, bytes_accessed=moved, transcendentals=transcendentals)


def passed_along(shard, axis, by):
    devices = lax.axis_size(axis)
    pairs = [(i, i + by) for i in range(devices) if 0 <= i + by < devices]
    return lax.ppermute(shard, axis, pairs)


def partner(shard, axis, bit):
    return lax.ppermute(shard, axis, [(i, i ^ 1 << bit) for i in range(lax.axis_size(axis))])


def digits(value, count):
    parts = []
    for place in range(count - 1, 0, -1):
        base = float(256**place)
        part = jnp.floor(value * (1.0 / base)) * base
        parts.append(part)
        value = value - part
    return parts + [value]


def row_pieces(x):
    x = x - 2048.0
    high = jnp.floor(x * (1.0 / 64.0)) * 64.0
    low = x - high
    one = jnp.ones_like(x)
    return [high, high, low, low] + digits(x * x, 3) + [one, one, one]


def column_pieces(x, depth):
    x = x - 2048.0
    high = jnp.floor(x * (1.0 / 64.0)) * 64.0
    low = x - high
    one = jnp.ones_like(x)
    squares = digits(x * x + depth * depth, 3)
    return [-2 * high, -2 * low, -2 * high, -2 * low, one, one, one] + squares


def stack_rows(ref, rows):
    ref[...] = jnp.zeros_like(ref)
    for k, row in enumerate(rows):
        ref[k : k + 1, :] = row


def cosine(squared, turns):
    u = (squared * lax.rsqrt(squared)) * turns
    r = u - jnp.round(u)
    w = jnp.abs(r) - 0.25
    q = w * w
    return w * ((q + POLY_A) * q + POLY_B)


def boxes_of(level, blocks):
    box = lax.axis_index("space") // blocks
    bit = 1 << level
    upper = (box // bit) % 2
    return box, box + bit - 2 * bit * upper


def tables_kernel(level, blocks, step, cell_x, cell_depth, slowness, near, far, piece, rows_b, cols_b):
    width = near.shape[0]
    last = level + 1 == LEVELS
    box, other = boxes_of(level, blocks)
    turns = slowness[level] * (0.5 / math.pi)

    def at(which):
        return pl.ds(pl.multiple_of(which * width, width), width)

    def rows_of(which):
        stack_rows(piece, row_pieces(cell_x[level : level + 1, at(which)].astype(jnp.float32)))
        rows_b[...] = piece[...].T.astype(jnp.bfloat16)

    def columns_of(which):
        x = cell_x[level + 1 : level + 2, at(which)].astype(jnp.float32)
        depth = cell_depth[pl.ds(which, 1), :].astype(jnp.float32)
        stack_rows(piece, column_pieces(x, depth))
        cols_b[...] = piece[...].astype(jnp.bfloat16)

    for out, row_box, column_box in ((near, box, box), (far, box if last else other, other if last else box)):
        if out is near or not last:
            rows_of(row_box)
        if out is near or last:
            columns_of(column_box)

        @pl.loop(0, width // step)
        def _(i):
            rows = pl.ds(pl.multiple_of(i * step, step), step)
            squared = jnp.dot(rows_b[rows, :], cols_b[...], preferred_element_type=jnp.float32)
            out[rows, :] = cosine(squared, turns).astype(jnp.bfloat16)


def tables(level, blocks, width, cell_x, cell_depth, slowness):
    shape = jax.ShapeDtypeStruct((width, width), jnp.bfloat16)
    return pl.pallas_call(
        functools.partial(tables_kernel, level, blocks, min(width, 128)),
        out_shape=(shape, shape),
        in_specs=[VMEM, VMEM, SMEM],
        out_specs=(VMEM, VMEM),
        scratch_shapes=[
            pltpu.VMEM((PIECES, width), jnp.float32),
            pltpu.VMEM((width, PIECES), jnp.bfloat16),
            pltpu.VMEM((PIECES, width), jnp.bfloat16),
        ],
        compiler_params=params(12),
        cost_estimate=cost(24 * 2 * width * width * 80, 4 * width * width),
        name=f"tables{level}",
    )(cell_x, cell_depth, slowness)


def redatum_kernel(reach, below, wave, above, taps, out, padded, taps_t):
    count, width = wave.shape
    length = taps.shape[1]
    edge = below.shape[1]
    for f in range(0, count, LANES):
        lane = f // LANES
        for source, start in ((below, 0), (wave, edge), (above, edge + width)):
            for x in range(0, source.shape[1], LANES):
                block = source[f : f + LANES, x : x + LANES].astype(jnp.float32)
                padded[lane, start + x : start + x + LANES, :] = block.T
    taps_t[...] = taps[...].T
    tiles = LANES // SUBLANES

    @pl.loop(0, width // LANES)
    def _(block):
        base = pl.multiple_of(block * LANES, LANES)
        for lane in range(count // LANES):
            sums = [jnp.zeros((SUBLANES, LANES), jnp.float32) for _ in range(tiles)]
            for rest in range(SUBLANES):
                shifts = range(rest, length, SUBLANES)
                weights = [
                    jnp.broadcast_to(
                        taps_t[j : j + 1, lane * LANES : (lane + 1) * LANES], (SUBLANES, LANES)
                    )
                    for j in shifts
                ]
                for m in range(tiles + len(weights) - 1):
                    offset = edge - reach + rest + SUBLANES * m
                    piece = padded[lane, pl.ds(base + offset, SUBLANES), :]
                    for k, weight in enumerate(weights):
                        if 0 <= m - k < tiles:
                            sums[m - k] = sums[m - k] + weight * piece
            total = jnp.concatenate(sums, 0)
            out[lane * LANES : (lane + 1) * LANES, pl.ds(base, LANES)] = total.T.astype(out.dtype)


def redatum(below, wave, above, taps):
    count, width = wave.shape
    reach = (taps.shape[1] - 1) // 2
    long = width + 2 * below.shape[1]
    return pl.pallas_call(
        functools.partial(redatum_kernel, reach),
        out_shape=jax.ShapeDtypeStruct((count, width), jnp.bfloat16),
        in_specs=[VMEM] * 4,
        out_specs=VMEM,
        scratch_shapes=[
            pltpu.VMEM((count // LANES, long, LANES), jnp.float32),
            pltpu.VMEM((taps.shape[1], count), jnp.float32),
        ],
        compiler_params=params(8),
        cost_estimate=cost(count * width * taps.shape[1] * 100, count * width * 4),
        name="redatum",
    )(below, wave, above, taps)


def mix_kernel(mine, theirs, near, far, out):
    width = near.shape[1]
    scale = SCALE / math.sqrt(width)
    step = min(width, 256)
    for c in range(0, width, step):
        columns = slice(c, c + step)
        total = jnp.dot(mine[...], near[:, columns], preferred_element_type=jnp.float32)
        total += jnp.dot(theirs[...], far[:, columns], preferred_element_type=jnp.float32)
        out[:, columns] = (total * scale).astype(out.dtype)


def mix(mine, theirs, near, far):
    count, width = mine.shape
    return pl.pallas_call(
        mix_kernel,
        out_shape=jax.ShapeDtypeStruct((count, width), jnp.bfloat16),
        in_specs=[VMEM] * 4,
        out_specs=VMEM,
        compiler_params=params(12),
        cost_estimate=cost(4 * count * width * width, 4 * width * width),
        name="mix",
    )(mine, theirs, near, far)


def last_kernel(state, near, far, own_mask, far_mask, own, other):
    width = near.shape[1]
    scale = SCALE / math.sqrt(width)
    step = min(width, 256)
    for table, mask, out in ((far, far_mask, other), (near, own_mask, own)):
        for c in range(0, width, step):
            columns = slice(c, c + step)
            mixed = jnp.dot(state[...], table[:, columns], preferred_element_type=jnp.float32)
            kept = jnp.where(mask[:, columns].astype(jnp.float32) > 0, mixed, 0.0)
            out[:, columns] = jnp.sum(kept, 0, keepdims=True) * scale


def last(state, near, far, own_mask, far_mask):
    count, width = state.shape
    shape = jax.ShapeDtypeStruct((1, width), jnp.float32)
    return pl.pallas_call(
        last_kernel,
        out_shape=(shape, shape),
        in_specs=[VMEM] * 5,
        out_specs=(VMEM, VMEM),
        compiler_params=params(12),
        cost_estimate=cost(4 * count * width * width, 4 * width * width),
        name="last",
    )(state, near, far, own_mask, far_mask)


def on_device(wavefield, redatum_taps, cell_x, cell_depth, slowness, illumination, aperture):
    index = lax.axis_index("space")
    blocks = lax.axis_size("space") // BOXES
    block_bits = blocks.bit_length() - 1
    box = index // blocks
    block = index % blocks
    count, width = wavefield.shape
    depths = cell_depth.reshape(BOXES, width)
    below = passed_along(wavefield[:, width - LANES :], "space", blocks)
    above = passed_along(wavefield[:, :LANES], "space", -blocks)
    masks = partner((aperture > 0).astype(jnp.bfloat16), "space", LEVELS - 1 + block_bits)
    taps = redatum_taps
    if blocks > 1:
        taps = lax.dynamic_slice_in_dim(redatum_taps, block * count, count, 0)
    level_tables = [
        tables(level, blocks, width, cell_x, depths, slowness) for level in range(LEVELS)
    ]
    state = redatum(below, wavefield, above, taps)
    for level in range(LEVELS - 1):
        received = partner(state, "space", level + block_bits)
        state = mix(state, received, *level_tables[level])
    own, other = last(state, *level_tables[-1], aperture, masks)
    summed = own + partner(other, "space", LEVELS - 1 + block_bits)
    weights = lax.dynamic_slice_in_dim(illumination, box * width, width)
    image = summed * weights[None] / jnp.sqrt(jnp.float32(count * blocks))
    for level in range(block_bits):
        image = image + partner(image, "space", level)
    share = width // blocks
    return lax.dynamic_slice_in_dim(image, block * share, share, 1)


def solution(mesh):
    placed = (
        P(("groups", "space"), None),
        P("groups", None),
        P(),
        P(),
        P(),
        P("groups"),
        P(("groups", "space"), None),
    )
    return jax.shard_map(
        on_device,
        mesh=mesh,
        in_specs=placed,
        out_specs=P(("groups", "space"), None),
        check_vma=False,
    )
```

time: 244 us -> 74.5 us (0.31); the launches traced: 240 us -> 74.2 us
  matrix products: 155 us -> 0 us
  Pallas kernels: 0 us -> 37.7 us
  other arithmetic: 26.8 us -> 0.71 us
  waiting for transfers between devices: 32.3 us -> 18.3 us
  local copies, waits for them, and re-layouts: 9.83 us -> 3.67 us
    dot_general x32 -> x0, matrix products: 155 us -> none  [translate(): pieces.append(jnp.dot(left, table, preferred_element_type=jnp.float32))]
    pallas_call x0 -> x9, Pallas kernels: none -> 37.7 us  [the longest x4 26 us: tables(): pl.pallas_call(functools.partial(tables_kernel, level, blocks, min(width,...]
    convert_element_type x5 -> x1, other arithmetic: 23.7 us -> 0.1 us  [on_device(): (aperture > 0).astype(jnp.bfloat16)]
    ppermute x4 -> x5, waiting for transfers between devices: 32.3 us -> 15.4 us  [partner(): lax.ppermute(shard, axis, [(i, i ^ 1 << bit) for i in range(lax.axis_size...]
    slice x9 -> x1, local copies, waits for them, and re-layouts: 8.09 us -> 0.88 us  [on_device(): above = passed_along(wavefield[:, :LANES], 'space', -blocks)]
    ppermute x2, waiting for transfers between devices: 0.01 us -> 2.9 us  [passed_along(): return lax.ppermute(shard, axis, pairs)]
    ppermute x4 -> x5, starting transfers between devices: 10.6 us -> 9.88 us  [partner(): lax.ppermute(shard, axis, [(i, i ^ 1 << bit) for i in range(lax.axis_size...]
  transfers between devices with their start and end apart: 6 -> 7, of which waited for: 3 -> 4; matrix products, arithmetic and copies ran while one was open for 36% -> 2% of each run, Pallas kernels for 0% -> 39%
where the time goes in v1:
time: 74.5 us; the launch traced here: 74.2 us
  Pallas kernels  37.7 us (51%)
  waiting for transfers between devices  18.3 us (25%)
  starting transfers between devices  13.6 us (18%)
  local copies, waits for them, and re-layouts  3.67 us (5%)
    pallas_call x4, Pallas kernels, tables(): pl.pallas_call(functools.partial(tables_kernel, level, blocks, min(width,...  26 us
    ppermute x5, waiting for transfers between devices, partner(): lax.ppermute(shard, axis, [(i, i ^ 1 << bit) for i in range(lax.axis_size...  15.4 us
    ppermute x5, starting transfers between devices, partner(): lax.ppermute(shard, axis, [(i, i ^ 1 << bit) for i in range(lax.axis_size...  9.88 us
    pallas_call x1, Pallas kernels, redatum(): pl.pallas_call(functools.partial(redatum_kernel, reach), out_shape=jax.Sh...  6.5 us
    pallas_call x3, Pallas kernels, mix(): pl.pallas_call(mix_kernel, out_shape=jax.ShapeDtypeStruct((count, width),...  3.83 us
    ppermute x2, starting transfers between devices, passed_along(): return lax.ppermute(shard, axis, pairs)  3.69 us
    ppermute x2, waiting for transfers between devices, passed_along(): return lax.ppermute(shard, axis, pairs)  2.9 us
    unnamed x11, local copies, waits for them, and re-layouts  2.08 us
  transfers between devices with their start and end apart: 7, of which 4 were waited for; matrix products, arithmetic and copies ran while one was open for 2% of the time, Pallas kernels for 39%

profile of v1, /device:TPU:0, one launch (start us, length us, event | category | flops | bytes accessed | tf_op | source)
XLA Modules:
  0.0 74.2 jit_solution(126079158970060993)
XLA Ops:
  0.0 0.9 %fusion = (bf16[256,128]{1,0:T(8,128)(2,1)S(1)}, bf16[256,128]{1,0:T(8,128)(2,1)S(1)}) fusion(bf16[256,1024]{1,0:T(8,128)(2,1)} %wave.1), kind=kLoop, calls=%fused_computation.2 | loop fusion | bytes 262144 | tf_op jit(solution)/shard_map/slice | solution.py:254
  0.9 2.4 %collective-permute-start = (bf16[256,128]{1,0:T(8,128)(2,1)S(1)}, bf16[256,128]{1,0:T(8,128)(2,1)S(1)}, u32[]{:S(2)}, u32[]{:S(2)}) collective-permute-start(bf16[256,128]{1,0:T(8,128)(2,1)S(1)} %get-tuple-element.26), channel_id=1, source_target_pairs={{0,1},{1,2},{2,3},{3,4},{4,5},{5,6},{6,7},{7,8},{8,9},{9,10},{10,1... | collective-permute-start | bytes 196616 | tf_op jit(solution)/shard_map/ppermute | solution.py:35
  3.3 1.3 %collective-permute-start.1 = (bf16[256,128]{1,0:T(8,128)(2,1)S(1)}, bf16[256,128]{1,0:T(8,128)(2,1)S(1)}, u32[]{:S(2)}, u32[]{:S(2)}) collective-permute-start(bf16[256,128]{1,0:T(8,128)(2,1)S(1)} %get-tuple-element.25), channel_id=1, source_target_pairs={{1,0},{2,1},{3,2},{4,3},{5,4},{6,5},{7,6},{8,7},{9,8},{10,9},{11,1... | collective-permute-start | bytes 196616 | tf_op jit(solution)/shard_map/ppermute | solution.py:35
  4.6 0.0 copy-start.4
  4.6 0.0 copy-start.3
  4.6 1.0 %copy.8.taps = f32[256,65]{1,0:T(8,128)S(1)} copy(f32[256,65]{0,1:T(8,128)} %param.8) | data formatting | bytes 133120 | tf_op args[1]
  5.6 0.0 collective-permute-done.below
  5.6 2.9 %collective-permute-done.1.above = bf16[256,128]{1,0:T(8,128)(2,1)S(1)} collective-permute-done((bf16[256,128]{1,0:T(8,128)(2,1)S(1)}, bf16[256,128]{1,0:T(8,128)(2,1)S(1)}, u32[]{:S(2)}, u32[]{:S(2)}) %collective-permute-start.1) | collective-permute-done | bytes 65568 | tf_op jit(solution)/shard_map/ppermute | solution.py:35
  8.5 1.0 %copy-done.1 = bf16[256,1024]{1,0:T(8,128)(2,1)S(1)} copy-done((bf16[256,1024]{1,0:T(8,128)(2,1)S(1)}, bf16[256,1024]{1,0:T(8,128)(2,1)}, u32[]{:S(2)}) %copy-start.1) | copy-done | bytes 524312
  9.6 6.5 %redatum.1.mine = bf16[256,1024]{1,0:T(8,128)(2,1)S(1)} custom-call(bf16[256,128]{1,0:T(8,128)(2,1)S(1)} %collective-permute-done.below, bf16[256,1024]{1,0:T(8,128)(2,1)S(1)} %copy-done.1, bf16[256,128]{1,0:T(8,128)(2,1)S(1)} %collective-permute-done.1.above, f32[256,65]{1,0:T(8,128)S(1)} %copy.8.taps), custom_call_target="tpu_custom_call" | custom-call | flops 1703936000 | bytes 1048576 | tf_op jit(solution)/shard_map/redatum/pallas_call | solution.py:180
  16.1 3.0 %collective-permute-start.2 = (bf16[256,1024]{1,0:T(8,128)(2,1)S(1)}, bf16[256,1024]{1,0:T(8,128)(2,1)S(1)}, u32[]{:S(2)}, u32[]{:S(2)}) collective-permute-start(bf16[256,1024]{1,0:T(8,128)(2,1)S(1)} %redatum.1.mine), channel_id=1, source_target_pairs={{0,1},{1,0},{2,3},{3,2},{4,5},{5,4},{6,7},{7,6},{8,9},{9,8},{10,11... | collective-permute-start | bytes 1572872 | tf_op jit(solution)/shard_map/ppermute | solution.py:39
  19.1 6.5 %tables0.1 = (bf16[1024,1024]{1,0:T(8,128)(2,1)S(1)}, bf16[1024,1024]{1,0:T(8,128)(2,1)S(1)}) custom-call(s32[5,16384]{1,0:T(8,128)S(1)} %copy-done.2, s32[16,1024]{1,0:T(8,128)S(1)} %reshape.3.cell_depth, f32[4]{0:T(128)S(1)} %copy-done.3), custom_call_target="tpu_custom_call" | custom-call | flops 4026531840 | bytes 4194304 | tf_op jit(solution)/shard_map/tables0/pallas_call | solution.py:124
  25.7 0.0 collective-permute-done.2.theirs
  25.7 0.0 copy-start
  25.7 1.3 %mix.3.mine = bf16[256,1024]{1,0:T(8,128)(2,1)S(1)} custom-call(bf16[256,1024]{1,0:T(8,128)(2,1)S(1)} %redatum.1.mine, bf16[256,1024]{1,0:T(8,128)(2,1)S(1)} %collective-permute-done.2.theirs, bf16[1024,1024]{1,0:T(8,128)(2,1)S(1)} %get-tuple-element.15.near, bf16[1024,1024]{1,0:T(8,128)(2,1)S(1)} %get-tuple-element.16.far), custom_call_target="tpu_custom_call" | custom-call | flops 1073741824 | bytes 4194304 | tf_op jit(solution)/shard_map/mix/pallas_call | solution.py:208
  27.0 2.5 %collective-permute-start.3 = (bf16[256,1024]{1,0:T(8,128)(2,1)S(1)}, bf16[256,1024]{1,0:T(8,128)(2,1)S(1)}, u32[]{:S(2)}, u32[]{:S(2)}) collective-permute-start(bf16[256,1024]{1,0:T(8,128)(2,1)S(1)} %mix.3.mine), channel_id=1, source_target_pairs={{0,2},{1,3},{2,0},{3,1},{4,6},{5,7},{6,4},{7,5},{8,10},{9,11},{10,... | collective-permute-start | bytes 1572872 | tf_op jit(solution)/shard_map/ppermute | solution.py:39
  29.5 0.1 compare_convert_fusion
  29.6 2.6 %collective-permute-start.5 = (bf16[256,1024]{1,0:T(8,128)(2,1)S(1)}, bf16[256,1024]{1,0:T(8,128)(2,1)S(1)}, u32[]{:S(2)}, u32[]{:S(2)}) collective-permute-start(bf16[256,1024]{1,0:T(8,128)(2,1)S(1)} %compare_convert_fusion), channel_id=1, source_target_pairs={{0,8},{1,9},{2,10},{3,11},{4,12},{5,13},{6,14},{7,15},{8,0},{9,1},... | collective-permute-start | bytes 1572872 | tf_op jit(solution)/shard_map/ppermute | solution.py:39
  32.3 6.5 %tables1.1 = (bf16[1024,1024]{1,0:T(8,128)(2,1)S(1)}, bf16[1024,1024]{1,0:T(8,128)(2,1)S(1)}) custom-call(s32[5,16384]{1,0:T(8,128)S(1)} %copy-done.2, s32[16,1024]{1,0:T(8,128)S(1)} %reshape.3.cell_depth, f32[4]{0:T(128)S(1)} %copy-done.3), custom_call_target="tpu_custom_call" | custom-call | flops 4026531840 | bytes 4194304 | tf_op jit(solution)/shard_map/tables1/pallas_call | solution.py:124
  38.8 2.8 %collective-permute-done.3.theirs = bf16[256,1024]{1,0:T(8,128)(2,1)S(1)} collective-permute-done((bf16[256,1024]{1,0:T(8,128)(2,1)S(1)}, bf16[256,1024]{1,0:T(8,128)(2,1)S(1)}, u32[]{:S(2)}, u32[]{:S(2)}) %collective-permute-start.3) | collective-permute-done | bytes 524320 | tf_op jit(solution)/shard_map/ppermute | solution.py:39
  41.6 1.3 %mix.4.mine = bf16[256,1024]{1,0:T(8,128)(2,1)S(1)} custom-call(bf16[256,1024]{1,0:T(8,128)(2,1)S(1)} %mix.3.mine, bf16[256,1024]{1,0:T(8,128)(2,1)S(1)} %collective-permute-done.3.theirs, bf16[1024,1024]{1,0:T(8,128)(2,1)S(1)} %get-tuple-element.17.near, bf16[1024,1024]{1,0:T(8,128)(2,1)S(1)} %get-tuple-element.18.far), custom_call_target="tpu_custom_call" | custom-call | flops 1073741824 | bytes 4194304 | tf_op jit(solution)/shard_map/mix/pallas_call | solution.py:208
  42.9 1.6 %collective-permute-start.4 = (bf16[256,1024]{1,0:T(8,128)(2,1)S(1)}, bf16[256,1024]{1,0:T(8,128)(2,1)S(1)}, u32[]{:S(2)}, u32[]{:S(2)}) collective-permute-start(bf16[256,1024]{1,0:T(8,128)(2,1)S(1)} %mix.4.mine), channel_id=1, source_target_pairs={{0,4},{1,5},{2,6},{3,7},{4,0},{5,1},{6,2},{7,3},{8,12},{9,13},{10,... | collective-permute-start | bytes 1572872 | tf_op jit(solution)/shard_map/ppermute | solution.py:39
  44.5 6.5 %tables2.1 = (bf16[1024,1024]{1,0:T(8,128)(2,1)S(1)}, bf16[1024,1024]{1,0:T(8,128)(2,1)S(1)}) custom-call(s32[5,16384]{1,0:T(8,128)S(1)} %copy-done.2, s32[16,1024]{1,0:T(8,128)S(1)} %reshape.3.cell_depth, f32[4]{0:T(128)S(1)} %copy-done.3), custom_call_target="tpu_custom_call" | custom-call | flops 4026531840 | bytes 4194304 | tf_op jit(solution)/shard_map/tables2/pallas_call | solution.py:124
  51.1 6.4 %tables3.1 = (bf16[1024,1024]{1,0:T(8,128)(2,1)S(1)}, bf16[1024,1024]{1,0:T(8,128)(2,1)S(1)}) custom-call(s32[5,16384]{1,0:T(8,128)S(1)} %copy-done.2, s32[16,1024]{1,0:T(8,128)S(1)} %reshape.3.cell_depth, f32[4]{0:T(128)S(1)} %copy-done.3), custom_call_target="tpu_custom_call" | custom-call | flops 4026531840 | bytes 4194304 | tf_op jit(solution)/shard_map/tables3/pallas_call | solution.py:124
  57.5 8.8 %collective-permute-done.4.theirs = bf16[256,1024]{1,0:T(8,128)(2,1)S(1)} collective-permute-done((bf16[256,1024]{1,0:T(8,128)(2,1)S(1)}, bf16[256,1024]{1,0:T(8,128)(2,1)S(1)}, u32[]{:S(2)}, u32[]{:S(2)}) %collective-permute-start.4) | collective-permute-done | bytes 524320 | tf_op jit(solution)/shard_map/ppermute | solution.py:39
  66.4 1.3 %mix.5.state = bf16[256,1024]{1,0:T(8,128)(2,1)S(1)} custom-call(bf16[256,1024]{1,0:T(8,128)(2,1)S(1)} %mix.4.mine, bf16[256,1024]{1,0:T(8,128)(2,1)S(1)} %collective-permute-done.4.theirs, bf16[1024,1024]{1,0:T(8,128)(2,1)S(1)} %get-tuple-element.19.near, bf16[1024,1024]{1,0:T(8,128)(2,1)S(1)} %get-tuple-element.20.far), custom_call_target="tpu_custom_call" | custom-call | flops 1073741824 | bytes 4194304 | tf_op jit(solution)/shard_map/mix/pallas_call | solution.py:208
  67.6 0.0 collective-permute-done.5.far_mask
  67.7 1.3 %last.1 = (f32[1,1024]{1,0:T(1,128)S(1)}, f32[1,1024]{1,0:T(1,128)S(1)}) custom-call(bf16[256,1024]{1,0:T(8,128)(2,1)S(1)} %mix.5.state, bf16[1024,1024]{1,0:T(8,128)(2,1)S(1)} %get-tuple-element.21.near, bf16[1024,1024]{1,0:T(8,128)(2,1)S(1)} %get-tuple-element.22.far, s32[256,1024]{1,0:T(8,128)S(1)} %copy-done, ...), custom_call_target="tpu_custom_call" | custom-call | flops 1073741824 | bytes 4194304 | tf_op jit(solution)/shard_map/last/pallas_call | solution.py:234
  69.0 0.1 collective-permute-start.6
  69.1 0.7 dynamic_slice.4
  69.8 3.8 %collective-permute-done.6 = f32[1,1024]{1,0:T(1,128)S(1)} collective-permute-done((f32[1,1024]{1,0:T(1,128)S(1)}, f32[1,1024]{1,0:T(1,128)S(1)}, u32[]{:S(2)}, u32[]{:S(2)}) %collective-permute-start.6) | collective-permute-done | bytes 4128 | tf_op jit(solution)/shard_map/ppermute | solution.py:39
  73.6 0.6 multiply_multiply_fusion
  (7 shorter events, 0.0 us)
Async XLA Ops:
  0.9 4.7 %collective-permute-start = (bf16[256,128]{1,0:T(8,128)(2,1)S(1)}, bf16[256,128]{1,0:T(8,128)(2,1)S(1)}, u32[]{:S(2)}, u32[]{:S(2)}) collective-permute-start(bf16[256,128]{1,0:T(8,128)(2,1)S(1)} %get-tuple-element.26), channel_id=1, source_target_pairs={{0,1},{1,2},{2,3},{3,4},{4,5},{5,6},{6,7},{7,8},{8,9},{9,10},{10,1... | collective-permute-start | bytes 196616 | tf_op jit(solution)/shard_map/ppermute | solution.py:35
  3.3 5.2 %collective-permute-start.1 = (bf16[256,128]{1,0:T(8,128)(2,1)S(1)}, bf16[256,128]{1,0:T(8,128)(2,1)S(1)}, u32[]{:S(2)}, u32[]{:S(2)}) collective-permute-start(bf16[256,128]{1,0:T(8,128)(2,1)S(1)} %get-tuple-element.25), channel_id=1, source_target_pairs={{1,0},{2,1},{3,2},{4,3},{5,4},{6,5},{7,6},{8,7},{9,8},{10,9},{11,1... | collective-permute-start | bytes 196616 | tf_op jit(solution)/shard_map/ppermute | solution.py:35
  4.6 14.5 %copy-start.4 = (s32[16384]{0:T(1024)S(1)}, s32[16384]{0:T(1024)}, u32[]{:S(2)}) copy-start(s32[16384]{0:T(1024)} %param.10) | copy-start | bytes 196612
  4.6 14.5 %copy-start.3 = (f32[4]{0:T(128)S(1)}, f32[4]{0:T(128)}, u32[]{:S(2)}) copy-start(f32[4]{0:T(128)} %slowness.7) | copy-start | bytes 52
  8.5 1.0 %copy-start.1 = (bf16[256,1024]{1,0:T(8,128)(2,1)S(1)}, bf16[256,1024]{1,0:T(8,128)(2,1)}, u32[]{:S(2)}) copy-start(bf16[256,1024]{1,0:T(8,128)(2,1)} %wave.1) | copy-start | bytes 1572868
  9.6 9.5 %copy-start.2 = (s32[5,16384]{1,0:T(8,128)S(1)}, s32[5,16384]{1,0:T(8,128)}, u32[]{:S(2)}) copy-start(s32[5,16384]{1,0:T(8,128)} %cell_x.7) | copy-start | bytes 983044
  16.1 9.6 %collective-permute-start.2 = (bf16[256,1024]{1,0:T(8,128)(2,1)S(1)}, bf16[256,1024]{1,0:T(8,128)(2,1)S(1)}, u32[]{:S(2)}, u32[]{:S(2)}) collective-permute-start(bf16[256,1024]{1,0:T(8,128)(2,1)S(1)} %redatum.1.mine), channel_id=1, source_target_pairs={{0,1},{1,0},{2,3},{3,2},{4,5},{5,4},{6,7},{7,6},{8,9},{9,8},{10,11... | collective-permute-start | bytes 1572872 | tf_op jit(solution)/shard_map/ppermute | solution.py:39
  25.7 3.8 %copy-start = (s32[256,1024]{1,0:T(8,128)S(1)}, s32[256,1024]{1,0:T(8,128)}, u32[]{:S(2)}) copy-start(s32[256,1024]{1,0:T(8,128)} %own_mask.1) | copy-start | bytes 3145732
  27.0 14.6 %collective-permute-start.3 = (bf16[256,1024]{1,0:T(8,128)(2,1)S(1)}, bf16[256,1024]{1,0:T(8,128)(2,1)S(1)}, u32[]{:S(2)}, u32[]{:S(2)}) collective-permute-start(bf16[256,1024]{1,0:T(8,128)(2,1)S(1)} %mix.3.mine), channel_id=1, source_target_pairs={{0,2},{1,3},{2,0},{3,1},{4,6},{5,7},{6,4},{7,5},{8,10},{9,11},{10,... | collective-permute-start | bytes 1572872 | tf_op jit(solution)/shard_map/ppermute | solution.py:39
  29.6 38.0 %collective-permute-start.5 = (bf16[256,1024]{1,0:T(8,128)(2,1)S(1)}, bf16[256,1024]{1,0:T(8,128)(2,1)S(1)}, u32[]{:S(2)}, u32[]{:S(2)}) collective-permute-start(bf16[256,1024]{1,0:T(8,128)(2,1)S(1)} %compare_convert_fusion), channel_id=1, source_target_pairs={{0,8},{1,9},{2,10},{3,11},{4,12},{5,13},{6,14},{7,15},{8,0},{9,1},... | collective-permute-start | bytes 1572872 | tf_op jit(solution)/shard_map/ppermute | solution.py:39
  42.9 23.5 %collective-permute-start.4 = (bf16[256,1024]{1,0:T(8,128)(2,1)S(1)}, bf16[256,1024]{1,0:T(8,128)(2,1)S(1)}, u32[]{:S(2)}, u32[]{:S(2)}) collective-permute-start(bf16[256,1024]{1,0:T(8,128)(2,1)S(1)} %mix.4.mine), channel_id=1, source_target_pairs={{0,4},{1,5},{2,6},{3,7},{4,0},{5,1},{6,2},{7,3},{8,12},{9,13},{10,... | collective-permute-start | bytes 1572872 | tf_op jit(solution)/shard_map/ppermute | solution.py:39
  69.0 4.6 %collective-permute-start.6 = (f32[1,1024]{1,0:T(1,128)S(1)}, f32[1,1024]{1,0:T(1,128)S(1)}, u32[]{:S(2)}, u32[]{:S(2)}) collective-permute-start(f32[1,1024]{1,0:T(1,128)S(1)} %get-tuple-element.24), channel_id=1, source_target_pairs={{0,8},{1,9},{2,10},{3,11},{4,12},{5,13},{6,14},{7,15},{8,0},{9,1},... | collective-permute-start | bytes 12296 | tf_op jit(solution)/shard_map/ppermute | solution.py:39

commit v2 on v1

v2 whole, which is shorter than its diff:
```python
import functools
import math

import jax
import jax.numpy as jnp
from jax import lax
from jax.experimental import pallas as pl
from jax.experimental.pallas import tpu as pltpu
from jax.sharding import PartitionSpec as P


LEVELS = 4
BOXES = 16
LANES = 128

POLY_A = -0.55846636
POLY_B = 0.08535978
SCALE = -73.58594804
VMEM = pl.BlockSpec(memory_space=pltpu.VMEM)
ANY = pl.BlockSpec(memory_space=pl.ANY)
SMEM = pl.BlockSpec(memory_space=pltpu.SMEM)


def params(mib):
    return pltpu.CompilerParams(vmem_limit_bytes=mib << 20)


def cost(flops, moved, transcendentals=0):
    return pl.CostEstimate(flops=flops, bytes_accessed=moved, transcendentals=transcendentals)


def passed_along(shard, axis, by):
    devices = lax.axis_size(axis)
    pairs = [(i, i + by) for i in range(devices) if 0 <= i + by < devices]
    return lax.ppermute(shard, axis, pairs)


def partner(shard, axis, bit):
    return lax.ppermute(shard, axis, [(i, i ^ 1 << bit) for i in range(lax.axis_size(axis))])


def cosine(squared):
    u = squared * lax.rsqrt(squared)
    r = u - jnp.round(u)
    w = jnp.abs(r) - 0.25
    q = w * w
    return w * ((q + POLY_A) * q + POLY_B)


def boxes_of(level, blocks):
    box = lax.axis_index("space") // blocks
    bit = 1 << level
    upper = (box // bit) % 2
    return box, box + bit - 2 * bit * upper


def tables_kernel(level, blocks, step, cell_x, cell_depth, slowness, *refs):
    near, far, rows = refs[-3:]
    width = near.shape[0]
    final = level + 1 == LEVELS
    box, other = boxes_of(level, blocks)
    turns = slowness[level] * (0.5 / math.pi)

    def place(which, of):
        at = pl.ds(pl.multiple_of(which * width, width), width)
        return cell_x[of : of + 1, at].astype(jnp.float32) * turns

    for out, row_box, column_box in (
        (near, box, box),
        (far, box if final else other, other if final else box),
    ):
        if out is near or not final:
            rows[...] = jnp.broadcast_to(place(row_box, level), (LANES, width)).T
        columns = place(column_box, level + 1)
        depth = cell_depth[pl.ds(column_box, 1), :].astype(jnp.float32) * turns
        below = depth * depth

        @pl.loop(0, width // step)
        def _(i):
            at = pl.ds(pl.multiple_of(i * step, step), step)
            for c in range(0, width, 2 * LANES):
                part = rows[at, :]
                across = jnp.concatenate([part, part], 1) - columns[:, c : c + 2 * LANES]
                squared = across * across + below[:, c : c + 2 * LANES]
                out[at, c : c + 2 * LANES] = cosine(squared).astype(jnp.bfloat16)


def tables(level, blocks, width, cell_x, cell_depth, slowness, *after):
    shape = jax.ShapeDtypeStruct((width, width), jnp.bfloat16)
    return pl.pallas_call(
        functools.partial(tables_kernel, level, blocks, min(width, 128)),
        out_shape=(shape, shape),
        in_specs=[VMEM, VMEM, SMEM] + [ANY] * len(after),
        out_specs=(VMEM, VMEM),
        scratch_shapes=[pltpu.VMEM((width, LANES), jnp.float32)],
        compiler_params=params(7),
        cost_estimate=cost(24 * 2 * width * width * 40, 4 * width * width),
    )(cell_x, cell_depth, slowness, *after)


def redatum_kernel(reach, part, below, wave, above, taps, *refs):
    out, padded = refs[-2:]
    width = wave.shape[1]
    edge = below.shape[1]
    held = slice(part * LANES, (part + 1) * LANES)
    for source, start in ((below, 0), (wave, edge), (above, edge + width)):
        for x in range(0, source.shape[1], LANES):
            block = source[held, x : x + LANES].astype(jnp.float32)
            padded[start + x : start + x + LANES, :] = block.T

    @pl.loop(0, width // LANES)
    def _(block):
        base = pl.multiple_of(block * LANES, LANES)
        total = None
        for j in range(taps.shape[0]):
            weight = jnp.broadcast_to(taps[j : j + 1, held], (LANES, LANES))
            term = weight * padded[pl.ds(base + edge - reach + j, LANES), :]
            total = term if total is None else total + term
        out[:, pl.ds(base, LANES)] = total.T.astype(out.dtype)


def redatum(part, below, wave, above, taps, *after):
    width = wave.shape[1]
    reach = (taps.shape[0] - 1) // 2
    long = width + 2 * below.shape[1]
    return pl.pallas_call(
        functools.partial(redatum_kernel, reach, part),
        out_shape=jax.ShapeDtypeStruct((LANES, width), jnp.bfloat16),
        in_specs=[VMEM] * 4 + [ANY] * len(after),
        out_specs=VMEM,
        scratch_shapes=[pltpu.VMEM((long, LANES), jnp.float32)],
        compiler_params=params(5),
        cost_estimate=cost(24 * 2 * width * width * 30, LANES * width * 4),
    )(below, wave, above, taps, *after)


def mix_kernel(mine, theirs, near, far, *refs):
    out = refs[-1]
    width = near.shape[1]
    scale = SCALE / math.sqrt(width)
    step = min(width, 256)
    for c in range(0, width, step):
        columns = slice(c, c + step)
        total = jnp.dot(mine[...], near[:, columns], preferred_element_type=jnp.float32)
        total += jnp.dot(theirs[...], far[:, columns], preferred_element_type=jnp.float32)
        out[:, columns] = (total * scale).astype(out.dtype)


def mix(mine, theirs, near, far, *after):
    count, width = mine.shape
    return pl.pallas_call(
        mix_kernel,
        out_shape=jax.ShapeDtypeStruct((count, width), jnp.bfloat16),
        in_specs=[VMEM] * 4 + [ANY] * len(after),
        out_specs=VMEM,
        compiler_params=params(7),
        cost_estimate=cost(4 * count * width * width, 4 * width * width),
        name="mix",
    )(mine, theirs, near, far, *after)


def last_kernel(part, state, near, far, own_mask, far_mask, *refs):
    own, other = refs[-2:]
    width = near.shape[1]
    scale = SCALE / math.sqrt(width)
    step = min(width, 256)
    held = slice(part * LANES, (part + 1) * LANES)
    for k, (table, mask, out) in enumerate(((far, far_mask, other), (near, own_mask, own))):
        for c in range(0, width, step):
            columns = slice(c, c + step)
            mixed = jnp.dot(state[...], table[:, columns], preferred_element_type=jnp.float32)
            kept = jnp.where(mask[held, columns].astype(jnp.float32) > 0, mixed, 0.0)
            total = jnp.sum(kept, 0, keepdims=True) * scale
            if part > 0:
                total = total + refs[1 - k][:, columns]
            out[:, columns] = total


def last(part, state, near, far, own_mask, far_mask, sums, *after):
    count, width = state.shape
    shape = jax.ShapeDtypeStruct((1, width), jnp.float32)
    return pl.pallas_call(
        functools.partial(last_kernel, part),
        out_shape=(shape, shape),
        in_specs=[VMEM] * (5 + len(sums)) + [ANY] * len(after),
        out_specs=(VMEM, VMEM),
        compiler_params=params(8),
        cost_estimate=cost(4 * count * width * width, 4 * width * width),
    )(state, near, far, own_mask, far_mask, *sums, *after)


def on_device(wavefield, redatum_taps, cell_x, cell_depth, slowness, illumination, aperture):
    index = lax.axis_index("space")
    blocks = lax.axis_size("space") // BOXES
    block_bits = blocks.bit_length() - 1
    box = index // blocks
    block = index % blocks
    count, width = wavefield.shape
    depths = cell_depth.reshape(BOXES, width)
    below = passed_along(wavefield[:, width - LANES :], "space", blocks)
    above = passed_along(wavefield[:, :LANES], "space", -blocks)
    mask = (aperture > 0).astype(jnp.bfloat16)
    masks = partner(mask, "space", LEVELS - 1 + block_bits)
    taps = redatum_taps
    if blocks > 1:
        taps = lax.dynamic_slice_in_dim(redatum_taps, block * count, count, 0)
    taps = taps.T
    parts = range(count // LANES)

    def exchange(states, level):
        return [partner(state, "space", level + block_bits) for state in states]

    shared = (blocks, width, cell_x, depths, slowness)
    table = tables(0, *shared, mask)
    states, ahead = [], table[0]
    for part in parts:
        states.append(redatum(part, below, wavefield, above, taps, ahead))
        ahead = states[-1]
    for level in range(LEVELS - 1):
        received = exchange(states, level)
        for part in parts:
            states[part] = mix(states[part], received[part], *table, ahead)
            ahead = states[part]
            if part == 0 and level > 0:
                following = tables(level + 1, *shared, ahead)
                ahead = following[0]
        if level == 0:
            following = tables(level + 1, *shared, ahead)
            ahead = following[0]
        table = following
    sums = ()
    for part in parts:
        sums = last(part, states[part], *table, aperture, masks, sums)
    own, other = sums
    summed = own + partner(other, "space", LEVELS - 1 + block_bits)
    weights = lax.dynamic_slice_in_dim(illumination, box * width, width)
    image = summed * weights[None] / jnp.sqrt(jnp.float32(count * blocks))
    for level in range(block_bits):
        image = image + partner(image, "space", level)
    share = width // blocks
    return lax.dynamic_slice_in_dim(image, block * share, share, 1)


def solution(mesh):
    placed = (
        P(("groups", "space"), None),
        P("groups", None),
        P(),
        P(),
        P(),
        P("groups"),
        P(("groups", "space"), None),
    )
    return jax.shard_map(
        on_device,
        mesh=mesh,
        in_specs=placed,
        out_specs=P(("groups", "space"), None),
        check_vma=False,
    )
```

time: 74.5 us -> 70.1 us (0.941)
  Pallas kernels: 37.7 us -> 32.3 us
  waiting for transfers between devices: 18.3 us -> 15.1 us
  starting transfers between devices: 13.6 us -> 15.6 us
  other arithmetic: 0.71 us -> 1.93 us
  local copies, waits for them, and re-layouts: 3.67 us -> 4.6 us
    pallas_call x4, Pallas kernels: 26 us -> 20.3 us  [tables(): pl.pallas_call(functools.partial(tables_kernel, level, blocks, min(width,...]
    ppermute x2, waiting for transfers between devices: 2.9 us -> 0.01 us  [passed_along(): return lax.ppermute(shard, axis, pairs)]
    ppermute x5 -> x8, starting transfers between devices: 9.88 us -> 11.9 us  [partner(): lax.ppermute(shard, axis, [(i, i ^ 1 << bit) for i in range(lax.axis_size...]
    convert_element_type x1, other arithmetic: 0.1 us -> 1.33 us  [on_device(): mask = (aperture > 0).astype(jnp.bfloat16)]
    reshape x1, local copies, waits for them, and re-layouts: 0.02 us -> 0.86 us  [on_device(): depths = cell_depth.reshape(BOXES, width)]
    pallas_call x3 -> x6, Pallas kernels: 3.83 us -> 4.43 us  [mix(): pl.pallas_call(mix_kernel, out_shape=jax.ShapeDtypeStruct((count, width),...]
    ppermute x5 -> x8, waiting for transfers between devices: 15.4 us -> 15 us  [partner(): lax.ppermute(shard, axis, [(i, i ^ 1 << bit) for i in range(lax.axis_size...]
    pallas_call x2 -> x4, Pallas kernels: 7.84 us -> 7.5 us  [the longest x2 5.97 us: redatum(): pl.pallas_call(functools.partial(redatum_kernel, reach, part), out_shape=...]
  transfers between devices with their start and end apart: 7 -> 10, of which waited for: 4 -> 2; matrix products, arithmetic and copies ran while one was open for 2% -> 4% of each run, Pallas kernels for 39% -> 40%
where the time goes in v2:
time: 70.1 us; the launch traced here: 69.7 us
  Pallas kernels  32.3 us (46%)
  starting transfers between devices  15.6 us (22%)
  waiting for transfers between devices  15.1 us (22%)
  local copies, waits for them, and re-layouts  4.6 us (7%)
  other arithmetic  1.93 us (3%)
    pallas_call x4, Pallas kernels, tables(): pl.pallas_call(functools.partial(tables_kernel, level, blocks, min(width,...  20.3 us
    ppermute x8, waiting for transfers between devices, partner(): lax.ppermute(shard, axis, [(i, i ^ 1 << bit) for i in range(lax.axis_size...  15 us
    ppermute x8, starting transfers between devices, partner(): lax.ppermute(shard, axis, [(i, i ^ 1 << bit) for i in range(lax.axis_size...  11.9 us
    pallas_call x2, Pallas kernels, redatum(): pl.pallas_call(functools.partial(redatum_kernel, reach, part), out_shape=...  5.97 us
    pallas_call x6, Pallas kernels, mix(): pl.pallas_call(mix_kernel, out_shape=jax.ShapeDtypeStruct((count, width),...  4.43 us
    ppermute x2, starting transfers between devices, passed_along(): return lax.ppermute(shard, axis, pairs)  3.69 us
    unnamed x12, local copies, waits for them, and re-layouts  2.17 us
    pallas_call x2, Pallas kernels, last(): pl.pallas_call(functools.partial(last_kernel, part), out_shape=(shape, sh...  1.53 us
  transfers between devices with their start and end apart: 10, of which 2 were waited for; matrix products, arithmetic and copies ran while one was open for 4% of the time, Pallas kernels for 40%

profile of v2, /device:TPU:0, one launch (start us, length us, event | category | flops | bytes accessed | tf_op | source)
XLA Modules:
  0.0 69.7 jit_solution(18166056831383760603)
XLA Ops:
  0.0 0.9 %fusion = (bf16[256,128]{1,0:T(8,128)(2,1)S(1)}, bf16[256,128]{1,0:T(8,128)(2,1)S(1)}) fusion(bf16[256,1024]{1,0:T(8,128)(2,1)} %wave.3), kind=kLoop, calls=%fused_computation.2 | loop fusion | bytes 262144 | tf_op jit(solution)/shard_map/slice | solution.py:201
  0.9 2.4 %collective-permute-start = (bf16[256,128]{1,0:T(8,128)(2,1)S(1)}, bf16[256,128]{1,0:T(8,128)(2,1)S(1)}, u32[]{:S(2)}, u32[]{:S(2)}) collective-permute-start(bf16[256,128]{1,0:T(8,128)(2,1)S(1)} %get-tuple-element.30), channel_id=1, source_target_pairs={{0,1},{1,2},{2,3},{3,4},{4,5},{5,6},{6,7},{7,8},{8,9},{9,10},{10,1... | collective-permute-start | bytes 196616 | tf_op jit(solution)/shard_map/ppermute | solution.py:35
  3.3 1.3 %collective-permute-start.1 = (bf16[256,128]{1,0:T(8,128)(2,1)S(1)}, bf16[256,128]{1,0:T(8,128)(2,1)S(1)}, u32[]{:S(2)}, u32[]{:S(2)}) collective-permute-start(bf16[256,128]{1,0:T(8,128)(2,1)S(1)} %get-tuple-element.29), channel_id=1, source_target_pairs={{1,0},{2,1},{3,2},{4,3},{5,4},{6,5},{7,6},{8,7},{9,8},{10,9},{11,1... | collective-permute-start | bytes 196616 | tf_op jit(solution)/shard_map/ppermute | solution.py:35
  4.6 0.9 %reshape.3.cell_depth = s32[16,1024]{1,0:T(8,128)S(1)} reshape(s32[16384]{0:T(1024)} %param.10) | data formatting | bytes 131072 | tf_op jit(solution)/shard_map/reshape | solution.py:199
  5.5 1.3 %compare_convert_fusion.refs_0_ = bf16[256,1024]{1,0:T(8,128)(2,1)S(1)} fusion(s32[256,1024]{1,0:T(8,128)} %own_mask.3), kind=kLoop, calls=%fused_computation | loop fusion | flops 524288 | bytes 1572864 | tf_op jit(solution)/shard_map/convert_element_type | solution.py:202
  6.8 1.0 %copy-done.2 = s32[5,16384]{1,0:T(8,128)S(1)} copy-done((s32[5,16384]{1,0:T(8,128)S(1)}, s32[5,16384]{1,0:T(8,128)}, u32[]{:S(2)}) %copy-start.2) | copy-done | bytes 327704
  7.8 0.7 copy-done.5
  8.5 5.1 %shard_map.73 = (bf16[1024,1024]{1,0:T(8,128)(2,1)S(1)}, bf16[1024,1024]{1,0:T(8,128)(2,1)S(1)}) custom-call(s32[5,16384]{1,0:T(8,128)S(1)} %copy-done.2, s32[16,1024]{1,0:T(8,128)S(1)} %reshape.3.cell_depth, f32[4]{0:T(128)S(1)} %copy-done.5, bf16[256,1024]{1,0:T(8,128)(2,1)S(1)} %compare_convert_fusion.refs_0_), custom_call_target="tpu_custom_call" | custom-call | flops 2013265920 | bytes 4194304 | tf_op jit(solution)/shard_map/pallas_call | solution.py:90
  13.7 3.0 %shard_map.74.refs_0_.mine = bf16[128,1024]{1,0:T(8,128)(2,1)S(1)} custom-call(bf16[256,128]{1,0:T(8,128)(2,1)S(1)} %collective-permute-done.below, bf16[256,1024]{1,0:T(8,128)(2,1)S(1)} %copy-done.1, bf16[256,128]{1,0:T(8,128)(2,1)S(1)} %collective-permute-done.1.above, f32[65,256]{1,0:T(8,128)S(1)} %bitcast.2, ...), custom_call_target="tpu_custom_call" | custom-call | flops 1509949440 | bytes 524288 | tf_op jit(solution)/shard_map/pallas_call | solution.py:126
  16.7 3.3 %collective-permute-start.3 = (bf16[128,1024]{1,0:T(8,128)(2,1)S(1)}, bf16[128,1024]{1,0:T(8,128)(2,1)S(1)}, u32[]{:S(2)}, u32[]{:S(2)}) collective-permute-start(bf16[128,1024]{1,0:T(8,128)(2,1)S(1)} %shard_map.74.refs_0_.mine), channel_id=1, source_target_pairs={{0,1},{1,0},{2,3},{3,2},{4,5},{5,4},{6,7},{7,6},{8,9},{9,8},{10,11... | collective-permute-start | bytes 786440 | tf_op jit(solution)/shard_map/ppermute | solution.py:39
  20.0 3.0 %shard_map.75.refs_0_.mine = bf16[128,1024]{1,0:T(8,128)(2,1)S(1)} custom-call(bf16[256,128]{1,0:T(8,128)(2,1)S(1)} %collective-permute-done.below, bf16[256,1024]{1,0:T(8,128)(2,1)S(1)} %copy-done.1, bf16[256,128]{1,0:T(8,128)(2,1)S(1)} %collective-permute-done.1.above, f32[65,256]{1,0:T(8,128)S(1)} %bitcast.3, bf16[128,1024]{1,0:T(8,128)(2,1)S(1)} %shard_map.74.refs_0_.mine), custom_call_target="tpu_custom_call" | custom-call | flops 1509949440 | bytes 524288 | tf_op jit(solution)/shard_map/pallas_call | solution.py:126
  23.0 0.8 %mix.6.refs_0_.mine = bf16[128,1024]{1,0:T(8,128)(2,1)S(1)} custom-call(bf16[128,1024]{1,0:T(8,128)(2,1)S(1)} %shard_map.74.refs_0_.mine, bf16[128,1024]{1,0:T(8,128)(2,1)S(1)} %collective-permute-done.3.theirs, bf16[1024,1024]{1,0:T(8,128)(2,1)S(1)} %get-tuple-element.17.refs_0_.near, bf16[1024,1024]{1,0:T(8,128)(2,1)S(1)} %get-tuple-element.18.far, ...), custom_call_target="tpu_custom_call" | custom-call | flops 536870912 | bytes 4194304 | tf_op jit(solution)/shard_map/mix/pallas_call | solution.py:151
  23.8 2.2 %collective-permute-start.5 = (bf16[128,1024]{1,0:T(8,128)(2,1)S(1)}, bf16[128,1024]{1,0:T(8,128)(2,1)S(1)}, u32[]{:S(2)}, u32[]{:S(2)}) collective-permute-start(bf16[128,1024]{1,0:T(8,128)(2,1)S(1)} %mix.6.refs_0_.mine), channel_id=1, source_target_pairs={{0,2},{1,3},{2,0},{3,1},{4,6},{5,7},{6,4},{7,5},{8,10},{9,11},{10,... | collective-permute-start | bytes 786440 | tf_op jit(solution)/shard_map/ppermute | solution.py:39
  26.0 2.6 %collective-permute-start.8 = (bf16[256,1024]{1,0:T(8,128)(2,1)S(1)}, bf16[256,1024]{1,0:T(8,128)(2,1)S(1)}, u32[]{:S(2)}, u32[]{:S(2)}) collective-permute-start(bf16[256,1024]{1,0:T(8,128)(2,1)S(1)} %compare_convert_fusion.refs_0_), channel_id=1, source_target_pairs={{0,8},{1,9},{2,10},{3,11},{4,12},{5,13},{6,14},{7,15},{8,0},{9,1},... | collective-permute-start | bytes 1572872 | tf_op jit(solution)/shard_map/ppermute | solution.py:39
  28.6 0.8 %mix.7.refs_0_.mine = bf16[128,1024]{1,0:T(8,128)(2,1)S(1)} custom-call(bf16[128,1024]{1,0:T(8,128)(2,1)S(1)} %shard_map.75.refs_0_.mine, bf16[128,1024]{1,0:T(8,128)(2,1)S(1)} %collective-permute-done.2.theirs, bf16[1024,1024]{1,0:T(8,128)(2,1)S(1)} %get-tuple-element.17.refs_0_.near, bf16[1024,1024]{1,0:T(8,128)(2,1)S(1)} %get-tuple-element.18.far, ...), custom_call_target="tpu_custom_call" | custom-call | flops 536870912 | bytes 4194304 | tf_op jit(solution)/shard_map/mix/pallas_call | solution.py:151
  29.3 1.5 %collective-permute-start.4 = (bf16[128,1024]{1,0:T(8,128)(2,1)S(1)}, bf16[128,1024]{1,0:T(8,128)(2,1)S(1)}, u32[]{:S(2)}, u32[]{:S(2)}) collective-permute-start(bf16[128,1024]{1,0:T(8,128)(2,1)S(1)} %mix.7.refs_0_.mine), channel_id=1, source_target_pairs={{0,2},{1,3},{2,0},{3,1},{4,6},{5,7},{6,4},{7,5},{8,10},{9,11},{10,... | collective-permute-start | bytes 786440 | tf_op jit(solution)/shard_map/ppermute | solution.py:39
  30.8 5.1 %shard_map.76 = (bf16[1024,1024]{1,0:T(8,128)(2,1)S(1)}, bf16[1024,1024]{1,0:T(8,128)(2,1)S(1)}) custom-call(s32[5,16384]{1,0:T(8,128)S(1)} %copy-done.3, s32[16,1024]{1,0:T(8,128)S(1)} %reshape.3.cell_depth, f32[4]{0:T(128)S(1)} %copy-done.5, bf16[128,1024]{1,0:T(8,128)(2,1)S(1)} %mix.7.refs_0_.mine), custom_call_target="tpu_custom_call" | custom-call | flops 2013265920 | bytes 4194304 | tf_op jit(solution)/shard_map/pallas_call | solution.py:90
  36.0 0.7 %mix.8.refs_0_.mine = bf16[128,1024]{1,0:T(8,128)(2,1)S(1)} custom-call(bf16[128,1024]{1,0:T(8,128)(2,1)S(1)} %mix.6.refs_0_.mine, bf16[128,1024]{1,0:T(8,128)(2,1)S(1)} %collective-permute-done.5.theirs, bf16[1024,1024]{1,0:T(8,128)(2,1)S(1)} %get-tuple-element.19.near.refs_0_, bf16[1024,1024]{1,0:T(8,128)(2,1)S(1)} %get-tuple-element.20.far, ...), custom_call_target="tpu_custom_call" | custom-call | flops 536870912 | bytes 4194304 | tf_op jit(solution)/shard_map/mix/pallas_call | solution.py:151
  36.7 1.6 %collective-permute-start.7 = (bf16[128,1024]{1,0:T(8,128)(2,1)S(1)}, bf16[128,1024]{1,0:T(8,128)(2,1)S(1)}, u32[]{:S(2)}, u32[]{:S(2)}) collective-permute-start(bf16[128,1024]{1,0:T(8,128)(2,1)S(1)} %mix.8.refs_0_.mine), channel_id=1, source_target_pairs={{0,4},{1,5},{2,6},{3,7},{4,0},{5,1},{6,2},{7,3},{8,12},{9,13},{10,... | collective-permute-start | bytes 786440 | tf_op jit(solution)/shard_map/ppermute | solution.py:39
  38.4 5.1 %shard_map.77 = (bf16[1024,1024]{1,0:T(8,128)(2,1)S(1)}, bf16[1024,1024]{1,0:T(8,128)(2,1)S(1)}) custom-call(s32[5,16384]{1,0:T(8,128)S(1)} %copy-done.3, s32[16,1024]{1,0:T(8,128)S(1)} %reshape.3.cell_depth, f32[4]{0:T(128)S(1)} %copy-done.5, bf16[128,1024]{1,0:T(8,128)(2,1)S(1)} %mix.8.refs_0_.mine), custom_call_target="tpu_custom_call" | custom-call | flops 2013265920 | bytes 4194304 | tf_op jit(solution)/shard_map/pallas_call | solution.py:90
  43.5 0.7 %mix.9.refs_0_.mine = bf16[128,1024]{1,0:T(8,128)(2,1)S(1)} custom-call(bf16[128,1024]{1,0:T(8,128)(2,1)S(1)} %mix.7.refs_0_.mine, bf16[128,1024]{1,0:T(8,128)(2,1)S(1)} %collective-permute-done.4.theirs, bf16[1024,1024]{1,0:T(8,128)(2,1)S(1)} %get-tuple-element.19.near.refs_0_, bf16[1024,1024]{1,0:T(8,128)(2,1)S(1)} %get-tuple-element.20.far, ...), custom_call_target="tpu_custom_call" | custom-call | flops 536870912 | bytes 4194304 | tf_op jit(solution)/shard_map/mix/pallas_call | solution.py:151
  44.3 0.5 collective-permute-start.6
  44.8 11.3 %collective-permute-done.7.theirs = bf16[128,1024]{1,0:T(8,128)(2,1)S(1)} collective-permute-done((bf16[128,1024]{1,0:T(8,128)(2,1)S(1)}, bf16[128,1024]{1,0:T(8,128)(2,1)S(1)}, u32[]{:S(2)}, u32[]{:S(2)}) %collective-permute-start.7) | collective-permute-done | bytes 262176 | tf_op jit(solution)/shard_map/ppermute | solution.py:39
  56.1 0.7 %mix.10.refs_0_.state = bf16[128,1024]{1,0:T(8,128)(2,1)S(1)} custom-call(bf16[128,1024]{1,0:T(8,128)(2,1)S(1)} %mix.8.refs_0_.mine, bf16[128,1024]{1,0:T(8,128)(2,1)S(1)} %collective-permute-done.7.theirs, bf16[1024,1024]{1,0:T(8,128)(2,1)S(1)} %get-tuple-element.21.refs_0_.near, bf16[1024,1024]{1,0:T(8,128)(2,1)S(1)} %get-tuple-element.22.far, ...), custom_call_target="tpu_custom_call" | custom-call | flops 536870912 | bytes 4194304 | tf_op jit(solution)/shard_map/mix/pallas_call | solution.py:151
  56.8 4.9 %shard_map.78 = (bf16[1024,1024]{1,0:T(8,128)(2,1)S(1)}, bf16[1024,1024]{1,0:T(8,128)(2,1)S(1)}) custom-call(s32[5,16384]{1,0:T(8,128)S(1)} %copy-done.3, s32[16,1024]{1,0:T(8,128)S(1)} %reshape.3.cell_depth, f32[4]{0:T(128)S(1)} %copy-done.5, bf16[128,1024]{1,0:T(8,128)(2,1)S(1)} %mix.10.refs_0_.state), custom_call_target="tpu_custom_call" | custom-call | flops 2013265920 | bytes 4194304 | tf_op jit(solution)/shard_map/pallas_call | solution.py:90
  61.8 0.7 %mix.11.state = bf16[128,1024]{1,0:T(8,128)(2,1)S(1)} custom-call(bf16[128,1024]{1,0:T(8,128)(2,1)S(1)} %mix.9.refs_0_.mine, bf16[128,1024]{1,0:T(8,128)(2,1)S(1)} %collective-permute-done.6.theirs, bf16[1024,1024]{1,0:T(8,128)(2,1)S(1)} %get-tuple-element.21.refs_0_.near, bf16[1024,1024]{1,0:T(8,128)(2,1)S(1)} %get-tuple-element.22.far, ...), custom_call_target="tpu_custom_call" | custom-call | flops 536870912 | bytes 4194304 | tf_op jit(solution)/shard_map/mix/pallas_call | solution.py:151
  62.5 0.5 copy-done
  63.0 0.8 %shard_map.79 = (f32[1,1024]{1,0:T(1,128)S(1)}, f32[1,1024]{1,0:T(1,128)S(1)}) custom-call(bf16[128,1024]{1,0:T(8,128)(2,1)S(1)} %mix.10.refs_0_.state, bf16[1024,1024]{1,0:T(8,128)(2,1)S(1)} %get-tuple-element.23.refs_0_.near, bf16[1024,1024]{1,0:T(8,128)(2,1)S(1)} %get-tuple-element.24.far, s32[256,1024]{1,0:T(8,128)S(1)} %copy-done, ...), custom_call_target="tpu_custom_call" | custom-call | flops 536870912 | bytes 4194304 | tf_op jit(solution)/shard_map/pallas_call | solution.py:182
  63.8 0.8 %shard_map.80 = (f32[1,1024]{1,0:T(1,128)S(1)}, f32[1,1024]{1,0:T(1,128)S(1)}) custom-call(bf16[128,1024]{1,0:T(8,128)(2,1)S(1)} %mix.11.state, bf16[1024,1024]{1,0:T(8,128)(2,1)S(1)} %get-tuple-element.23.refs_0_.near, bf16[1024,1024]{1,0:T(8,128)(2,1)S(1)} %get-tuple-element.24.far, s32[256,1024]{1,0:T(8,128)S(1)} %copy-done, ...), custom_call_target="tpu_custom_call" | custom-call | flops 536870912 | bytes 4194304 | tf_op jit(solution)/shard_map/pallas_call | solution.py:182
  64.7 0.7 dynamic_slice.4
  65.4 3.7 %collective-permute-done.9 = f32[1,1024]{1,0:T(1,128)S(1)} collective-permute-done((f32[1,1024]{1,0:T(1,128)S(1)}, f32[1,1024]{1,0:T(1,128)S(1)}, u32[]{:S(2)}, u32[]{:S(2)}) %collective-permute-start.9) | collective-permute-done | bytes 4128 | tf_op jit(solution)/shard_map/ppermute | solution.py:39
  69.1 0.6 multiply_multiply_fusion
  (19 shorter events, 0.3 us)
Async XLA Ops:
  0.9 12.8 %collective-permute-start = (bf16[256,128]{1,0:T(8,128)(2,1)S(1)}, bf16[256,128]{1,0:T(8,128)(2,1)S(1)}, u32[]{:S(2)}, u32[]{:S(2)}) collective-permute-start(bf16[256,128]{1,0:T(8,128)(2,1)S(1)} %get-tuple-element.30), channel_id=1, source_target_pairs={{0,1},{1,2},{2,3},{3,4},{4,5},{5,6},{6,7},{7,8},{8,9},{9,10},{10,1... | collective-permute-start | bytes 196616 | tf_op jit(solution)/shard_map/ppermute | solution.py:35
  3.3 10.4 %collective-permute-start.1 = (bf16[256,128]{1,0:T(8,128)(2,1)S(1)}, bf16[256,128]{1,0:T(8,128)(2,1)S(1)}, u32[]{:S(2)}, u32[]{:S(2)}) collective-permute-start(bf16[256,128]{1,0:T(8,128)(2,1)S(1)} %get-tuple-element.29), channel_id=1, source_target_pairs={{1,0},{2,1},{3,2},{4,3},{5,4},{6,5},{7,6},{8,7},{9,8},{10,9},{11,1... | collective-permute-start | bytes 196616 | tf_op jit(solution)/shard_map/ppermute | solution.py:35
  6.8 1.0 %copy-start.2 = (s32[5,16384]{1,0:T(8,128)S(1)}, s32[5,16384]{1,0:T(8,128)}, u32[]{:S(2)}) copy-start(s32[5,16384]{1,0:T(8,128)} %cell_x.7) | copy-start | bytes 983044
  7.8 0.7 copy-start.5
  8.5 5.2 %copy-start.1 = (bf16[256,1024]{1,0:T(8,128)(2,1)S(1)}, bf16[256,1024]{1,0:T(8,128)(2,1)}, u32[]{:S(2)}) copy-start(bf16[256,1024]{1,0:T(8,128)(2,1)} %wave.3) | copy-start | bytes 1572868
  8.5 5.2 %copy-start.4 = (f32[256,65]{0,1:T(8,128)S(1)}, f32[256,65]{0,1:T(8,128)}, u32[]{:S(2)}) copy-start(f32[256,65]{0,1:T(8,128)} %param.8) | copy-start | bytes 199684
  16.7 6.4 %collective-permute-start.3 = (bf16[128,1024]{1,0:T(8,128)(2,1)S(1)}, bf16[128,1024]{1,0:T(8,128)(2,1)S(1)}, u32[]{:S(2)}, u32[]{:S(2)}) collective-permute-start(bf16[128,1024]{1,0:T(8,128)(2,1)S(1)} %shard_map.74.refs_0_.mine), channel_id=1, source_target_pairs={{0,1},{1,0},{2,3},{3,2},{4,5},{5,4},{6,7},{7,6},{8,9},{9,8},{10,11... | collective-permute-start | bytes 786440 | tf_op jit(solution)/shard_map/ppermute | solution.py:39
  22.9 5.6 %collective-permute-start.2 = (bf16[128,1024]{1,0:T(8,128)(2,1)S(1)}, bf16[128,1024]{1,0:T(8,128)(2,1)S(1)}, u32[]{:S(2)}, u32[]{:S(2)}) collective-permute-start(bf16[128,1024]{1,0:T(8,128)(2,1)S(1)} %shard_map.75.refs_0_.mine), channel_id=1, source_target_pairs={{0,1},{1,0},{2,3},{3,2},{4,5},{5,4},{6,7},{7,6},{8,9},{9,8},{10,11... | collective-permute-start | bytes 786440 | tf_op jit(solution)/shard_map/ppermute | solution.py:39
  23.8 7.0 %copy-start.3 = (s32[5,16384]{1,0:T(8,128)S(1)}, s32[5,16384]{1,0:T(8,128)}, u32[]{:S(2)}) copy-start(s32[5,16384]{1,0:T(8,128)} %cell_x.7) | copy-start | bytes 983044
  23.8 12.2 %collective-permute-start.5 = (bf16[128,1024]{1,0:T(8,128)(2,1)S(1)}, bf16[128,1024]{1,0:T(8,128)(2,1)S(1)}, u32[]{:S(2)}, u32[]{:S(2)}) collective-permute-start(bf16[128,1024]{1,0:T(8,128)(2,1)S(1)} %mix.6.refs_0_.mine), channel_id=1, source_target_pairs={{0,2},{1,3},{2,0},{3,1},{4,6},{5,7},{6,4},{7,5},{8,10},{9,11},{10,... | collective-permute-start | bytes 786440 | tf_op jit(solution)/shard_map/ppermute | solution.py:39
  26.0 36.5 %collective-permute-start.8 = (bf16[256,1024]{1,0:T(8,128)(2,1)S(1)}, bf16[256,1024]{1,0:T(8,128)(2,1)S(1)}, u32[]{:S(2)}, u32[]{:S(2)}) collective-permute-start(bf16[256,1024]{1,0:T(8,128)(2,1)S(1)} %compare_convert_fusion.refs_0_), channel_id=1, source_target_pairs={{0,8},{1,9},{2,10},{3,11},{4,12},{5,13},{6,14},{7,15},{8,0},{9,1},... | collective-permute-start | bytes 1572872 | tf_op jit(solution)/shard_map/ppermute | solution.py:39
  29.3 14.2 %collective-permute-start.4 = (bf16[128,1024]{1,0:T(8,128)(2,1)S(1)}, bf16[128,1024]{1,0:T(8,128)(2,1)S(1)}, u32[]{:S(2)}, u32[]{:S(2)}) collective-permute-start(bf16[128,1024]{1,0:T(8,128)(2,1)S(1)} %mix.7.refs_0_.mine), channel_id=1, source_target_pairs={{0,2},{1,3},{2,0},{3,1},{4,6},{5,7},{6,4},{7,5},{8,10},{9,11},{10,... | collective-permute-start | bytes 786440 | tf_op jit(solution)/shard_map/ppermute | solution.py:39
  36.7 19.4 %collective-permute-start.7 = (bf16[128,1024]{1,0:T(8,128)(2,1)S(1)}, bf16[128,1024]{1,0:T(8,128)(2,1)S(1)}, u32[]{:S(2)}, u32[]{:S(2)}) collective-permute-start(bf16[128,1024]{1,0:T(8,128)(2,1)S(1)} %mix.8.refs_0_.mine), channel_id=1, source_target_pairs={{0,4},{1,5},{2,6},{3,7},{4,0},{5,1},{6,2},{7,3},{8,12},{9,13},{10,... | collective-permute-start | bytes 786440 | tf_op jit(solution)/shard_map/ppermute | solution.py:39
  44.3 17.5 %collective-permute-start.6 = (bf16[128,1024]{1,0:T(8,128)(2,1)S(1)}, bf16[128,1024]{1,0:T(8,128)(2,1)S(1)}, u32[]{:S(2)}, u32[]{:S(2)}) collective-permute-start(bf16[128,1024]{1,0:T(8,128)(2,1)S(1)} %mix.9.refs_0_.mine), channel_id=1, source_target_pairs={{0,4},{1,5},{2,6},{3,7},{4,0},{5,1},{6,2},{7,3},{8,12},{9,13},{10,... | collective-permute-start | bytes 786440 | tf_op jit(solution)/shard_map/ppermute | solution.py:39
  61.8 1.2 %copy-start = (s32[256,1024]{1,0:T(8,128)S(1)}, s32[256,1024]{1,0:T(8,128)}, u32[]{:S(2)}) copy-start(s32[256,1024]{1,0:T(8,128)} %own_mask.3) | copy-start | bytes 3145732
  64.5 4.6 %collective-permute-start.9 = (f32[1,1024]{1,0:T(1,128)S(1)}, f32[1,1024]{1,0:T(1,128)S(1)}, u32[]{:S(2)}, u32[]{:S(2)}) collective-permute-start(f32[1,1024]{1,0:T(1,128)S(1)} %get-tuple-element.28), channel_id=1, source_target_pairs={{0,8},{1,9},{2,10},{3,11},{4,12},{5,13},{6,14},{7,15},{8,0},{9,1},... | collective-permute-start | bytes 12296 | tf_op jit(solution)/shard_map/ppermute | solution.py:39

commit v3 on v2

v3 whole, which is shorter than its diff:
```python
import functools
import math

import jax
import jax.numpy as jnp
from jax import lax
from jax.experimental import pallas as pl
from jax.experimental.pallas import tpu as pltpu
from jax.sharding import PartitionSpec as P


LEVELS = 4
BOXES = 16
LANES = 128

POLY_A = -0.55846636
POLY_B = 0.08535978
SCALE = -73.58594804
VMEM = pl.BlockSpec(memory_space=pltpu.VMEM)
ANY = pl.BlockSpec(memory_space=pl.ANY)
SMEM = pl.BlockSpec(memory_space=pltpu.SMEM)


def params(mib):
    return pltpu.CompilerParams(vmem_limit_bytes=mib << 20)


def cost(flops, moved, transcendentals=0):
    return pl.CostEstimate(flops=flops, bytes_accessed=moved, transcendentals=transcendentals)


def passed_along(shard, axis, by):
    devices = lax.axis_size(axis)
    pairs = [(i, i + by) for i in range(devices) if 0 <= i + by < devices]
    return lax.ppermute(shard, axis, pairs)


def partner(shard, axis, bit):
    return lax.ppermute(shard, axis, [(i, i ^ 1 << bit) for i in range(lax.axis_size(axis))])


def cosine(squared):
    u = squared * lax.rsqrt(squared)
    r = u - jnp.round(u)
    w = jnp.abs(r) - 0.25
    q = w * w
    return w * ((q + POLY_A) * q + POLY_B)


def boxes_of(level, blocks):
    box = lax.axis_index("space") // blocks
    bit = 1 << level
    upper = (box // bit) % 2
    return box, box + bit - 2 * bit * upper


ROW, OTHER_ROW, COLUMN, BELOW, OTHER_COLUMN, OTHER_BELOW = range(6)


def prepare_kernel(blocks, wave, aperture, cell_x, depth, slowness, *refs):
    head, tail, mask, coords, cells, depths, slow, marks, sems = refs
    width = wave.shape[1]
    tall = width // LANES
    box = boxes_of(0, blocks)[0]
    others = [boxes_of(level, blocks)[1] for level in range(LEVELS)]
    copies = [pltpu.make_async_copy(slowness, slow, sems.at[0])]
    for k, which in enumerate([box] + others):
        at = pl.ds(pl.multiple_of(which * width, width), width)
        copies.append(pltpu.make_async_copy(cell_x.at[:, at], cells.at[k], sems.at[1 + k]))
    for k, which in enumerate((box, others[-1])):
        at = pl.ds(pl.multiple_of(which * tall, tall), tall)
        copies.append(pltpu.make_async_copy(depth.at[at, :], depths.at[k], sems.at[6 + k]))
    late = [
        pltpu.make_async_copy(wave.at[:, pl.ds(0, LANES)], head, sems.at[8]),
        pltpu.make_async_copy(wave.at[:, pl.ds(width - LANES, LANES)], tail, sems.at[9]),
        pltpu.make_async_copy(aperture, marks, sems.at[10]),
    ]
    for copy in copies + late:
        copy.start()
    for copy in copies:
        copy.wait()
    coords[...] = jnp.zeros_like(coords)
    for level in range(LEVELS):
        turns = slow[level] * (0.5 / math.pi)
        base = 8 * level

        def put(kind, source, row):
            coords[base + kind : base + kind + 1, :] = (
                cells[source, row : row + 1, :].astype(jnp.float32) * turns
            )

        def put_below(kind, source):
            for k in range(tall):
                part = depths[source, k : k + 1, :].astype(jnp.float32) * turns
                coords[base + kind : base + kind + 1, k * LANES : (k + 1) * LANES] = part * part

        put(ROW, 0, level)
        put(OTHER_ROW, 1 + level, level)
        put(COLUMN, 0, level + 1)
        put_below(BELOW, 0)
        if level + 1 == LEVELS:
            put(OTHER_COLUMN, LEVELS, level + 1)
            put_below(OTHER_BELOW, 1)
    for copy in late:
        copy.wait()
    mask[...] = (marks[...] > 0).astype(jnp.float32).astype(jnp.bfloat16)


def prepare(blocks, wave, aperture, cell_x, depth, slowness):
    count, width = wave.shape
    levels = cell_x.shape[0]
    edge = jax.ShapeDtypeStruct((count, LANES), wave.dtype)
    return pl.pallas_call(
        functools.partial(prepare_kernel, blocks),
        out_shape=(
            edge,
            edge,
            jax.ShapeDtypeStruct((count, width), jnp.bfloat16),
            jax.ShapeDtypeStruct((8 * LEVELS, width), jnp.float32),
        ),
        in_specs=[ANY] * 5,
        out_specs=(VMEM,) * 4,
        scratch_shapes=[
            pltpu.VMEM((1 + LEVELS, levels, width), jnp.int32),
            pltpu.VMEM((2, width // LANES, LANES), jnp.int32),
            pltpu.SMEM((LEVELS,), jnp.float32),
            pltpu.VMEM((count, width), jnp.int32),
            pltpu.SemaphoreType.DMA((11,)),
        ],
        compiler_params=params(6),
        cost_estimate=cost(24 * 2 * width * width * 15, count * width * 8),
        name="prepare",
    )(wave, aperture, cell_x, depth, slowness)


def tables_kernel(jobs, step, coords, *refs):
    outs, rows = refs[-1 - len(jobs) : -1], refs[-1]
    width = outs[0].shape[0]
    steps = width // step

    def fill(slot, row, i):
        at = pl.ds(pl.multiple_of(i * step, step), step)
        rows[slot] = jnp.broadcast_to(coords[row : row + 1, at], (LANES, step)).T

    for (row, column, below), out in zip(jobs, outs):
        fill(0, row, 0)

        @pl.loop(0, steps)
        def _(i):
            at = pl.ds(pl.multiple_of(i * step, step), step)
            part = rows[i % 2]
            part = jnp.concatenate([part, part], 1)
            for c in range(0, width, 2 * LANES):
                columns = slice(c, c + 2 * LANES)
                across = part - coords[column : column + 1, columns]
                squared = across * across + coords[below : below + 1, columns]
                out[at, columns] = cosine(squared).astype(jnp.bfloat16)
            fill((i + 1) % 2, row, jnp.minimum(i + 1, steps - 1))


def tables(level, which, coords, *after):
    width = coords.shape[1]
    base = 8 * level
    near = (base + ROW, base + COLUMN, base + BELOW)
    far = (base + OTHER_ROW, base + COLUMN, base + BELOW)
    if level + 1 == LEVELS:
        far = (base + ROW, base + OTHER_COLUMN, base + OTHER_BELOW)
    jobs = [(near, far)[k] for k in which]
    shape = jax.ShapeDtypeStruct((width, width), jnp.bfloat16)
    step = LANES
    return pl.pallas_call(
        functools.partial(tables_kernel, jobs, step),
        out_shape=(shape,) * len(jobs),
        in_specs=[VMEM] + [ANY] * len(after),
        out_specs=(VMEM,) * len(jobs),
        scratch_shapes=[pltpu.VMEM((2, step, LANES), jnp.float32)],
        compiler_params=params(6),
        cost_estimate=cost(24 * len(jobs) * width * width * 40, 2 * len(jobs) * width * width),
    )(coords, *after)


def redatum_kernel(reach, below, wave, above, taps, *refs):
    out, padded = refs[-2:]
    count, width = wave.shape
    edge = below.shape[1]
    blocks = width // LANES
    halves = range(count // LANES)

    def held(lane):
        return slice(lane * LANES, (lane + 1) * LANES)

    def fill(source, x, start):
        for lane in halves:
            block = source[held(lane), pl.ds(x, LANES)].astype(jnp.float32)
            padded[lane, pl.ds(start, LANES), :] = block.T

    fill(below, 0, 0)
    fill(above, 0, edge + width)
    for k in range(min(2, blocks)):
        fill(wave, k * LANES, edge + k * LANES)

    @pl.loop(0, blocks)
    def _(block):
        base = pl.multiple_of(block * LANES, LANES)
        for lane in halves:
            total = None
            for j in range(taps.shape[0]):
                weight = jnp.broadcast_to(taps[j : j + 1, held(lane)], (LANES, LANES))
                term = weight * padded[lane, pl.ds(base + edge - reach + j, LANES), :]
                total = term if total is None else total + term
            out[held(lane), pl.ds(base, LANES)] = total.T.astype(out.dtype)
        ahead = pl.multiple_of(jnp.minimum(block + 2, blocks - 1) * LANES, LANES)
        fill(wave, ahead, edge + ahead)


def redatum(below, wave, above, taps, *after):
    count, width = wave.shape
    reach = (taps.shape[0] - 1) // 2
    long = width + 2 * below.shape[1]
    return pl.pallas_call(
        functools.partial(redatum_kernel, reach),
        out_shape=jax.ShapeDtypeStruct((count, width), jnp.bfloat16),
        in_specs=[VMEM] * 4 + [ANY] * len(after),
        out_specs=VMEM,
        scratch_shapes=[pltpu.VMEM((count // LANES, long, LANES), jnp.float32)],
        compiler_params=params(6),
        cost_estimate=cost(24 * 2 * width * width * 60, count * width * 4),
        name="redatum",
    )(below, wave, above, taps, *after)


def mix_kernel(held, mine, theirs, near, far, *refs):
    out = refs[-1]
    width = near.shape[1]
    scale = SCALE / math.sqrt(width)
    step = min(width, 256)
    for c in range(0, width, step):
        columns = slice(c, c + step)
        total = jnp.dot(mine[held, :], near[:, columns], preferred_element_type=jnp.float32)
        total += jnp.dot(theirs[held, :], far[:, columns], preferred_element_type=jnp.float32)
        out[:, columns] = (total * scale).astype(out.dtype)


def mix(part, mine, theirs, near, far, *after):
    count, width = mine.shape
    held = slice(part * LANES, (part + 1) * LANES) if count > LANES else slice(0, LANES)
    return pl.pallas_call(
        functools.partial(mix_kernel, held),
        out_shape=jax.ShapeDtypeStruct((LANES, width), jnp.bfloat16),
        in_specs=[VMEM] * 4 + [ANY] * len(after),
        out_specs=VMEM,
        compiler_params=params(7),
        cost_estimate=cost(24 * width * width * 15, 4 * width * width),
        name="mix",
    )(mine, theirs, near, far, *after)


def last_kernel(part, state, near, far, own_mask, far_mask, *refs):
    own, other = refs[-2:]
    width = near.shape[1]
    scale = SCALE / math.sqrt(width)
    step = min(width, 256)
    held = slice(part * LANES, (part + 1) * LANES)
    for k, (table, mask, out) in enumerate(((far, far_mask, other), (near, own_mask, own))):
        for c in range(0, width, step):
            columns = slice(c, c + step)
            mixed = jnp.dot(state[...], table[:, columns], preferred_element_type=jnp.float32)
            kept = jnp.where(mask[held, columns].astype(jnp.float32) > 0, mixed, 0.0)
            total = jnp.sum(kept, 0, keepdims=True) * scale
            if part > 0:
                total = total + refs[1 - k][:, columns]
            out[:, columns] = total


def last(part, state, near, far, own_mask, far_mask, sums, *after):
    count, width = state.shape
    shape = jax.ShapeDtypeStruct((1, width), jnp.float32)
    return pl.pallas_call(
        functools.partial(last_kernel, part),
        out_shape=(shape, shape),
        in_specs=[VMEM] * (5 + len(sums)) + [ANY] * len(after),
        out_specs=(VMEM, VMEM),
        compiler_params=params(8),
        cost_estimate=cost(4 * count * width * width, 4 * width * width),
    )(state, near, far, own_mask, far_mask, *sums, *after)


def on_device(wavefield, redatum_taps, cell_x, cell_depth, slowness, illumination, aperture):
    index = lax.axis_index("space")
    blocks = lax.axis_size("space") // BOXES
    block_bits = blocks.bit_length() - 1
    box = index // blocks
    block = index % blocks
    count, width = wavefield.shape
    depth = cell_depth.reshape(BOXES * width // LANES, LANES)
    head, tail, mask, coords = prepare(blocks, wavefield, aperture, cell_x, depth, slowness)
    below = passed_along(tail, "space", blocks)
    above = passed_along(head, "space", -blocks)
    masks = partner(mask, "space", LEVELS - 1 + block_bits)
    taps = redatum_taps
    if blocks > 1:
        taps = lax.dynamic_slice_in_dim(redatum_taps, block * count, count, 0)
    taps = taps.T
    parts = range(count // LANES)

    (near,) = tables(0, (0,), coords)
    state = redatum(below, wavefield, above, taps, near)
    received = partner(state, "space", block_bits)
    (far,) = tables(0, (1,), coords, state)
    states = [state for _ in parts]
    theirs = [received for _ in parts]
    table, ahead = (near, far), far
    for level in range(LEVELS - 1):
        for part in parts:
            states[part] = mix(part, states[part], theirs[part], *table, ahead)
            ahead = states[part]
            if level + 2 < LEVELS:
                theirs[part] = partner(states[part], "space", level + 1 + block_bits)
            if part == (len(parts) - 1 if level == 0 else 0):
                following = tables(level + 1, (0, 1), coords, ahead)
                ahead = following[0]
        table = following
    sums = ()
    for part in parts:
        sums = last(part, states[part], *table, mask, masks, sums)
    own, other = sums
    summed = own + partner(other, "space", LEVELS - 1 + block_bits)
    weights = lax.dynamic_slice_in_dim(illumination, box * width, width)
    image = summed * weights[None] / jnp.sqrt(jnp.float32(count * blocks))
    for level in range(block_bits):
        image = image + partner(image, "space", level)
    share = width // blocks
    return lax.dynamic_slice_in_dim(image, block * share, share, 1)


def solution(mesh):
    placed = (
        P(("groups", "space"), None),
        P("groups", None),
        P(),
        P(),
        P(),
        P("groups"),
        P(("groups", "space"), None),
    )
    return jax.shard_map(
        on_device,
        mesh=mesh,
        in_specs=placed,
        out_specs=P(("groups", "space"), None),
        check_vma=False,
    )
```

time: 70.1 us -> 68.9 us (0.983)
  waiting for transfers between devices: 15.1 us -> 17 us
  Pallas kernels: 32.3 us -> 30.9 us
  other arithmetic: 1.93 us -> 0.6 us
  starting transfers between devices: 15.6 us -> 14.3 us
  local copies, waits for them, and re-layouts: 4.6 us -> 5.51 us
    unnamed x12 -> x14, local copies, waits for them, and re-layouts: 2.17 us -> 4.81 us
    ppermute x2, waiting for transfers between devices: 0.01 us -> 1.76 us  [passed_along(): return lax.ppermute(shard, axis, pairs)]
    ppermute x8 -> x7, starting transfers between devices: 11.9 us -> 10.5 us  [partner(): lax.ppermute(shard, axis, [(i, i ^ 1 << bit) for i in range(lax.axis_size...]
    pallas_call x12 -> x13, Pallas kernels: 30.7 us -> 29.3 us  [the longest x5 17.3 us: tables(): pl.pallas_call(functools.partial(tables_kernel, jobs, step), out_shape=(s...]
    convert_element_type x1 -> x0, other arithmetic: 1.33 us -> none  [on_device(): mask = (aperture > 0).astype(jnp.bfloat16)]
    slice x1 -> x0, local copies, waits for them, and re-layouts: 0.88 us -> none  [on_device(): above = passed_along(wavefield[:, :LANES], 'space', -blocks)]
    reshape x1 -> x0, local copies, waits for them, and re-layouts: 0.86 us -> none  [on_device(): depths = cell_depth.reshape(BOXES, width)]
    ppermute x8 -> x7, waiting for transfers between devices: 15 us -> 15.3 us  [partner(): lax.ppermute(shard, axis, [(i, i ^ 1 << bit) for i in range(lax.axis_size...]
  transfers between devices with their start and end apart: 10 -> 9, of which waited for: 2 -> 3; matrix products, arithmetic and copies ran while one was open for 4% -> 1% of each run, Pallas kernels for 40% -> 31%
where the time goes in v3:
time: 68.9 us; the launch traced here: 68.5 us
  Pallas kernels  30.9 us (45%)
  waiting for transfers between devices  17 us (25%)
  starting transfers between devices  14.3 us (21%)
  local copies, waits for them, and re-layouts  5.51 us (8%)
    pallas_call x5, Pallas kernels, tables(): pl.pallas_call(functools.partial(tables_kernel, jobs, step), out_shape=(s...  17.3 us
    ppermute x7, waiting for transfers between devices, partner(): lax.ppermute(shard, axis, [(i, i ^ 1 << bit) for i in range(lax.axis_size...  15.3 us
    ppermute x7, starting transfers between devices, partner(): lax.ppermute(shard, axis, [(i, i ^ 1 << bit) for i in range(lax.axis_size...  10.5 us
    pallas_call x1, Pallas kernels, redatum(): pl.pallas_call(functools.partial(redatum_kernel, reach), out_shape=jax.Sh...  6.92 us
    unnamed x14, local copies, waits for them, and re-layouts  4.81 us
    pallas_call x6, Pallas kernels, mix(): pl.pallas_call(functools.partial(mix_kernel, held), out_shape=jax.ShapeDt...  4.34 us
    ppermute x2, starting transfers between devices, passed_along(): return lax.ppermute(shard, axis, pairs)  3.82 us
    ppermute x2, waiting for transfers between devices, passed_along(): return lax.ppermute(shard, axis, pairs)  1.76 us
  transfers between devices with their start and end apart: 9, of which 3 were waited for; matrix products, arithmetic and copies ran while one was open for 1% of the time, Pallas kernels for 31%

profile of v3, /device:TPU:0, one launch (start us, length us, event | category | flops | bytes accessed | tf_op | source)
XLA Modules:
  0.0 68.5 jit_solution(10711816437209795360)
XLA Ops:
  0.0 1.2 %copy-done = s32[256,1024]{1,0:T(8,128)S(1)} copy-done((s32[256,1024]{1,0:T(8,128)S(1)}, s32[256,1024]{1,0:T(8,128)}, u32[]{:S(2)}) %copy-start) | copy-done | bytes 1048600
  1.2 1.0 %copy-done.1 = s32[5,16384]{1,0:T(8,128)S(1)} copy-done((s32[5,16384]{1,0:T(8,128)S(1)}, s32[5,16384]{1,0:T(8,128)}, u32[]{:S(2)}) %copy-start.1) | copy-done | bytes 327704
  2.3 1.0 %copy-done.2 = bf16[256,1024]{1,0:T(8,128)(2,1)S(1)} copy-done((bf16[256,1024]{1,0:T(8,128)(2,1)S(1)}, bf16[256,1024]{1,0:T(8,128)(2,1)}, u32[]{:S(2)}) %copy-start.2) | copy-done | bytes 524312
  3.3 0.8 %copy-done.5 = s32[16384]{0:T(1024)S(1)} copy-done((s32[16384]{0:T(1024)S(1)}, s32[16384]{0:T(1024)}, u32[]{:S(2)}) %copy-start.5) | copy-done | bytes 65560
  4.2 0.7 copy-done.6
  4.8 0.8 %prepare.1 = (bf16[256,128]{1,0:T(8,128)(2,1)S(1)}, bf16[256,128]{1,0:T(8,128)(2,1)S(1)}, bf16[256,1024]{1,0:T(8,128)(2,1)S(1)}, f32[32,1024]{1,0:T(8,128)S(1)}) custom-call(bf16[256,1024]{1,0:T(8,128)(2,1)S(1)} %copy-done.2, s32[256,1024]{1,0:T(8,128)S(1)} %copy-done, s32[5,16384]{1,0:T(8,128)S(1)} %copy-done.1, s32[128,128]{1,0:T(8,128)S(1)} %bitcast.4, ...), custom_call_target="tpu_custom_call" | custom-call | flops 754974720 | bytes 2097152 | tf_op jit(solution)/shard_map/prepare/pallas_call | solution.py:113
  5.6 2.5 %collective-permute-start = (bf16[256,128]{1,0:T(8,128)(2,1)S(1)}, bf16[256,128]{1,0:T(8,128)(2,1)S(1)}, u32[]{:S(2)}, u32[]{:S(2)}) collective-permute-start(bf16[256,128]{1,0:T(8,128)(2,1)S(1)} %get-tuple-element.19), channel_id=1, source_target_pairs={{0,1},{1,2},{2,3},{3,4},{4,5},{5,6},{6,7},{7,8},{8,9},{9,10},{10,1... | collective-permute-start | bytes 196616 | tf_op jit(solution)/shard_map/ppermute | solution.py:35
  8.1 1.3 %collective-permute-start.1 = (bf16[256,128]{1,0:T(8,128)(2,1)S(1)}, bf16[256,128]{1,0:T(8,128)(2,1)S(1)}, u32[]{:S(2)}, u32[]{:S(2)}) collective-permute-start(bf16[256,128]{1,0:T(8,128)(2,1)S(1)} %get-tuple-element.20), channel_id=1, source_target_pairs={{1,0},{2,1},{3,2},{4,3},{5,4},{6,5},{7,6},{8,7},{9,8},{10,9},{11,1... | collective-permute-start | bytes 196616 | tf_op jit(solution)/shard_map/ppermute | solution.py:35
  9.4 2.2 %shard_map.73.refs_0_.near = bf16[1024,1024]{1,0:T(8,128)(2,1)S(1)} custom-call(f32[32,1024]{1,0:T(8,128)S(1)} %get-tuple-element.21.coords), custom_call_target="tpu_custom_call" | custom-call | flops 1006632960 | bytes 2097152 | tf_op jit(solution)/shard_map/pallas_call | solution.py:171
  11.6 1.8 %collective-permute-done.1.above = bf16[256,128]{1,0:T(8,128)(2,1)S(1)} collective-permute-done((bf16[256,128]{1,0:T(8,128)(2,1)S(1)}, bf16[256,128]{1,0:T(8,128)(2,1)S(1)}, u32[]{:S(2)}, u32[]{:S(2)}) %collective-permute-start.1) | collective-permute-done | bytes 65568 | tf_op jit(solution)/shard_map/ppermute | solution.py:35
  13.4 6.9 %redatum.1.refs_0_.mine = bf16[256,1024]{1,0:T(8,128)(2,1)S(1)} custom-call(bf16[256,128]{1,0:T(8,128)(2,1)S(1)} %collective-permute-done.below, bf16[256,1024]{1,0:T(8,128)(2,1)S(1)} %copy-done.3, bf16[256,128]{1,0:T(8,128)(2,1)S(1)} %collective-permute-done.1.above, f32[65,256]{1,0:T(8,128)S(1)} %bitcast.3, bf16[1024,1024]{1,0:T(8,128)(2,1)S(1)} %shard_map.73.refs_0_.near), custom_call_target="tpu_custom_call" | custom-call | flops 3019898880 | bytes 1048576 | tf_op jit(solution)/shard_map/redatum/pallas_call | solution.py:220
  20.3 3.0 %collective-permute-start.2 = (bf16[256,1024]{1,0:T(8,128)(2,1)S(1)}, bf16[256,1024]{1,0:T(8,128)(2,1)S(1)}, u32[]{:S(2)}, u32[]{:S(2)}) collective-permute-start(bf16[256,1024]{1,0:T(8,128)(2,1)S(1)} %redatum.1.refs_0_.mine), channel_id=1, source_target_pairs={{0,1},{1,0},{2,3},{3,2},{4,5},{5,4},{6,7},{7,6},{8,9},{9,8},{10,11... | collective-permute-start | bytes 1572872 | tf_op jit(solution)/shard_map/ppermute | solution.py:39
  23.3 2.2 %shard_map.74.far.refs_0_ = bf16[1024,1024]{1,0:T(8,128)(2,1)S(1)} custom-call(f32[32,1024]{1,0:T(8,128)S(1)} %get-tuple-element.21.coords, bf16[256,1024]{1,0:T(8,128)(2,1)S(1)} %redatum.1.refs_0_.mine), custom_call_target="tpu_custom_call" | custom-call | flops 1006632960 | bytes 2097152 | tf_op jit(solution)/shard_map/pallas_call | solution.py:171
  25.5 0.7 %mix.6.refs_0_.mine = bf16[128,1024]{1,0:T(8,128)(2,1)S(1)} custom-call(bf16[256,1024]{1,0:T(8,128)(2,1)S(1)} %redatum.1.refs_0_.mine, bf16[256,1024]{1,0:T(8,128)(2,1)S(1)} %collective-permute-done.2.theirs, bf16[1024,1024]{1,0:T(8,128)(2,1)S(1)} %shard_map.73.refs_0_.near, bf16[1024,1024]{1,0:T(8,128)(2,1)S(1)} %shard_map.74.far.refs_0_, ...), custom_call_target="tpu_custom_call" | custom-call | flops 377487360 | bytes 4194304 | tf_op jit(solution)/shard_map/mix/pallas_call | solution.py:247
  26.2 2.5 %collective-permute-start.4 = (bf16[128,1024]{1,0:T(8,128)(2,1)S(1)}, bf16[128,1024]{1,0:T(8,128)(2,1)S(1)}, u32[]{:S(2)}, u32[]{:S(2)}) collective-permute-start(bf16[128,1024]{1,0:T(8,128)(2,1)S(1)} %mix.6.refs_0_.mine), channel_id=1, source_target_pairs={{0,2},{1,3},{2,0},{3,1},{4,6},{5,7},{6,4},{7,5},{8,10},{9,11},{10,... | collective-permute-start | bytes 786440 | tf_op jit(solution)/shard_map/ppermute | solution.py:39
  28.7 2.6 %collective-permute-start.7 = (bf16[256,1024]{1,0:T(8,128)(2,1)S(1)}, bf16[256,1024]{1,0:T(8,128)(2,1)S(1)}, u32[]{:S(2)}, u32[]{:S(2)}) collective-permute-start(bf16[256,1024]{1,0:T(8,128)(2,1)S(1)} %get-tuple-element.28.own_mask), channel_id=1, source_target_pairs={{0,8},{1,9},{2,10},{3,11},{4,12},{5,13},{6,14},{7,15},{8,0},{9,1},... | collective-permute-start | bytes 1572872 | tf_op jit(solution)/shard_map/ppermute | solution.py:39
  31.3 0.7 %mix.7.refs_0_.mine = bf16[128,1024]{1,0:T(8,128)(2,1)S(1)} custom-call(bf16[256,1024]{1,0:T(8,128)(2,1)S(1)} %redatum.1.refs_0_.mine, bf16[256,1024]{1,0:T(8,128)(2,1)S(1)} %collective-permute-done.2.theirs, bf16[1024,1024]{1,0:T(8,128)(2,1)S(1)} %shard_map.73.refs_0_.near, bf16[1024,1024]{1,0:T(8,128)(2,1)S(1)} %shard_map.74.far.refs_0_, ...), custom_call_target="tpu_custom_call" | custom-call | flops 377487360 | bytes 4194304 | tf_op jit(solution)/shard_map/mix/pallas_call | solution.py:247
  32.2 4.3 %shard_map.75 = (bf16[1024,1024]{1,0:T(8,128)(2,1)S(1)}, bf16[1024,1024]{1,0:T(8,128)(2,1)S(1)}) custom-call(f32[32,1024]{1,0:T(8,128)S(1)} %get-tuple-element.21.coords, bf16[128,1024]{1,0:T(8,128)(2,1)S(1)} %mix.7.refs_0_.mine), custom_call_target="tpu_custom_call" | custom-call | flops 2013265920 | bytes 4194304 | tf_op jit(solution)/shard_map/pallas_call | solution.py:171
  36.6 0.7 %mix.8.refs_0_.mine = bf16[128,1024]{1,0:T(8,128)(2,1)S(1)} custom-call(bf16[128,1024]{1,0:T(8,128)(2,1)S(1)} %mix.6.refs_0_.mine, bf16[128,1024]{1,0:T(8,128)(2,1)S(1)} %collective-permute-done.4.theirs, bf16[1024,1024]{1,0:T(8,128)(2,1)S(1)} %get-tuple-element.22.near.refs_0_, bf16[1024,1024]{1,0:T(8,128)(2,1)S(1)} %get-tuple-element.23.far, ...), custom_call_target="tpu_custom_call" | custom-call | flops 377487360 | bytes 4194304 | tf_op jit(solution)/shard_map/mix/pallas_call | solution.py:247
  37.3 1.2 %collective-permute-start.6 = (bf16[128,1024]{1,0:T(8,128)(2,1)S(1)}, bf16[128,1024]{1,0:T(8,128)(2,1)S(1)}, u32[]{:S(2)}, u32[]{:S(2)}) collective-permute-start(bf16[128,1024]{1,0:T(8,128)(2,1)S(1)} %mix.8.refs_0_.mine), channel_id=1, source_target_pairs={{0,4},{1,5},{2,6},{3,7},{4,0},{5,1},{6,2},{7,3},{8,12},{9,13},{10,... | collective-permute-start | bytes 786440 | tf_op jit(solution)/shard_map/ppermute | solution.py:39
  38.4 4.3 %shard_map.76 = (bf16[1024,1024]{1,0:T(8,128)(2,1)S(1)}, bf16[1024,1024]{1,0:T(8,128)(2,1)S(1)}) custom-call(f32[32,1024]{1,0:T(8,128)S(1)} %get-tuple-element.21.coords, bf16[128,1024]{1,0:T(8,128)(2,1)S(1)} %mix.8.refs_0_.mine), custom_call_target="tpu_custom_call" | custom-call | flops 2013265920 | bytes 4194304 | tf_op jit(solution)/shard_map/pallas_call | solution.py:171
  42.8 0.7 %mix.9.refs_0_.mine = bf16[128,1024]{1,0:T(8,128)(2,1)S(1)} custom-call(bf16[128,1024]{1,0:T(8,128)(2,1)S(1)} %mix.7.refs_0_.mine, bf16[128,1024]{1,0:T(8,128)(2,1)S(1)} %collective-permute-done.3.theirs, bf16[1024,1024]{1,0:T(8,128)(2,1)S(1)} %get-tuple-element.22.near.refs_0_, bf16[1024,1024]{1,0:T(8,128)(2,1)S(1)} %get-tuple-element.23.far, ...), custom_call_target="tpu_custom_call" | custom-call | flops 377487360 | bytes 4194304 | tf_op jit(solution)/shard_map/mix/pallas_call | solution.py:247
  43.5 1.0 %collective-permute-start.5 = (bf16[128,1024]{1,0:T(8,128)(2,1)S(1)}, bf16[128,1024]{1,0:T(8,128)(2,1)S(1)}, u32[]{:S(2)}, u32[]{:S(2)}) collective-permute-start(bf16[128,1024]{1,0:T(8,128)(2,1)S(1)} %mix.9.refs_0_.mine), channel_id=1, source_target_pairs={{0,4},{1,5},{2,6},{3,7},{4,0},{5,1},{6,2},{7,3},{8,12},{9,13},{10,... | collective-permute-start | bytes 786440 | tf_op jit(solution)/shard_map/ppermute | solution.py:39
  44.5 11.5 %collective-permute-done.6.theirs = bf16[128,1024]{1,0:T(8,128)(2,1)S(1)} collective-permute-done((bf16[128,1024]{1,0:T(8,128)(2,1)S(1)}, bf16[128,1024]{1,0:T(8,128)(2,1)S(1)}, u32[]{:S(2)}, u32[]{:S(2)}) %collective-permute-start.6) | collective-permute-done | bytes 262176 | tf_op jit(solution)/shard_map/ppermute | solution.py:39
  56.0 0.7 %mix.10.refs_0_.state = bf16[128,1024]{1,0:T(8,128)(2,1)S(1)} custom-call(bf16[128,1024]{1,0:T(8,128)(2,1)S(1)} %mix.8.refs_0_.mine, bf16[128,1024]{1,0:T(8,128)(2,1)S(1)} %collective-permute-done.6.theirs, bf16[1024,1024]{1,0:T(8,128)(2,1)S(1)} %get-tuple-element.24.refs_0_.near, bf16[1024,1024]{1,0:T(8,128)(2,1)S(1)} %get-tuple-element.25.far, ...), custom_call_target="tpu_custom_call" | custom-call | flops 377487360 | bytes 4194304 | tf_op jit(solution)/shard_map/mix/pallas_call | solution.py:247
  56.7 4.3 %shard_map.77 = (bf16[1024,1024]{1,0:T(8,128)(2,1)S(1)}, bf16[1024,1024]{1,0:T(8,128)(2,1)S(1)}) custom-call(f32[32,1024]{1,0:T(8,128)S(1)} %get-tuple-element.21.coords, bf16[128,1024]{1,0:T(8,128)(2,1)S(1)} %mix.10.refs_0_.state), custom_call_target="tpu_custom_call" | custom-call | flops 2013265920 | bytes 4194304 | tf_op jit(solution)/shard_map/pallas_call | solution.py:171
  61.1 0.7 %mix.11.state = bf16[128,1024]{1,0:T(8,128)(2,1)S(1)} custom-call(bf16[128,1024]{1,0:T(8,128)(2,1)S(1)} %mix.9.refs_0_.mine, bf16[128,1024]{1,0:T(8,128)(2,1)S(1)} %collective-permute-done.5.theirs, bf16[1024,1024]{1,0:T(8,128)(2,1)S(1)} %get-tuple-element.24.refs_0_.near, bf16[1024,1024]{1,0:T(8,128)(2,1)S(1)} %get-tuple-element.25.far, ...), custom_call_target="tpu_custom_call" | custom-call | flops 377487360 | bytes 4194304 | tf_op jit(solution)/shard_map/mix/pallas_call | solution.py:247
  61.8 0.8 %shard_map.78 = (f32[1,1024]{1,0:T(1,128)S(1)}, f32[1,1024]{1,0:T(1,128)S(1)}) custom-call(bf16[128,1024]{1,0:T(8,128)(2,1)S(1)} %mix.10.refs_0_.state, bf16[1024,1024]{1,0:T(8,128)(2,1)S(1)} %get-tuple-element.26.refs_0_.near, bf16[1024,1024]{1,0:T(8,128)(2,1)S(1)} %get-tuple-element.27.far, bf16[256,1024]{1,0:T(8,128)(2,1)S(1)} %get-tuple-element.28.own_mask, ...), custom_call_target="tpu_custom_call" | custom-call | flops 536870912 | bytes 4194304 | tf_op jit(solution)/shard_map/pallas_call | solution.py:278
  62.6 0.8 %shard_map.79 = (f32[1,1024]{1,0:T(1,128)S(1)}, f32[1,1024]{1,0:T(1,128)S(1)}) custom-call(bf16[128,1024]{1,0:T(8,128)(2,1)S(1)} %mix.11.state, bf16[1024,1024]{1,0:T(8,128)(2,1)S(1)} %get-tuple-element.26.refs_0_.near, bf16[1024,1024]{1,0:T(8,128)(2,1)S(1)} %get-tuple-element.27.far, bf16[256,1024]{1,0:T(8,128)(2,1)S(1)} %get-tuple-element.28.own_mask, ...), custom_call_target="tpu_custom_call" | custom-call | flops 536870912 | bytes 4194304 | tf_op jit(solution)/shard_map/pallas_call | solution.py:278
  63.4 0.7 %dynamic_slice.4 = f32[1024]{0:T(1024)S(1)} dynamic-slice(f32[16384]{0:T(1024)} %param.12, s32[]{:T(128)S(6)} %select_n.11), dynamic_slice_sizes={1024} | dynamic-slice | bytes 8196 | tf_op jit(solution)/shard_map/dynamic_slice | solution.py:328
  64.1 3.8 %collective-permute-done.8 = f32[1,1024]{1,0:T(1,128)S(1)} collective-permute-done((f32[1,1024]{1,0:T(1,128)S(1)}, f32[1,1024]{1,0:T(1,128)S(1)}, u32[]{:S(2)}, u32[]{:S(2)}) %collective-permute-start.8) | collective-permute-done | bytes 4128 | tf_op jit(solution)/shard_map/ppermute | solution.py:39
  67.9 0.6 multiply_multiply_fusion
  (17 shorter events, 0.2 us)
Async XLA Ops:
  0.0 1.2 %copy-start = (s32[256,1024]{1,0:T(8,128)S(1)}, s32[256,1024]{1,0:T(8,128)}, u32[]{:S(2)}) copy-start(s32[256,1024]{1,0:T(8,128)} %aperture.1) | copy-start | bytes 3145732
  1.2 1.0 %copy-start.1 = (s32[5,16384]{1,0:T(8,128)S(1)}, s32[5,16384]{1,0:T(8,128)}, u32[]{:S(2)}) copy-start(s32[5,16384]{1,0:T(8,128)} %cell_x.1) | copy-start | bytes 983044
  2.3 1.0 %copy-start.2 = (bf16[256,1024]{1,0:T(8,128)(2,1)S(1)}, bf16[256,1024]{1,0:T(8,128)(2,1)}, u32[]{:S(2)}) copy-start(bf16[256,1024]{1,0:T(8,128)(2,1)} %wave.3) | copy-start | bytes 1572868
  3.3 0.8 %copy-start.5 = (s32[16384]{0:T(1024)S(1)}, s32[16384]{0:T(1024)}, u32[]{:S(2)}) copy-start(s32[16384]{0:T(1024)} %param.10) | copy-start | bytes 196612
  4.2 0.7 copy-start.6
  5.6 7.8 %copy-start.3 = (bf16[256,1024]{1,0:T(8,128)(2,1)S(1)}, bf16[256,1024]{1,0:T(8,128)(2,1)}, u32[]{:S(2)}) copy-start(bf16[256,1024]{1,0:T(8,128)(2,1)} %wave.3) | copy-start | bytes 1572868
  5.6 7.8 %copy-start.4 = (f32[256,65]{0,1:T(8,128)S(1)}, f32[256,65]{0,1:T(8,128)}, u32[]{:S(2)}) copy-start(f32[256,65]{0,1:T(8,128)} %param.8) | copy-start | bytes 199684
  5.6 6.0 %collective-permute-start = (bf16[256,128]{1,0:T(8,128)(2,1)S(1)}, bf16[256,128]{1,0:T(8,128)(2,1)S(1)}, u32[]{:S(2)}, u32[]{:S(2)}) collective-permute-start(bf16[256,128]{1,0:T(8,128)(2,1)S(1)} %get-tuple-element.19), channel_id=1, source_target_pairs={{0,1},{1,2},{2,3},{3,4},{4,5},{5,6},{6,7},{7,8},{8,9},{9,10},{10,1... | collective-permute-start | bytes 196616 | tf_op jit(solution)/shard_map/ppermute | solution.py:35
  8.1 5.2 %collective-permute-start.1 = (bf16[256,128]{1,0:T(8,128)(2,1)S(1)}, bf16[256,128]{1,0:T(8,128)(2,1)S(1)}, u32[]{:S(2)}, u32[]{:S(2)}) collective-permute-start(bf16[256,128]{1,0:T(8,128)(2,1)S(1)} %get-tuple-element.20), channel_id=1, source_target_pairs={{1,0},{2,1},{3,2},{4,3},{5,4},{6,5},{7,6},{8,7},{9,8},{10,9},{11,1... | collective-permute-start | bytes 196616 | tf_op jit(solution)/shard_map/ppermute | solution.py:35
  20.3 5.2 %collective-permute-start.2 = (bf16[256,1024]{1,0:T(8,128)(2,1)S(1)}, bf16[256,1024]{1,0:T(8,128)(2,1)S(1)}, u32[]{:S(2)}, u32[]{:S(2)}) collective-permute-start(bf16[256,1024]{1,0:T(8,128)(2,1)S(1)} %redatum.1.refs_0_.mine), channel_id=1, source_target_pairs={{0,1},{1,0},{2,3},{3,2},{4,5},{5,4},{6,7},{7,6},{8,9},{9,8},{10,11... | collective-permute-start | bytes 1572872 | tf_op jit(solution)/shard_map/ppermute | solution.py:39
  26.2 10.3 %collective-permute-start.4 = (bf16[128,1024]{1,0:T(8,128)(2,1)S(1)}, bf16[128,1024]{1,0:T(8,128)(2,1)S(1)}, u32[]{:S(2)}, u32[]{:S(2)}) collective-permute-start(bf16[128,1024]{1,0:T(8,128)(2,1)S(1)} %mix.6.refs_0_.mine), channel_id=1, source_target_pairs={{0,2},{1,3},{2,0},{3,1},{4,6},{5,7},{6,4},{7,5},{8,10},{9,11},{10,... | collective-permute-start | bytes 786440 | tf_op jit(solution)/shard_map/ppermute | solution.py:39
  28.7 33.1 %collective-permute-start.7 = (bf16[256,1024]{1,0:T(8,128)(2,1)S(1)}, bf16[256,1024]{1,0:T(8,128)(2,1)S(1)}, u32[]{:S(2)}, u32[]{:S(2)}) collective-permute-start(bf16[256,1024]{1,0:T(8,128)(2,1)S(1)} %get-tuple-element.28.own_mask), channel_id=1, source_target_pairs={{0,8},{1,9},{2,10},{3,11},{4,12},{5,13},{6,14},{7,15},{8,0},{9,1},... | collective-permute-start | bytes 1572872 | tf_op jit(solution)/shard_map/ppermute | solution.py:39
  32.1 10.7 %collective-permute-start.3 = (bf16[128,1024]{1,0:T(8,128)(2,1)S(1)}, bf16[128,1024]{1,0:T(8,128)(2,1)S(1)}, u32[]{:S(2)}, u32[]{:S(2)}) collective-permute-start(bf16[128,1024]{1,0:T(8,128)(2,1)S(1)} %mix.7.refs_0_.mine), channel_id=1, source_target_pairs={{0,2},{1,3},{2,0},{3,1},{4,6},{5,7},{6,4},{7,5},{8,10},{9,11},{10,... | collective-permute-start | bytes 786440 | tf_op jit(solution)/shard_map/ppermute | solution.py:39
  37.3 18.7 %collective-permute-start.6 = (bf16[128,1024]{1,0:T(8,128)(2,1)S(1)}, bf16[128,1024]{1,0:T(8,128)(2,1)S(1)}, u32[]{:S(2)}, u32[]{:S(2)}) collective-permute-start(bf16[128,1024]{1,0:T(8,128)(2,1)S(1)} %mix.8.refs_0_.mine), channel_id=1, source_target_pairs={{0,4},{1,5},{2,6},{3,7},{4,0},{5,1},{6,2},{7,3},{8,12},{9,13},{10,... | collective-permute-start | bytes 786440 | tf_op jit(solution)/shard_map/ppermute | solution.py:39
  43.5 17.5 %collective-permute-start.5 = (bf16[128,1024]{1,0:T(8,128)(2,1)S(1)}, bf16[128,1024]{1,0:T(8,128)(2,1)S(1)}, u32[]{:S(2)}, u32[]{:S(2)}) collective-permute-start(bf16[128,1024]{1,0:T(8,128)(2,1)S(1)} %mix.9.refs_0_.mine), channel_id=1, source_target_pairs={{0,4},{1,5},{2,6},{3,7},{4,0},{5,1},{6,2},{7,3},{8,12},{9,13},{10,... | collective-permute-start | bytes 786440 | tf_op jit(solution)/shard_map/ppermute | solution.py:39
  63.4 4.6 %collective-permute-start.8 = (f32[1,1024]{1,0:T(1,128)S(1)}, f32[1,1024]{1,0:T(1,128)S(1)}, u32[]{:S(2)}, u32[]{:S(2)}) collective-permute-start(f32[1,1024]{1,0:T(1,128)S(1)} %get-tuple-element.32), channel_id=1, source_target_pairs={{0,8},{1,9},{2,10},{3,11},{4,12},{5,13},{6,14},{7,15},{8,0},{9,1},... | collective-permute-start | bytes 12296 | tf_op jit(solution)/shard_map/ppermute | solution.py:39

commit v4 on v3

--- a/solution.py
+++ b/solution.py
@@ -17,7 +17,9 @@
 POLY_B = 0.08535978
 SCALE = -73.58594804
 VMEM = pl.BlockSpec(memory_space=pltpu.VMEM)
+GRANT = 56 << 20
 ANY = pl.BlockSpec(memory_space=pl.ANY)
+HBM = pl.BlockSpec(memory_space=pltpu.HBM)
 SMEM = pl.BlockSpec(memory_space=pltpu.SMEM)
 
 
@@ -118,7 +120,7 @@
             jax.ShapeDtypeStruct((count, width), jnp.bfloat16),
             jax.ShapeDtypeStruct((8 * LEVELS, width), jnp.float32),
         ),
-        in_specs=[ANY] * 5,
+        in_specs=[HBM] * 5,
         out_specs=(VMEM,) * 4,
         scratch_shapes=[
             pltpu.VMEM((1 + LEVELS, levels, width), jnp.int32),
@@ -127,7 +129,7 @@
             pltpu.VMEM((count, width), jnp.int32),
             pltpu.SemaphoreType.DMA((11,)),
         ],
-        compiler_params=params(6),
+        compiler_params=pltpu.CompilerParams(vmem_limit_bytes=GRANT),
         cost_estimate=cost(24 * 2 * width * width * 15, count * width * 8),
         name="prepare",
     )(wave, aperture, cell_x, depth, slowness)
@@ -186,31 +188,29 @@
     blocks = width // LANES
     halves = range(count // LANES)
 
-    def held(lane):
-        return slice(lane * LANES, (lane + 1) * LANES)
-
-    def fill(source, x, start):
-        for lane in halves:
-            block = source[held(lane), pl.ds(x, LANES)].astype(jnp.float32)
-            padded[lane, pl.ds(start, LANES), :] = block.T
-
-    fill(below, 0, 0)
-    fill(above, 0, edge + width)
-    for k in range(min(2, blocks)):
-        fill(wave, k * LANES, edge + k * LANES)
-
-    @pl.loop(0, blocks)
-    def _(block):
-        base = pl.multiple_of(block * LANES, LANES)
-        for lane in halves:
+    def fill(lane, source, x, start):
+        held = slice(lane * LANES, (lane + 1) * LANES)
+        block = source[held, pl.ds(x, LANES)].astype(jnp.float32)
+        padded[lane, pl.ds(start, LANES), :] = block.T
+
+    for lane in halves:
+        held = slice(lane * LANES, (lane + 1) * LANES)
+        fill(lane, below, 0, 0)
+        fill(lane, above, 0, edge + width)
+        for k in range(min(2, blocks)):
+            fill(lane, wave, k * LANES, edge + k * LANES)
+
+        @pl.loop(0, blocks)
+        def _(block):
+            base = pl.multiple_of(block * LANES, LANES)
             total = None
             for j in range(taps.shape[0]):
-                weight = jnp.broadcast_to(taps[j : j + 1, held(lane)], (LANES, LANES))
+                weight = jnp.broadcast_to(taps[j : j + 1, held], (LANES, LANES))
                 term = weight * padded[lane, pl.ds(base + edge - reach + j, LANES), :]
                 total = term if total is None else total + term
-            out[held(lane), pl.ds(base, LANES)] = total.T.astype(out.dtype)
-        ahead = pl.multiple_of(jnp.minimum(block + 2, blocks - 1) * LANES, LANES)
-        fill(wave, ahead, edge + ahead)
+            out[held, pl.ds(base, LANES)] = total.T.astype(out.dtype)
+            ahead = pl.multiple_of(jnp.minimum(block + 2, blocks - 1) * LANES, LANES)
+            fill(lane, wave, ahead, edge + ahead)
 
 
 def redatum(below, wave, above, taps, *after):
@@ -296,7 +296,6 @@
     head, tail, mask, coords = prepare(blocks, wavefield, aperture, cell_x, depth, slowness)
     below = passed_along(tail, "space", blocks)
     above = passed_along(head, "space", -blocks)
-    masks = partner(mask, "space", LEVELS - 1 + block_bits)
     taps = redatum_taps
     if blocks > 1:
         taps = lax.dynamic_slice_in_dim(redatum_taps, block * count, count, 0)
@@ -304,6 +303,8 @@
     parts = range(count // LANES)
 
     (near,) = tables(0, (0,), coords)
+    below, above, held_mask = lax.optimization_barrier((below, above, mask))
+    masks = partner(held_mask, "space", LEVELS - 1 + block_bits)
     state = redatum(below, wavefield, above, taps, near)
     received = partner(state, "space", block_bits)
     (far,) = tables(0, (1,), coords, state)

time: 68.9 us -> 65.8 us (0.955)
  local copies, waits for them, and re-layouts: 5.51 us -> 1.61 us
  Pallas kernels: 30.9 us -> 32.4 us
  waiting for transfers between devices: 17 us -> 15.5 us
  starting transfers between devices: 14.3 us -> 15.2 us
    unnamed x14 -> x10, local copies, waits for them, and re-layouts: 4.81 us -> 0.92 us
    pallas_call x1, Pallas kernels: 0.77 us -> 2.41 us  [prepare(): pl.pallas_call(functools.partial(prepare_kernel, blocks), out_shape=(edge...]
    ppermute x7, starting transfers between devices: 10.5 us -> 11.3 us  [partner(): lax.ppermute(shard, axis, [(i, i ^ 1 << bit) for i in range(lax.axis_size...]
    ppermute x7, waiting for transfers between devices: 15.3 us -> 14.5 us  [partner(): lax.ppermute(shard, axis, [(i, i ^ 1 << bit) for i in range(lax.axis_size...]
    ppermute x2, waiting for transfers between devices: 1.76 us -> 1.06 us  [passed_along(): return lax.ppermute(shard, axis, pairs)]
  transfers between devices with their start and end apart: 9 -> 9, of which waited for: 3 -> 3; matrix products, arithmetic and copies ran while one was open for 1% -> 1% of each run, Pallas kernels for 31% -> 32%
where the time goes in v4:
time: 65.8 us; the launch traced here: 65.6 us
  Pallas kernels  32.4 us (49%)
  waiting for transfers between devices  15.5 us (24%)
  starting transfers between devices  15.2 us (23%)
  local copies, waits for them, and re-layouts  1.61 us (2%)
    pallas_call x5, Pallas kernels, tables(): pl.pallas_call(functools.partial(tables_kernel, jobs, step), out_shape=(s...  17.3 us
    ppermute x7, waiting for transfers between devices, partner(): lax.ppermute(shard, axis, [(i, i ^ 1 << bit) for i in range(lax.axis_size...  14.5 us
    ppermute x7, starting transfers between devices, partner(): lax.ppermute(shard, axis, [(i, i ^ 1 << bit) for i in range(lax.axis_size...  11.3 us
    pallas_call x1, Pallas kernels, redatum(): pl.pallas_call(functools.partial(redatum_kernel, reach), out_shape=jax.Sh...  6.85 us
    pallas_call x6, Pallas kernels, mix(): pl.pallas_call(functools.partial(mix_kernel, held), out_shape=jax.ShapeDt...  4.33 us
    ppermute x2, starting transfers between devices, passed_along(): return lax.ppermute(shard, axis, pairs)  3.82 us
    pallas_call x1, Pallas kernels, prepare(): pl.pallas_call(functools.partial(prepare_kernel, blocks), out_shape=(edge...  2.41 us
    pallas_call x2, Pallas kernels, last(): pl.pallas_call(functools.partial(last_kernel, part), out_shape=(shape, sh...  1.53 us
  transfers between devices with their start and end apart: 9, of which 3 were waited for; matrix products, arithmetic and copies ran while one was open for 1% of the time, Pallas kernels for 32%

profile of v4, /device:TPU:0, one launch (start us, length us, event | category | flops | bytes accessed | tf_op | source)
XLA Modules:
  0.0 65.6 jit_solution(8876195023999687381)
XLA Ops:
  0.0 2.4 %prepare.1 = (bf16[256,128]{1,0:T(8,128)(2,1)}, bf16[256,128]{1,0:T(8,128)(2,1)}, bf16[256,1024]{1,0:T(8,128)(2,1)}, f32[32,1024]{1,0:T(8,128)}) custom-call(bf16[256,1024]{1,0:T(8,128)(2,1)} %wave.3, s32[256,1024]{1,0:T(8,128)} %aperture.1, s32[5,16384]{1,0:T(8,128)} %cell_x.1, s32[128,128]{1,0:T(8,128)} %bitcast.5, f32[4]{0:T(128)} %slowness.1), custom_call_target="tpu_custom_call" | custom-call | flops 754974720 | bytes 2097152 | tf_op jit(solution)/shard_map/prepare/pallas_call | solution.py:115
  2.4 0.0 copy-start.1
  2.4 0.0 copy-start.2
  2.4 2.5 %collective-permute-start = (bf16[256,128]{1,0:T(8,128)(2,1)}, bf16[256,128]{1,0:T(8,128)(2,1)S(1)}, u32[]{:S(2)}, u32[]{:S(2)}) collective-permute-start(bf16[256,128]{1,0:T(8,128)(2,1)} %get-tuple-element.22), channel_id=1, source_target_pairs={{0,1},{1,2},{2,3},{3,4},{4,5},{5,6},{6,7},{7,8},{8,9},{9,10},{10,1... | collective-permute-start | bytes 196616 | tf_op jit(solution)/shard_map/ppermute | solution.py:37
  5.0 1.3 %collective-permute-start.1 = (bf16[256,128]{1,0:T(8,128)(2,1)}, bf16[256,128]{1,0:T(8,128)(2,1)S(1)}, u32[]{:S(2)}, u32[]{:S(2)}) collective-permute-start(bf16[256,128]{1,0:T(8,128)(2,1)} %get-tuple-element.23), channel_id=1, source_target_pairs={{1,0},{2,1},{3,2},{4,3},{5,4},{6,5},{7,6},{8,7},{9,8},{10,9},{11,1... | collective-permute-start | bytes 196616 | tf_op jit(solution)/shard_map/ppermute | solution.py:37
  6.3 0.9 %copy-done.3 = f32[32,1024]{1,0:T(8,128)S(1)} copy-done((f32[32,1024]{1,0:T(8,128)S(1)}, f32[32,1024]{1,0:T(8,128)}, u32[]{:S(2)}) %copy-start.3) | copy-done | bytes 131096
  7.2 2.2 %shard_map.73.refs_0_.near = bf16[1024,1024]{1,0:T(8,128)(2,1)S(1)} custom-call(f32[32,1024]{1,0:T(8,128)S(1)} %copy-done.3), custom_call_target="tpu_custom_call" | custom-call | flops 1006632960 | bytes 2097152 | tf_op jit(solution)/shard_map/pallas_call | solution.py:173
  9.4 1.1 %collective-permute-done.1.above = bf16[256,128]{1,0:T(8,128)(2,1)S(1)} collective-permute-done((bf16[256,128]{1,0:T(8,128)(2,1)}, bf16[256,128]{1,0:T(8,128)(2,1)S(1)}, u32[]{:S(2)}, u32[]{:S(2)}) %collective-permute-start.1) | collective-permute-done | bytes 65568 | tf_op jit(solution)/shard_map/ppermute | solution.py:37
  10.4 6.9 %redatum.1.refs_0_.mine = bf16[256,1024]{1,0:T(8,128)(2,1)S(1)} custom-call(bf16[256,128]{1,0:T(8,128)(2,1)S(1)} %collective-permute-done.below, bf16[256,1024]{1,0:T(8,128)(2,1)S(1)} %copy-done.1, bf16[256,128]{1,0:T(8,128)(2,1)S(1)} %collective-permute-done.1.above, f32[65,256]{1,0:T(8,128)S(1)} %bitcast.3, bf16[1024,1024]{1,0:T(8,128)(2,1)S(1)} %shard_map.73.refs_0_.near), custom_call_target="tpu_custom_call" | custom-call | flops 3019898880 | bytes 1048576 | tf_op jit(solution)/shard_map/redatum/pallas_call | solution.py:220
  17.3 3.0 %collective-permute-start.2 = (bf16[256,1024]{1,0:T(8,128)(2,1)S(1)}, bf16[256,1024]{1,0:T(8,128)(2,1)S(1)}, u32[]{:S(2)}, u32[]{:S(2)}) collective-permute-start(bf16[256,1024]{1,0:T(8,128)(2,1)S(1)} %redatum.1.refs_0_.mine), channel_id=1, source_target_pairs={{0,1},{1,0},{2,3},{3,2},{4,5},{5,4},{6,7},{7,6},{8,9},{9,8},{10,11... | collective-permute-start | bytes 1572872 | tf_op jit(solution)/shard_map/ppermute | solution.py:41
  20.3 2.2 %shard_map.74.far.refs_0_ = bf16[1024,1024]{1,0:T(8,128)(2,1)S(1)} custom-call(f32[32,1024]{1,0:T(8,128)S(1)} %copy-done.4, bf16[256,1024]{1,0:T(8,128)(2,1)S(1)} %redatum.1.refs_0_.mine), custom_call_target="tpu_custom_call" | custom-call | flops 1006632960 | bytes 2097152 | tf_op jit(solution)/shard_map/pallas_call | solution.py:173
  22.5 0.7 %mix.6.refs_0_.mine = bf16[128,1024]{1,0:T(8,128)(2,1)S(1)} custom-call(bf16[256,1024]{1,0:T(8,128)(2,1)S(1)} %redatum.1.refs_0_.mine, bf16[256,1024]{1,0:T(8,128)(2,1)S(1)} %collective-permute-done.2.theirs, bf16[1024,1024]{1,0:T(8,128)(2,1)S(1)} %shard_map.73.refs_0_.near, bf16[1024,1024]{1,0:T(8,128)(2,1)S(1)} %shard_map.74.far.refs_0_, ...), custom_call_target="tpu_custom_call" | custom-call | flops 377487360 | bytes 4194304 | tf_op jit(solution)/shard_map/mix/pallas_call | solution.py:247
  23.2 2.5 %collective-permute-start.4 = (bf16[128,1024]{1,0:T(8,128)(2,1)S(1)}, bf16[128,1024]{1,0:T(8,128)(2,1)S(1)}, u32[]{:S(2)}, u32[]{:S(2)}) collective-permute-start(bf16[128,1024]{1,0:T(8,128)(2,1)S(1)} %mix.6.refs_0_.mine), channel_id=1, source_target_pairs={{0,2},{1,3},{2,0},{3,1},{4,6},{5,7},{6,4},{7,5},{8,10},{9,11},{10,... | collective-permute-start | bytes 786440 | tf_op jit(solution)/shard_map/ppermute | solution.py:41
  25.7 2.6 %collective-permute-start.7 = (bf16[256,1024]{1,0:T(8,128)(2,1)S(1)}, bf16[256,1024]{1,0:T(8,128)(2,1)S(1)}, u32[]{:S(2)}, u32[]{:S(2)}) collective-permute-start(bf16[256,1024]{1,0:T(8,128)(2,1)S(1)} %copy-done), channel_id=1, source_target_pairs={{0,8},{1,9},{2,10},{3,11},{4,12},{5,13},{6,14},{7,15},{8,0},{9,1},... | collective-permute-start | bytes 1572872 | tf_op jit(solution)/shard_map/ppermute | solution.py:41
  28.3 0.7 %mix.7.refs_0_.mine = bf16[128,1024]{1,0:T(8,128)(2,1)S(1)} custom-call(bf16[256,1024]{1,0:T(8,128)(2,1)S(1)} %redatum.1.refs_0_.mine, bf16[256,1024]{1,0:T(8,128)(2,1)S(1)} %collective-permute-done.2.theirs, bf16[1024,1024]{1,0:T(8,128)(2,1)S(1)} %shard_map.73.refs_0_.near, bf16[1024,1024]{1,0:T(8,128)(2,1)S(1)} %shard_map.74.far.refs_0_, ...), custom_call_target="tpu_custom_call" | custom-call | flops 377487360 | bytes 4194304 | tf_op jit(solution)/shard_map/mix/pallas_call | solution.py:247
  29.1 0.3 collective-permute-start.3
  29.4 4.3 %shard_map.75 = (bf16[1024,1024]{1,0:T(8,128)(2,1)S(1)}, bf16[1024,1024]{1,0:T(8,128)(2,1)S(1)}) custom-call(f32[32,1024]{1,0:T(8,128)S(1)} %copy-done.4, bf16[128,1024]{1,0:T(8,128)(2,1)S(1)} %mix.7.refs_0_.mine), custom_call_target="tpu_custom_call" | custom-call | flops 2013265920 | bytes 4194304 | tf_op jit(solution)/shard_map/pallas_call | solution.py:173
  33.7 0.7 %mix.8.refs_0_.mine = bf16[128,1024]{1,0:T(8,128)(2,1)S(1)} custom-call(bf16[128,1024]{1,0:T(8,128)(2,1)S(1)} %mix.6.refs_0_.mine, bf16[128,1024]{1,0:T(8,128)(2,1)S(1)} %collective-permute-done.4.theirs, bf16[1024,1024]{1,0:T(8,128)(2,1)S(1)} %get-tuple-element.28.near.refs_0_, bf16[1024,1024]{1,0:T(8,128)(2,1)S(1)} %get-tuple-element.29.far, ...), custom_call_target="tpu_custom_call" | custom-call | flops 377487360 | bytes 4194304 | tf_op jit(solution)/shard_map/mix/pallas_call | solution.py:247
  34.4 1.3 %collective-permute-start.6 = (bf16[128,1024]{1,0:T(8,128)(2,1)S(1)}, bf16[128,1024]{1,0:T(8,128)(2,1)S(1)}, u32[]{:S(2)}, u32[]{:S(2)}) collective-permute-start(bf16[128,1024]{1,0:T(8,128)(2,1)S(1)} %mix.8.refs_0_.mine), channel_id=1, source_target_pairs={{0,4},{1,5},{2,6},{3,7},{4,0},{5,1},{6,2},{7,3},{8,12},{9,13},{10,... | collective-permute-start | bytes 786440 | tf_op jit(solution)/shard_map/ppermute | solution.py:41
  35.7 4.3 %shard_map.76 = (bf16[1024,1024]{1,0:T(8,128)(2,1)S(1)}, bf16[1024,1024]{1,0:T(8,128)(2,1)S(1)}) custom-call(f32[32,1024]{1,0:T(8,128)S(1)} %copy-done.4, bf16[128,1024]{1,0:T(8,128)(2,1)S(1)} %mix.8.refs_0_.mine), custom_call_target="tpu_custom_call" | custom-call | flops 2013265920 | bytes 4194304 | tf_op jit(solution)/shard_map/pallas_call | solution.py:173
  40.1 0.7 %mix.9.refs_0_.mine = bf16[128,1024]{1,0:T(8,128)(2,1)S(1)} custom-call(bf16[128,1024]{1,0:T(8,128)(2,1)S(1)} %mix.7.refs_0_.mine, bf16[128,1024]{1,0:T(8,128)(2,1)S(1)} %collective-permute-done.3.theirs, bf16[1024,1024]{1,0:T(8,128)(2,1)S(1)} %get-tuple-element.28.near.refs_0_, bf16[1024,1024]{1,0:T(8,128)(2,1)S(1)} %get-tuple-element.29.far, ...), custom_call_target="tpu_custom_call" | custom-call | flops 377487360 | bytes 4194304 | tf_op jit(solution)/shard_map/mix/pallas_call | solution.py:247
  40.8 0.9 %collective-permute-start.5 = (bf16[128,1024]{1,0:T(8,128)(2,1)S(1)}, bf16[128,1024]{1,0:T(8,128)(2,1)S(1)}, u32[]{:S(2)}, u32[]{:S(2)}) collective-permute-start(bf16[128,1024]{1,0:T(8,128)(2,1)S(1)} %mix.9.refs_0_.mine), channel_id=1, source_target_pairs={{0,4},{1,5},{2,6},{3,7},{4,0},{5,1},{6,2},{7,3},{8,12},{9,13},{10,... | collective-permute-start | bytes 786440 | tf_op jit(solution)/shard_map/ppermute | solution.py:41
  41.7 11.4 %collective-permute-done.6.theirs = bf16[128,1024]{1,0:T(8,128)(2,1)S(1)} collective-permute-done((bf16[128,1024]{1,0:T(8,128)(2,1)S(1)}, bf16[128,1024]{1,0:T(8,128)(2,1)S(1)}, u32[]{:S(2)}, u32[]{:S(2)}) %collective-permute-start.6) | collective-permute-done | bytes 262176 | tf_op jit(solution)/shard_map/ppermute | solution.py:41
  53.0 0.7 %mix.10.refs_0_.state = bf16[128,1024]{1,0:T(8,128)(2,1)S(1)} custom-call(bf16[128,1024]{1,0:T(8,128)(2,1)S(1)} %mix.8.refs_0_.mine, bf16[128,1024]{1,0:T(8,128)(2,1)S(1)} %collective-permute-done.6.theirs, bf16[1024,1024]{1,0:T(8,128)(2,1)S(1)} %get-tuple-element.30.refs_0_.near, bf16[1024,1024]{1,0:T(8,128)(2,1)S(1)} %get-tuple-element.31.far, ...), custom_call_target="tpu_custom_call" | custom-call | flops 377487360 | bytes 4194304 | tf_op jit(solution)/shard_map/mix/pallas_call | solution.py:247
  53.8 4.3 %shard_map.77 = (bf16[1024,1024]{1,0:T(8,128)(2,1)S(1)}, bf16[1024,1024]{1,0:T(8,128)(2,1)S(1)}) custom-call(f32[32,1024]{1,0:T(8,128)S(1)} %copy-done.4, bf16[128,1024]{1,0:T(8,128)(2,1)S(1)} %mix.10.refs_0_.state), custom_call_target="tpu_custom_call" | custom-call | flops 2013265920 | bytes 4194304 | tf_op jit(solution)/shard_map/pallas_call | solution.py:173
  58.1 0.7 %mix.11.state = bf16[128,1024]{1,0:T(8,128)(2,1)S(1)} custom-call(bf16[128,1024]{1,0:T(8,128)(2,1)S(1)} %mix.9.refs_0_.mine, bf16[128,1024]{1,0:T(8,128)(2,1)S(1)} %collective-permute-done.5.theirs, bf16[1024,1024]{1,0:T(8,128)(2,1)S(1)} %get-tuple-element.30.refs_0_.near, bf16[1024,1024]{1,0:T(8,128)(2,1)S(1)} %get-tuple-element.31.far, ...), custom_call_target="tpu_custom_call" | custom-call | flops 377487360 | bytes 4194304 | tf_op jit(solution)/shard_map/mix/pallas_call | solution.py:247
  58.8 0.8 %shard_map.78 = (f32[1,1024]{1,0:T(1,128)S(1)}, f32[1,1024]{1,0:T(1,128)S(1)}) custom-call(bf16[128,1024]{1,0:T(8,128)(2,1)S(1)} %mix.10.refs_0_.state, bf16[1024,1024]{1,0:T(8,128)(2,1)S(1)} %get-tuple-element.32.refs_0_.near, bf16[1024,1024]{1,0:T(8,128)(2,1)S(1)} %get-tuple-element.33.far, bf16[256,1024]{1,0:T(8,128)(2,1)S(1)} %copy-done, ...), custom_call_target="tpu_custom_call" | custom-call | flops 536870912 | bytes 4194304 | tf_op jit(solution)/shard_map/pallas_call | solution.py:278
  59.6 0.8 %shard_map.79 = (f32[1,1024]{1,0:T(1,128)S(1)}, f32[1,1024]{1,0:T(1,128)S(1)}) custom-call(bf16[128,1024]{1,0:T(8,128)(2,1)S(1)} %mix.11.state, bf16[1024,1024]{1,0:T(8,128)(2,1)S(1)} %get-tuple-element.32.refs_0_.near, bf16[1024,1024]{1,0:T(8,128)(2,1)S(1)} %get-tuple-element.33.far, bf16[256,1024]{1,0:T(8,128)(2,1)S(1)} %copy-done, ...), custom_call_target="tpu_custom_call" | custom-call | flops 536870912 | bytes 4194304 | tf_op jit(solution)/shard_map/pallas_call | solution.py:278
  60.4 0.8 %collective-permute-start.8 = (f32[1,1024]{1,0:T(1,128)S(1)}, f32[1,1024]{1,0:T(1,128)S(1)}, u32[]{:S(2)}, u32[]{:S(2)}) collective-permute-start(f32[1,1024]{1,0:T(1,128)S(1)} %get-tuple-element.38), channel_id=1, source_target_pairs={{0,8},{1,9},{2,10},{3,11},{4,12},{5,13},{6,14},{7,15},{8,0},{9,1},... | collective-permute-start | bytes 12296 | tf_op jit(solution)/shard_map/ppermute | solution.py:41
  61.2 0.7 %dynamic_slice.4 = f32[1024]{0:T(1024)S(1)} dynamic-slice(f32[16384]{0:T(1024)} %param.12, s32[]{:T(128)S(6)} %select_n.11), dynamic_slice_sizes={1024} | dynamic-slice | bytes 8196 | tf_op jit(solution)/shard_map/dynamic_slice | solution.py:329
  61.8 3.1 %collective-permute-done.8 = f32[1,1024]{1,0:T(1,128)S(1)} collective-permute-done((f32[1,1024]{1,0:T(1,128)S(1)}, f32[1,1024]{1,0:T(1,128)S(1)}, u32[]{:S(2)}, u32[]{:S(2)}) %collective-permute-start.8) | collective-permute-done | bytes 4128 | tf_op jit(solution)/shard_map/ppermute | solution.py:41
  65.0 0.6 multiply_multiply_fusion
  (13 shorter events, 0.0 us)
Async XLA Ops:
  2.4 8.0 %copy-start.1 = (bf16[256,1024]{1,0:T(8,128)(2,1)S(1)}, bf16[256,1024]{1,0:T(8,128)(2,1)}, u32[]{:S(2)}) copy-start(bf16[256,1024]{1,0:T(8,128)(2,1)} %wave.3) | copy-start | bytes 1572868
  2.4 8.0 %copy-start.2 = (f32[256,65]{0,1:T(8,128)S(1)}, f32[256,65]{0,1:T(8,128)}, u32[]{:S(2)}) copy-start(f32[256,65]{0,1:T(8,128)} %param.8) | copy-start | bytes 199684
  2.4 6.9 %collective-permute-start = (bf16[256,128]{1,0:T(8,128)(2,1)}, bf16[256,128]{1,0:T(8,128)(2,1)S(1)}, u32[]{:S(2)}, u32[]{:S(2)}) collective-permute-start(bf16[256,128]{1,0:T(8,128)(2,1)} %get-tuple-element.22), channel_id=1, source_target_pairs={{0,1},{1,2},{2,3},{3,4},{4,5},{5,6},{6,7},{7,8},{8,9},{9,10},{10,1... | collective-permute-start | bytes 196616 | tf_op jit(solution)/shard_map/ppermute | solution.py:37
  5.0 5.5 %collective-permute-start.1 = (bf16[256,128]{1,0:T(8,128)(2,1)}, bf16[256,128]{1,0:T(8,128)(2,1)S(1)}, u32[]{:S(2)}, u32[]{:S(2)}) collective-permute-start(bf16[256,128]{1,0:T(8,128)(2,1)} %get-tuple-element.23), channel_id=1, source_target_pairs={{1,0},{2,1},{3,2},{4,3},{5,4},{6,5},{7,6},{8,7},{9,8},{10,9},{11,1... | collective-permute-start | bytes 196616 | tf_op jit(solution)/shard_map/ppermute | solution.py:37
  6.3 0.9 %copy-start.3 = (f32[32,1024]{1,0:T(8,128)S(1)}, f32[32,1024]{1,0:T(8,128)}, u32[]{:S(2)}) copy-start(f32[32,1024]{1,0:T(8,128)} %get-tuple-element.27.coords) | copy-start | bytes 393220
  10.4 9.9 %copy-start.4 = (f32[32,1024]{1,0:T(8,128)S(1)}, f32[32,1024]{1,0:T(8,128)}, u32[]{:S(2)}) copy-start(f32[32,1024]{1,0:T(8,128)} %get-tuple-element.27.coords) | copy-start | bytes 393220
  17.3 5.2 %collective-permute-start.2 = (bf16[256,1024]{1,0:T(8,128)(2,1)S(1)}, bf16[256,1024]{1,0:T(8,128)(2,1)S(1)}, u32[]{:S(2)}, u32[]{:S(2)}) collective-permute-start(bf16[256,1024]{1,0:T(8,128)(2,1)S(1)} %redatum.1.refs_0_.mine), channel_id=1, source_target_pairs={{0,1},{1,0},{2,3},{3,2},{4,5},{5,4},{6,7},{7,6},{8,9},{9,8},{10,11... | collective-permute-start | bytes 1572872 | tf_op jit(solution)/shard_map/ppermute | solution.py:41
  22.5 3.3 %copy-start = (bf16[256,1024]{1,0:T(8,128)(2,1)S(1)}, bf16[256,1024]{1,0:T(8,128)(2,1)}, u32[]{:S(2)}) copy-start(bf16[256,1024]{1,0:T(8,128)(2,1)} %get-tuple-element.34.own_mask) | copy-start | bytes 1572868
  23.2 10.5 %collective-permute-start.4 = (bf16[128,1024]{1,0:T(8,128)(2,1)S(1)}, bf16[128,1024]{1,0:T(8,128)(2,1)S(1)}, u32[]{:S(2)}, u32[]{:S(2)}) collective-permute-start(bf16[128,1024]{1,0:T(8,128)(2,1)S(1)} %mix.6.refs_0_.mine), channel_id=1, source_target_pairs={{0,2},{1,3},{2,0},{3,1},{4,6},{5,7},{6,4},{7,5},{8,10},{9,11},{10,... | collective-permute-start | bytes 786440 | tf_op jit(solution)/shard_map/ppermute | solution.py:41
  25.7 33.1 %collective-permute-start.7 = (bf16[256,1024]{1,0:T(8,128)(2,1)S(1)}, bf16[256,1024]{1,0:T(8,128)(2,1)S(1)}, u32[]{:S(2)}, u32[]{:S(2)}) collective-permute-start(bf16[256,1024]{1,0:T(8,128)(2,1)S(1)} %copy-done), channel_id=1, source_target_pairs={{0,8},{1,9},{2,10},{3,11},{4,12},{5,13},{6,14},{7,15},{8,0},{9,1},... | collective-permute-start | bytes 1572872 | tf_op jit(solution)/shard_map/ppermute | solution.py:41
  29.1 11.0 %collective-permute-start.3 = (bf16[128,1024]{1,0:T(8,128)(2,1)S(1)}, bf16[128,1024]{1,0:T(8,128)(2,1)S(1)}, u32[]{:S(2)}, u32[]{:S(2)}) collective-permute-start(bf16[128,1024]{1,0:T(8,128)(2,1)S(1)} %mix.7.refs_0_.mine), channel_id=1, source_target_pairs={{0,2},{1,3},{2,0},{3,1},{4,6},{5,7},{6,4},{7,5},{8,10},{9,11},{10,... | collective-permute-start | bytes 786440 | tf_op jit(solution)/shard_map/ppermute | solution.py:41
  34.4 18.6 %collective-permute-start.6 = (bf16[128,1024]{1,0:T(8,128)(2,1)S(1)}, bf16[128,1024]{1,0:T(8,128)(2,1)S(1)}, u32[]{:S(2)}, u32[]{:S(2)}) collective-permute-start(bf16[128,1024]{1,0:T(8,128)(2,1)S(1)} %mix.8.refs_0_.mine), channel_id=1, source_target_pairs={{0,4},{1,5},{2,6},{3,7},{4,0},{5,1},{6,2},{7,3},{8,12},{9,13},{10,... | collective-permute-start | bytes 786440 | tf_op jit(solution)/shard_map/ppermute | solution.py:41
  40.8 17.3 %collective-permute-start.5 = (bf16[128,1024]{1,0:T(8,128)(2,1)S(1)}, bf16[128,1024]{1,0:T(8,128)(2,1)S(1)}, u32[]{:S(2)}, u32[]{:S(2)}) collective-permute-start(bf16[128,1024]{1,0:T(8,128)(2,1)S(1)} %mix.9.refs_0_.mine), channel_id=1, source_target_pairs={{0,4},{1,5},{2,6},{3,7},{4,0},{5,1},{6,2},{7,3},{8,12},{9,13},{10,... | collective-permute-start | bytes 786440 | tf_op jit(solution)/shard_map/ppermute | solution.py:41
  60.4 4.6 %collective-permute-start.8 = (f32[1,1024]{1,0:T(1,128)S(1)}, f32[1,1024]{1,0:T(1,128)S(1)}, u32[]{:S(2)}, u32[]{:S(2)}) collective-permute-start(f32[1,1024]{1,0:T(1,128)S(1)} %get-tuple-element.38), channel_id=1, source_target_pairs={{0,8},{1,9},{2,10},{3,11},{4,12},{5,13},{6,14},{7,15},{8,0},{9,1},... | collective-permute-start | bytes 12296 | tf_op jit(solution)/shard_map/ppermute | solution.py:41

commit v5 on v4

--- a/solution.py
+++ b/solution.py
@@ -31,9 +31,10 @@
     return pl.CostEstimate(flops=flops, bytes_accessed=moved, transcendentals=transcendentals)
 
 
-def passed_along(shard, axis, by):
+def across(shard, axis, blocks):
     devices = lax.axis_size(axis)
-    pairs = [(i, i + by) for i in range(devices) if 0 <= i + by < devices]
+    shift = [blocks if i // blocks % 2 else -blocks for i in range(devices)]
+    pairs = [(i, i + by) for i, by in enumerate(shift) if 0 <= i + by < devices]
     return lax.ppermute(shard, axis, pairs)
 
 
@@ -60,7 +61,7 @@
 
 
 def prepare_kernel(blocks, wave, aperture, cell_x, depth, slowness, *refs):
-    head, tail, mask, coords, cells, depths, slow, marks, sems = refs
+    near_edge, far_edge, mask, coords, cells, depths, slow, marks, sems = refs
     width = wave.shape[1]
     tall = width // LANES
     box = boxes_of(0, blocks)[0]
@@ -72,9 +73,13 @@
     for k, which in enumerate((box, others[-1])):
         at = pl.ds(pl.multiple_of(which * tall, tall), tall)
         copies.append(pltpu.make_async_copy(depth.at[at, :], depths.at[k], sems.at[6 + k]))
+    end = width - LANES
+    even = 1 - box % 2
+    first = pl.ds(pl.multiple_of(even * end, LANES), LANES)
+    second = pl.ds(pl.multiple_of((1 - even) * end, LANES), LANES)
     late = [
-        pltpu.make_async_copy(wave.at[:, pl.ds(0, LANES)], head, sems.at[8]),
-        pltpu.make_async_copy(wave.at[:, pl.ds(width - LANES, LANES)], tail, sems.at[9]),
+        pltpu.make_async_copy(wave.at[:, first], near_edge, sems.at[8]),
+        pltpu.make_async_copy(wave.at[:, second], far_edge, sems.at[9]),
         pltpu.make_async_copy(aperture, marks, sems.at[10]),
     ]
     for copy in copies + late:
@@ -181,26 +186,21 @@
     )(coords, *after)
 
 
-def redatum_kernel(reach, below, wave, above, taps, *refs):
+def redatum_kernel(reach, blocks, near_edge, wave, far_edge, taps, *refs):
     out, padded = refs[-2:]
     count, width = wave.shape
-    edge = below.shape[1]
-    blocks = width // LANES
-    halves = range(count // LANES)
-
-    def fill(lane, source, x, start):
+    edge = near_edge.shape[1]
+    even = 1 - boxes_of(0, blocks)[0] % 2
+    after = edge + width
+    starts = (pl.multiple_of(even * after, LANES), pl.multiple_of((1 - even) * after, LANES))
+    for lane in range(count // LANES):
         held = slice(lane * LANES, (lane + 1) * LANES)
-        block = source[held, pl.ds(x, LANES)].astype(jnp.float32)
-        padded[lane, pl.ds(start, LANES), :] = block.T
-
-    for lane in halves:
-        held = slice(lane * LANES, (lane + 1) * LANES)
-        fill(lane, below, 0, 0)
-        fill(lane, above, 0, edge + width)
-        for k in range(min(2, blocks)):
-            fill(lane, wave, k * LANES, edge + k * LANES)
-
-        @pl.loop(0, blocks)
+        for source, start in ((near_edge, starts[0]), (far_edge, starts[1]), (wave, edge)):
+            for x in range(0, source.shape[1], LANES):
+                block = source[held, x : x + LANES].astype(jnp.float32)
+                padded[lane, pl.ds(start + x, LANES), :] = block.T
+
+        @pl.loop(0, width // LANES)
         def _(block):
             base = pl.multiple_of(block * LANES, LANES)
             total = None
@@ -209,16 +209,14 @@
                 term = weight * padded[lane, pl.ds(base + edge - reach + j, LANES), :]
                 total = term if total is None else total + term
             out[held, pl.ds(base, LANES)] = total.T.astype(out.dtype)
-            ahead = pl.multiple_of(jnp.minimum(block + 2, blocks - 1) * LANES, LANES)
-            fill(lane, wave, ahead, edge + ahead)
-
-
-def redatum(below, wave, above, taps, *after):
+
+
+def redatum(blocks, near_edge, wave, far_edge, taps, *after):
     count, width = wave.shape
     reach = (taps.shape[0] - 1) // 2
-    long = width + 2 * below.shape[1]
-    return pl.pallas_call(
-        functools.partial(redatum_kernel, reach),
+    long = width + 2 * near_edge.shape[1]
+    return pl.pallas_call(
+        functools.partial(redatum_kernel, reach, blocks),
         out_shape=jax.ShapeDtypeStruct((count, width), jnp.bfloat16),
         in_specs=[VMEM] * 4 + [ANY] * len(after),
         out_specs=VMEM,
@@ -226,7 +224,7 @@
         compiler_params=params(6),
         cost_estimate=cost(24 * 2 * width * width * 60, count * width * 4),
         name="redatum",
-    )(below, wave, above, taps, *after)
+    )(near_edge, wave, far_edge, taps, *after)
 
 
 def mix_kernel(held, mine, theirs, near, far, *refs):
@@ -255,34 +253,35 @@
     )(mine, theirs, near, far, *after)
 
 
-def last_kernel(part, state, near, far, own_mask, far_mask, *refs):
-    own, other = refs[-2:]
-    width = near.shape[1]
+def last_kernel(part, count, added, state, *refs):
+    tables, masks, sums = refs[:count], refs[count : 2 * count], refs[2 * count : 2 * count + added]
+    width = tables[0].shape[1]
     scale = SCALE / math.sqrt(width)
     step = min(width, 256)
     held = slice(part * LANES, (part + 1) * LANES)
-    for k, (table, mask, out) in enumerate(((far, far_mask, other), (near, own_mask, own))):
+    for k, out in enumerate(refs[-count:]):
         for c in range(0, width, step):
             columns = slice(c, c + step)
-            mixed = jnp.dot(state[...], table[:, columns], preferred_element_type=jnp.float32)
-            kept = jnp.where(mask[held, columns].astype(jnp.float32) > 0, mixed, 0.0)
+            mixed = jnp.dot(state[...], tables[k][:, columns], preferred_element_type=jnp.float32)
+            kept = jnp.where(masks[k][held, columns].astype(jnp.float32) > 0, mixed, 0.0)
             total = jnp.sum(kept, 0, keepdims=True) * scale
-            if part > 0:
-                total = total + refs[1 - k][:, columns]
+            if added:
+                total = total + sums[k][:, columns]
             out[:, columns] = total
 
 
-def last(part, state, near, far, own_mask, far_mask, sums, *after):
-    count, width = state.shape
+def last(part, state, tables, masks, sums, *after):
+    width = state.shape[1]
+    count = len(tables)
     shape = jax.ShapeDtypeStruct((1, width), jnp.float32)
     return pl.pallas_call(
-        functools.partial(last_kernel, part),
-        out_shape=(shape, shape),
-        in_specs=[VMEM] * (5 + len(sums)) + [ANY] * len(after),
-        out_specs=(VMEM, VMEM),
-        compiler_params=params(8),
-        cost_estimate=cost(4 * count * width * width, 4 * width * width),
-    )(state, near, far, own_mask, far_mask, *sums, *after)
+        functools.partial(last_kernel, part, count, len(sums)),
+        out_shape=(shape,) * count,
+        in_specs=[VMEM] * (1 + 2 * count + len(sums)) + [ANY] * len(after),
+        out_specs=(VMEM,) * count,
+        compiler_params=params(7),
+        cost_estimate=cost(24 * count * width * width * 8, 2 * count * width * width),
+    )(state, *tables, *masks, *sums, *after)
 
 
 def on_device(wavefield, redatum_taps, cell_x, cell_depth, slowness, illumination, aperture):
@@ -293,9 +292,11 @@
     block = index % blocks
     count, width = wavefield.shape
     depth = cell_depth.reshape(BOXES * width // LANES, LANES)
-    head, tail, mask, coords = prepare(blocks, wavefield, aperture, cell_x, depth, slowness)
-    below = passed_along(tail, "space", blocks)
-    above = passed_along(head, "space", -blocks)
+    near_edge, far_edge, mask, coords = prepare(
+        blocks, wavefield, aperture, cell_x, depth, slowness
+    )
+    near_edge = partner(near_edge, "space", block_bits)
+    far_edge = across(far_edge, "space", blocks)
     taps = redatum_taps
     if blocks > 1:
         taps = lax.dynamic_slice_in_dim(redatum_taps, block * count, count, 0)
@@ -303,28 +304,34 @@
     parts = range(count // LANES)
 
     (near,) = tables(0, (0,), coords)
-    below, above, held_mask = lax.optimization_barrier((below, above, mask))
+    near_edge, far_edge, held_mask = lax.optimization_barrier((near_edge, far_edge, mask))
     masks = partner(held_mask, "space", LEVELS - 1 + block_bits)
-    state = redatum(below, wavefield, above, taps, near)
+    state = redatum(blocks, near_edge, wavefield, far_edge, taps, near)
     received = partner(state, "space", block_bits)
     (far,) = tables(0, (1,), coords, state)
     states = [state for _ in parts]
     theirs = [received for _ in parts]
     table, ahead = (near, far), far
+    both, sums = (mask, masks), ()
     for level in range(LEVELS - 1):
         for part in parts:
             states[part] = mix(part, states[part], theirs[part], *table, ahead)
             ahead = states[part]
+            if level + 2 == LEVELS and part + 1 < len(parts):
+                sums = last(part, states[part], later, both, sums)
+                ahead = sums[0]
+            if level + 2 == LEVELS and part + 1 == len(parts):
+                (other,) = last(part, states[part], later[1:], both[1:], sums[1:])
+                (own,) = last(part, states[part], later[:1], both[:1], sums[:1], other)
             if level + 2 < LEVELS:
                 theirs[part] = partner(states[part], "space", level + 1 + block_bits)
-            if part == (len(parts) - 1 if level == 0 else 0):
+            if part == (0 if level == 1 else len(parts) - 1) and level < 2:
                 following = tables(level + 1, (0, 1), coords, ahead)
                 ahead = following[0]
+            if part == len(parts) - 1 and level == 1:
+                later = tables(level + 2, (0, 1), coords, ahead)
+                ahead = later[0]
         table = following
-    sums = ()
-    for part in parts:
-        sums = last(part, states[part], *table, mask, masks, sums)
-    own, other = sums
     summed = own + partner(other, "space", LEVELS - 1 + block_bits)
     weights = lax.dynamic_slice_in_dim(illumination, box * width, width)
     image = summed * weights[None] / jnp.sqrt(jnp.float32(count * blocks))

time: 65.8 us -> 64.4 us (0.979)
  starting transfers between devices: 15.2 us -> 12.5 us
  local copies, waits for them, and re-layouts: 1.61 us -> 3.62 us
  waiting for transfers between devices: 15.5 us -> 14.4 us
    ppermute x2 -> x1, starting transfers between devices: 3.82 us -> 0.65 us  [across(): return lax.ppermute(shard, axis, pairs)]
    unnamed x10 -> x18, local copies, waits for them, and re-layouts: 0.92 us -> 3.61 us
    ppermute x2 -> x1, waiting for transfers between devices: 1.06 us -> 0.01 us  [across(): return lax.ppermute(shard, axis, pairs)]
    pallas_call x6, Pallas kernels: 4.33 us -> 5.3 us  [mix(): pl.pallas_call(functools.partial(mix_kernel, held), out_shape=jax.ShapeDt...]
    pallas_call x3 -> x4, Pallas kernels: 8.38 us -> 7.68 us  [the longest x1 5.95 us: redatum(): pl.pallas_call(functools.partial(redatum_kernel, reach, blocks), out_shap...]
    dynamic_slice x1 -> x2, local copies, waits for them, and re-layouts: 0.69 us -> 0.01 us  [on_device(): weights = lax.dynamic_slice_in_dim(illumination, box * width, width)]
    ppermute x7 -> x8, starting transfers between devices: 11.3 us -> 11.9 us  [partner(): lax.ppermute(shard, axis, [(i, i ^ 1 << bit) for i in range(lax.axis_size...]
    ppermute x7 -> x8, waiting for transfers between devices: 14.5 us -> 14.4 us  [partner(): lax.ppermute(shard, axis, [(i, i ^ 1 << bit) for i in range(lax.axis_size...]
  transfers between devices with their start and end apart: 9 -> 9, of which waited for: 3 -> 3; matrix products, arithmetic and copies ran while one was open for 1% -> 0% of each run, Pallas kernels for 32% -> 35%
where the time goes in v5:
time: 64.4 us; the launch traced here: 64.1 us
  Pallas kernels  32.7 us (51%)
  waiting for transfers between devices  14.4 us (22%)
  starting transfers between devices  12.5 us (19%)
  local copies, waits for them, and re-layouts  3.62 us (6%)
    pallas_call x5, Pallas kernels, tables(): pl.pallas_call(functools.partial(tables_kernel, jobs, step), out_shape=(s...  17.3 us
    ppermute x8, waiting for transfers between devices, partner(): lax.ppermute(shard, axis, [(i, i ^ 1 << bit) for i in range(lax.axis_size...  14.4 us
    ppermute x8, starting transfers between devices, partner(): lax.ppermute(shard, axis, [(i, i ^ 1 << bit) for i in range(lax.axis_size...  11.9 us
    pallas_call x1, Pallas kernels, redatum(): pl.pallas_call(functools.partial(redatum_kernel, reach, blocks), out_shap...  5.95 us
    pallas_call x6, Pallas kernels, mix(): pl.pallas_call(functools.partial(mix_kernel, held), out_shape=jax.ShapeDt...  5.3 us
    unnamed x18, local copies, waits for them, and re-layouts  3.61 us
    pallas_call x1, Pallas kernels, prepare(): pl.pallas_call(functools.partial(prepare_kernel, blocks), out_shape=(edge...  2.41 us
    pallas_call x3, Pallas kernels, last(): pl.pallas_call(functools.partial(last_kernel, part, count, len(sums)), ou...  1.72 us
  transfers between devices with their start and end apart: 9, of which 3 were waited for; matrix products, arithmetic and copies ran while one was open for 0% of the time, Pallas kernels for 35%

profile of v5, /device:TPU:0, one launch (start us, length us, event | category | flops | bytes accessed | tf_op | source)
XLA Modules:
  0.0 64.1 jit_solution(3977129868059767871)
XLA Ops:
  0.0 2.4 %prepare.1 = (bf16[256,128]{1,0:T(8,128)(2,1)}, bf16[256,128]{1,0:T(8,128)(2,1)}, bf16[256,1024]{1,0:T(8,128)(2,1)}, f32[32,1024]{1,0:T(8,128)}) custom-call(bf16[256,1024]{1,0:T(8,128)(2,1)} %wave.3, s32[256,1024]{1,0:T(8,128)} %aperture.1, s32[5,16384]{1,0:T(8,128)} %cell_x.1, s32[128,128]{1,0:T(8,128)} %bitcast.5, f32[4]{0:T(128)} %slowness.1), custom_call_target="tpu_custom_call" | custom-call | flops 754974720 | bytes 2097152 | tf_op jit(solution)/shard_map/prepare/pallas_call | solution.py:120
  2.4 0.6 collective-permute-start
  3.0 0.7 %collective-permute-start.1 = (bf16[256,128]{1,0:T(8,128)(2,1)}, bf16[256,128]{1,0:T(8,128)(2,1)S(1)}, u32[]{:S(2)}, u32[]{:S(2)}) collective-permute-start(bf16[256,128]{1,0:T(8,128)(2,1)} %get-tuple-element.21), channel_id=1, source_target_pairs={{1,2},{2,1},{3,4},{4,3},{5,6},{6,5},{7,8},{8,7},{9,10},{10,9},{11,... | collective-permute-start | bytes 196616 | tf_op jit(solution)/shard_map/ppermute | solution.py:38
  3.7 0.9 %copy-done.7 = f32[32,1024]{1,0:T(8,128)S(1)} copy-done((f32[32,1024]{1,0:T(8,128)S(1)}, f32[32,1024]{1,0:T(8,128)}, u32[]{:S(2)}) %copy-start.7) | copy-done | bytes 131096
  4.6 2.2 %shard_map.73.refs_0_.near = bf16[1024,1024]{1,0:T(8,128)(2,1)S(1)} custom-call(f32[32,1024]{1,0:T(8,128)S(1)} %copy-done.7), custom_call_target="tpu_custom_call" | custom-call | flops 1006632960 | bytes 2097152 | tf_op jit(solution)/shard_map/pallas_call | solution.py:178
  6.8 6.0 %redatum.1.refs_0_.mine = bf16[256,1024]{1,0:T(8,128)(2,1)S(1)} custom-call(bf16[256,128]{1,0:T(8,128)(2,1)S(1)} %collective-permute-done.near_edge, bf16[256,1024]{1,0:T(8,128)(2,1)S(1)} %copy-done.5, bf16[256,128]{1,0:T(8,128)(2,1)S(1)} %collective-permute-done.1.far_edge, f32[65,256]{1,0:T(8,128)S(1)} %bitcast.3, ...), custom_call_target="tpu_custom_call" | custom-call | flops 3019898880 | bytes 1048576 | tf_op jit(solution)/shard_map/redatum/pallas_call | solution.py:218
  12.8 4.1 %collective-permute-start.2 = (bf16[256,1024]{1,0:T(8,128)(2,1)S(1)}, bf16[256,1024]{1,0:T(8,128)(2,1)S(1)}, u32[]{:S(2)}, u32[]{:S(2)}) collective-permute-start(bf16[256,1024]{1,0:T(8,128)(2,1)S(1)} %redatum.1.refs_0_.mine), channel_id=1, source_target_pairs={{0,1},{1,0},{2,3},{3,2},{4,5},{5,4},{6,7},{7,6},{8,9},{9,8},{10,11... | collective-permute-start | bytes 1572872 | tf_op jit(solution)/shard_map/ppermute | solution.py:42
  16.8 2.2 %shard_map.74.far.refs_0_ = bf16[1024,1024]{1,0:T(8,128)(2,1)S(1)} custom-call(f32[32,1024]{1,0:T(8,128)S(1)} %copy-done.7, bf16[256,1024]{1,0:T(8,128)(2,1)S(1)} %redatum.1.refs_0_.mine), custom_call_target="tpu_custom_call" | custom-call | flops 1006632960 | bytes 2097152 | tf_op jit(solution)/shard_map/pallas_call | solution.py:178
  19.0 0.7 %mix.6.refs_0_.mine = bf16[128,1024]{1,0:T(8,128)(2,1)S(1)} custom-call(bf16[256,1024]{1,0:T(8,128)(2,1)S(1)} %redatum.1.refs_0_.mine, bf16[256,1024]{1,0:T(8,128)(2,1)S(1)} %collective-permute-done.2.theirs, bf16[1024,1024]{1,0:T(8,128)(2,1)S(1)} %shard_map.73.refs_0_.near, bf16[1024,1024]{1,0:T(8,128)(2,1)S(1)} %shard_map.74.far.refs_0_, ...), custom_call_target="tpu_custom_call" | custom-call | flops 377487360 | bytes 4194304 | tf_op jit(solution)/shard_map/mix/pallas_call | solution.py:245
  19.8 1.9 %collective-permute-start.4 = (bf16[128,1024]{1,0:T(8,128)(2,1)S(1)}, bf16[128,1024]{1,0:T(8,128)(2,1)}, u32[]{:S(2)}, u32[]{:S(2)}) collective-permute-start(bf16[128,1024]{1,0:T(8,128)(2,1)S(1)} %mix.6.refs_0_.mine), channel_id=1, source_target_pairs={{0,2},{1,3},{2,0},{3,1},{4,6},{5,7},{6,4},{7,5},{8,10},{9,11},{10,... | collective-permute-start | bytes 786440 | tf_op jit(solution)/shard_map/ppermute | solution.py:42
  21.7 2.6 %collective-permute-start.7 = (bf16[256,1024]{1,0:T(8,128)(2,1)S(1)}, bf16[256,1024]{1,0:T(8,128)(2,1)S(1)}, u32[]{:S(2)}, u32[]{:S(2)}) collective-permute-start(bf16[256,1024]{1,0:T(8,128)(2,1)S(1)} %copy-done.2), channel_id=1, source_target_pairs={{0,8},{1,9},{2,10},{3,11},{4,12},{5,13},{6,14},{7,15},{8,0},{9,1},... | collective-permute-start | bytes 1572872 | tf_op jit(solution)/shard_map/ppermute | solution.py:42
  24.3 1.6 %copy-done.1 = bf16[1024,1024]{1,0:T(8,128)(2,1)S(1)} copy-done((bf16[1024,1024]{1,0:T(8,128)(2,1)S(1)}, bf16[1024,1024]{1,0:T(8,128)(2,1)}, u32[]{:S(2)}) %copy-start.1) | copy-done | bytes 2097176
  25.9 1.0 %copy-done.4 = bf16[256,1024]{1,0:T(8,128)(2,1)S(1)} copy-done((bf16[256,1024]{1,0:T(8,128)(2,1)S(1)}, bf16[256,1024]{1,0:T(8,128)(2,1)}, u32[]{:S(2)}) %copy-start.4) | copy-done | bytes 524312
  26.9 0.7 %mix.7.refs_0_.mine = bf16[128,1024]{1,0:T(8,128)(2,1)S(1)} custom-call(bf16[256,1024]{1,0:T(8,128)(2,1)S(1)} %redatum.1.refs_0_.mine, bf16[256,1024]{1,0:T(8,128)(2,1)S(1)} %copy-done.4, bf16[1024,1024]{1,0:T(8,128)(2,1)S(1)} %copy-done.1, bf16[1024,1024]{1,0:T(8,128)(2,1)S(1)} %shard_map.74.far.refs_0_, bf16[128,1024]{1,0:T(8,128)(2,1)S(1)} %mix.6.refs_0_.mine), custom_call_target="tpu_custom_call" | custom-call | flops 377487360 | bytes 4194304 | tf_op jit(solution)/shard_map/mix/pallas_call | solution.py:245
  27.7 0.4 collective-permute-start.3
  28.1 4.3 %shard_map.75 = (bf16[1024,1024]{1,0:T(8,128)(2,1)S(1)}, bf16[1024,1024]{1,0:T(8,128)(2,1)S(1)}) custom-call(f32[32,1024]{1,0:T(8,128)S(1)} %copy-done.8, bf16[128,1024]{1,0:T(8,128)(2,1)S(1)} %mix.7.refs_0_.mine), custom_call_target="tpu_custom_call" | custom-call | flops 2013265920 | bytes 4194304 | tf_op jit(solution)/shard_map/pallas_call | solution.py:178
  32.5 1.7 %mix.8.refs_0_.mine = bf16[128,1024]{1,0:T(8,128)(2,1)S(1)} custom-call(bf16[128,1024]{1,0:T(8,128)(2,1)S(1)} %mix.6.refs_0_.mine, bf16[128,1024]{1,0:T(8,128)(2,1)} %collective-permute-done.4.theirs, bf16[1024,1024]{1,0:T(8,128)(2,1)S(1)} %get-tuple-element.26.near.refs_0_, bf16[1024,1024]{1,0:T(8,128)(2,1)S(1)} %get-tuple-element.27.far, ...), custom_call_target="tpu_custom_call" | custom-call | flops 377487360 | bytes 4194304 | tf_op jit(solution)/shard_map/mix/pallas_call | solution.py:245
  34.2 1.6 %collective-permute-start.6 = (bf16[128,1024]{1,0:T(8,128)(2,1)S(1)}, bf16[128,1024]{1,0:T(8,128)(2,1)S(1)}, u32[]{:S(2)}, u32[]{:S(2)}) collective-permute-start(bf16[128,1024]{1,0:T(8,128)(2,1)S(1)} %mix.8.refs_0_.mine), channel_id=1, source_target_pairs={{0,4},{1,5},{2,6},{3,7},{4,0},{5,1},{6,2},{7,3},{8,12},{9,13},{10,... | collective-permute-start | bytes 786440 | tf_op jit(solution)/shard_map/ppermute | solution.py:42
  35.7 4.3 %shard_map.76 = (bf16[1024,1024]{1,0:T(8,128)(2,1)S(1)}, bf16[1024,1024]{1,0:T(8,128)(2,1)S(1)}) custom-call(f32[32,1024]{1,0:T(8,128)S(1)} %copy-done.8, bf16[128,1024]{1,0:T(8,128)(2,1)S(1)} %mix.8.refs_0_.mine), custom_call_target="tpu_custom_call" | custom-call | flops 2013265920 | bytes 4194304 | tf_op jit(solution)/shard_map/pallas_call | solution.py:178
  40.1 0.7 %mix.9.refs_0_.mine = bf16[128,1024]{1,0:T(8,128)(2,1)S(1)} custom-call(bf16[128,1024]{1,0:T(8,128)(2,1)S(1)} %mix.7.refs_0_.mine, bf16[128,1024]{1,0:T(8,128)(2,1)S(1)} %collective-permute-done.3.theirs, bf16[1024,1024]{1,0:T(8,128)(2,1)S(1)} %get-tuple-element.26.near.refs_0_, bf16[1024,1024]{1,0:T(8,128)(2,1)S(1)} %get-tuple-element.27.far, ...), custom_call_target="tpu_custom_call" | custom-call | flops 377487360 | bytes 4194304 | tf_op jit(solution)/shard_map/mix/pallas_call | solution.py:245
  40.8 0.6 collective-permute-start.5
  41.4 4.3 %shard_map.77 = (bf16[1024,1024]{1,0:T(8,128)(2,1)S(1)}, bf16[1024,1024]{1,0:T(8,128)(2,1)S(1)}) custom-call(f32[32,1024]{1,0:T(8,128)S(1)} %copy-done.8, bf16[128,1024]{1,0:T(8,128)(2,1)S(1)} %mix.9.refs_0_.mine), custom_call_target="tpu_custom_call" | custom-call | flops 2013265920 | bytes 4194304 | tf_op jit(solution)/shard_map/pallas_call | solution.py:178
  45.7 7.0 %collective-permute-done.6.theirs = bf16[128,1024]{1,0:T(8,128)(2,1)S(1)} collective-permute-done((bf16[128,1024]{1,0:T(8,128)(2,1)S(1)}, bf16[128,1024]{1,0:T(8,128)(2,1)S(1)}, u32[]{:S(2)}, u32[]{:S(2)}) %collective-permute-start.6) | collective-permute-done | bytes 262176 | tf_op jit(solution)/shard_map/ppermute | solution.py:42
  52.7 0.7 %mix.10.state = bf16[128,1024]{1,0:T(8,128)(2,1)S(1)} custom-call(bf16[128,1024]{1,0:T(8,128)(2,1)S(1)} %mix.8.refs_0_.mine, bf16[128,1024]{1,0:T(8,128)(2,1)S(1)} %collective-permute-done.6.theirs, bf16[1024,1024]{1,0:T(8,128)(2,1)S(1)} %get-tuple-element.28.refs_0_.near, bf16[1024,1024]{1,0:T(8,128)(2,1)S(1)} %get-tuple-element.29.far, ...), custom_call_target="tpu_custom_call" | custom-call | flops 377487360 | bytes 4194304 | tf_op jit(solution)/shard_map/mix/pallas_call | solution.py:245
  53.5 0.8 %shard_map.78 = (f32[1,1024]{1,0:T(1,128)S(1)}, f32[1,1024]{1,0:T(1,128)S(1)}) custom-call(bf16[128,1024]{1,0:T(8,128)(2,1)S(1)} %mix.10.state, bf16[1024,1024]{1,0:T(8,128)(2,1)S(1)} %get-tuple-element.30.refs_0_, bf16[1024,1024]{1,0:T(8,128)(2,1)S(1)} %get-tuple-element.31.refs_1_.refs_0_, bf16[256,1024]{1,0:T(8,128)(2,1)S(1)} %copy-done.2, ...), custom_call_target="tpu_custom_call" | custom-call | flops 402653184 | bytes 4194304 | tf_op jit(solution)/shard_map/pallas_call | solution.py:277
  54.3 3.4 %collective-permute-done.5.theirs = bf16[128,1024]{1,0:T(8,128)(2,1)S(1)} collective-permute-done((bf16[128,1024]{1,0:T(8,128)(2,1)S(1)}, bf16[128,1024]{1,0:T(8,128)(2,1)S(1)}, u32[]{:S(2)}, u32[]{:S(2)}) %collective-permute-start.5) | collective-permute-done | bytes 262176 | tf_op jit(solution)/shard_map/ppermute | solution.py:42
  57.7 0.7 %mix.11.state = bf16[128,1024]{1,0:T(8,128)(2,1)S(1)} custom-call(bf16[128,1024]{1,0:T(8,128)(2,1)S(1)} %mix.9.refs_0_.mine, bf16[128,1024]{1,0:T(8,128)(2,1)S(1)} %collective-permute-done.5.theirs, bf16[1024,1024]{1,0:T(8,128)(2,1)S(1)} %get-tuple-element.28.refs_0_.near, bf16[1024,1024]{1,0:T(8,128)(2,1)S(1)} %get-tuple-element.29.far, ...), custom_call_target="tpu_custom_call" | custom-call | flops 377487360 | bytes 4194304 | tf_op jit(solution)/shard_map/mix/pallas_call | solution.py:245
  58.4 0.5 shard_map.79.refs_3_
  58.9 0.1 collective-permute-start.8
  59.0 0.5 shard_map.80
  59.5 3.9 %collective-permute-done.8 = f32[1,1024]{1,0:T(1,128)S(1)} collective-permute-done((f32[1,1024]{1,0:T(1,128)S(1)}, f32[1,1024]{1,0:T(1,128)S(1)}, u32[]{:S(2)}, u32[]{:S(2)}) %collective-permute-start.8) | collective-permute-done | bytes 4128 | tf_op jit(solution)/shard_map/ppermute | solution.py:42
  63.5 0.6 multiply_multiply_fusion
  (23 shorter events, 0.1 us)
Async XLA Ops:
  2.4 4.4 %copy-start.5 = (bf16[256,1024]{1,0:T(8,128)(2,1)S(1)}, bf16[256,1024]{1,0:T(8,128)(2,1)}, u32[]{:S(2)}) copy-start(bf16[256,1024]{1,0:T(8,128)(2,1)} %wave.3) | copy-start | bytes 1572868
  2.4 4.4 %copy-start.6 = (f32[256,65]{0,1:T(8,128)S(1)}, f32[256,65]{0,1:T(8,128)}, u32[]{:S(2)}) copy-start(f32[256,65]{0,1:T(8,128)} %param.8) | copy-start | bytes 199684
  2.4 4.3 %collective-permute-start = (bf16[256,128]{1,0:T(8,128)(2,1)}, bf16[256,128]{1,0:T(8,128)(2,1)S(1)}, u32[]{:S(2)}, u32[]{:S(2)}) collective-permute-start(bf16[256,128]{1,0:T(8,128)(2,1)} %get-tuple-element.20), channel_id=1, source_target_pairs={{0,1},{1,0},{2,3},{3,2},{4,5},{5,4},{6,7},{7,6},{8,9},{9,8},{10,11... | collective-permute-start | bytes 196616 | tf_op jit(solution)/shard_map/ppermute | solution.py:42
  3.0 3.8 %collective-permute-start.1 = (bf16[256,128]{1,0:T(8,128)(2,1)}, bf16[256,128]{1,0:T(8,128)(2,1)S(1)}, u32[]{:S(2)}, u32[]{:S(2)}) collective-permute-start(bf16[256,128]{1,0:T(8,128)(2,1)} %get-tuple-element.21), channel_id=1, source_target_pairs={{1,2},{2,1},{3,4},{4,3},{5,6},{6,5},{7,8},{8,7},{9,10},{10,9},{11,... | collective-permute-start | bytes 196616 | tf_op jit(solution)/shard_map/ppermute | solution.py:38
  3.7 0.9 %copy-start.7 = (f32[32,1024]{1,0:T(8,128)S(1)}, f32[32,1024]{1,0:T(8,128)}, u32[]{:S(2)}) copy-start(f32[32,1024]{1,0:T(8,128)} %get-tuple-element.25.coords) | copy-start | bytes 393220
  6.7 12.3 %copy-start = (bf16[1024,1024]{1,0:T(8,128)(2,1)}, bf16[1024,1024]{1,0:T(8,128)(2,1)S(1)}, u32[]{:S(2)}) copy-start(bf16[1024,1024]{1,0:T(8,128)(2,1)S(1)} %shard_map.73.refs_0_.near) | copy-start | bytes 6291460
  12.8 6.2 %collective-permute-start.2 = (bf16[256,1024]{1,0:T(8,128)(2,1)S(1)}, bf16[256,1024]{1,0:T(8,128)(2,1)S(1)}, u32[]{:S(2)}, u32[]{:S(2)}) collective-permute-start(bf16[256,1024]{1,0:T(8,128)(2,1)S(1)} %redatum.1.refs_0_.mine), channel_id=1, source_target_pairs={{0,1},{1,0},{2,3},{3,2},{4,5},{5,4},{6,7},{7,6},{8,9},{9,8},{10,11... | collective-permute-start | bytes 1572872 | tf_op jit(solution)/shard_map/ppermute | solution.py:42
  19.0 2.7 %copy-start.2 = (bf16[256,1024]{1,0:T(8,128)(2,1)S(1)}, bf16[256,1024]{1,0:T(8,128)(2,1)}, u32[]{:S(2)}) copy-start(bf16[256,1024]{1,0:T(8,128)(2,1)} %get-tuple-element.32.refs_2_.refs_1_) | copy-start | bytes 1572868
  19.0 0.8 %copy-start.3 = (bf16[256,1024]{1,0:T(8,128)(2,1)}, bf16[256,1024]{1,0:T(8,128)(2,1)S(1)}, u32[]{:S(2)}) copy-start(bf16[256,1024]{1,0:T(8,128)(2,1)S(1)} %collective-permute-done.2.theirs) | copy-start | bytes 1572868
  19.8 12.7 %collective-permute-start.4 = (bf16[128,1024]{1,0:T(8,128)(2,1)S(1)}, bf16[128,1024]{1,0:T(8,128)(2,1)}, u32[]{:S(2)}, u32[]{:S(2)}) collective-permute-start(bf16[128,1024]{1,0:T(8,128)(2,1)S(1)} %mix.6.refs_0_.mine), channel_id=1, source_target_pairs={{0,2},{1,3},{2,0},{3,1},{4,6},{5,7},{6,4},{7,5},{8,10},{9,11},{10,... | collective-permute-start | bytes 786440 | tf_op jit(solution)/shard_map/ppermute | solution.py:42
  21.7 31.8 %collective-permute-start.7 = (bf16[256,1024]{1,0:T(8,128)(2,1)S(1)}, bf16[256,1024]{1,0:T(8,128)(2,1)S(1)}, u32[]{:S(2)}, u32[]{:S(2)}) collective-permute-start(bf16[256,1024]{1,0:T(8,128)(2,1)S(1)} %copy-done.2), channel_id=1, source_target_pairs={{0,8},{1,9},{2,10},{3,11},{4,12},{5,13},{6,14},{7,15},{8,0},{9,1},... | collective-permute-start | bytes 1572872 | tf_op jit(solution)/shard_map/ppermute | solution.py:42
  24.3 1.6 %copy-start.1 = (bf16[1024,1024]{1,0:T(8,128)(2,1)S(1)}, bf16[1024,1024]{1,0:T(8,128)(2,1)}, u32[]{:S(2)}) copy-start(bf16[1024,1024]{1,0:T(8,128)(2,1)} %copy-done) | copy-start | bytes 6291460
  25.9 1.0 %copy-start.4 = (bf16[256,1024]{1,0:T(8,128)(2,1)S(1)}, bf16[256,1024]{1,0:T(8,128)(2,1)}, u32[]{:S(2)}) copy-start(bf16[256,1024]{1,0:T(8,128)(2,1)} %copy-done.3) | copy-start | bytes 1572868
  26.9 1.2 %copy-start.8 = (f32[32,1024]{1,0:T(8,128)S(1)}, f32[32,1024]{1,0:T(8,128)}, u32[]{:S(2)}) copy-start(f32[32,1024]{1,0:T(8,128)} %get-tuple-element.25.coords) | copy-start | bytes 393220
  27.7 12.4 %collective-permute-start.3 = (bf16[128,1024]{1,0:T(8,128)(2,1)S(1)}, bf16[128,1024]{1,0:T(8,128)(2,1)S(1)}, u32[]{:S(2)}, u32[]{:S(2)}) collective-permute-start(bf16[128,1024]{1,0:T(8,128)(2,1)S(1)} %mix.7.refs_0_.mine), channel_id=1, source_target_pairs={{0,2},{1,3},{2,0},{3,1},{4,6},{5,7},{6,4},{7,5},{8,10},{9,11},{10,... | collective-permute-start | bytes 786440 | tf_op jit(solution)/shard_map/ppermute | solution.py:42
  34.2 18.6 %collective-permute-start.6 = (bf16[128,1024]{1,0:T(8,128)(2,1)S(1)}, bf16[128,1024]{1,0:T(8,128)(2,1)S(1)}, u32[]{:S(2)}, u32[]{:S(2)}) collective-permute-start(bf16[128,1024]{1,0:T(8,128)(2,1)S(1)} %mix.8.refs_0_.mine), channel_id=1, source_target_pairs={{0,4},{1,5},{2,6},{3,7},{4,0},{5,1},{6,2},{7,3},{8,12},{9,13},{10,... | collective-permute-start | bytes 786440 | tf_op jit(solution)/shard_map/ppermute | solution.py:42
  40.8 16.8 %collective-permute-start.5 = (bf16[128,1024]{1,0:T(8,128)(2,1)S(1)}, bf16[128,1024]{1,0:T(8,128)(2,1)S(1)}, u32[]{:S(2)}, u32[]{:S(2)}) collective-permute-start(bf16[128,1024]{1,0:T(8,128)(2,1)S(1)} %mix.9.refs_0_.mine), channel_id=1, source_target_pairs={{0,4},{1,5},{2,6},{3,7},{4,0},{5,1},{6,2},{7,3},{8,12},{9,13},{10,... | collective-permute-start | bytes 786440 | tf_op jit(solution)/shard_map/ppermute | solution.py:42
  58.9 4.6 %dynamic-slice-start = ((f32[16384]{0:T(1024)}, s32[]{:T(128)}), f32[1024]{0:T(1024)S(1)}, s32[]{:S(2)}) async-start(f32[16384]{0:T(1024)} %param.12, s32[]{:T(128)} %select_n.11), calls=%async_computation | async-start | bytes 8704 | tf_op jit(solution)/shard_map/dynamic_slice | solution.py:336
  58.9 4.6 %collective-permute-start.8 = (f32[1,1024]{1,0:T(1,128)S(1)}, f32[1,1024]{1,0:T(1,128)S(1)}, u32[]{:S(2)}, u32[]{:S(2)}) collective-permute-start(f32[1,1024]{1,0:T(1,128)S(1)} %shard_map.79.refs_3_), channel_id=1, source_target_pairs={{0,8},{1,9},{2,10},{3,11},{4,12},{5,13},{6,14},{7,15},{8,0},{9,1},... | collective-permute-start | bytes 12296 | tf_op jit(solution)/shard_map/ppermute | solution.py:42

commit v6 on v5

--- a/solution.py
+++ b/solution.py
@@ -57,11 +57,11 @@
     return box, box + bit - 2 * bit * upper
 
 
-ROW, OTHER_ROW, COLUMN, BELOW, OTHER_COLUMN, OTHER_BELOW = range(6)
-
-
-def prepare_kernel(blocks, wave, aperture, cell_x, depth, slowness, *refs):
-    near_edge, far_edge, mask, coords, cells, depths, slow, marks, sems = refs
+ROW, OTHER_ROW, COLUMN, BELOW, OTHER_COLUMN, OTHER_BELOW, WEIGHT, OTHER_WEIGHT = range(8)
+
+
+def prepare_kernel(blocks, wave, aperture, cell_x, depth, illumination, slowness, *refs):
+    near_edge, far_edge, mask, coords, cells, depths, lights, slow, marks, sems = refs
     width = wave.shape[1]
     tall = width // LANES
     box = boxes_of(0, blocks)[0]
@@ -73,6 +73,8 @@
     for k, which in enumerate((box, others[-1])):
         at = pl.ds(pl.multiple_of(which * tall, tall), tall)
         copies.append(pltpu.make_async_copy(depth.at[at, :], depths.at[k], sems.at[6 + k]))
+        light = illumination.at[at, :]
+        copies.append(pltpu.make_async_copy(light, lights.at[k], sems.at[11 + k]))
     end = width - LANES
     even = 1 - box % 2
     first = pl.ds(pl.multiple_of(even * end, LANES), LANES)
@@ -108,12 +110,19 @@
         if level + 1 == LEVELS:
             put(OTHER_COLUMN, LEVELS, level + 1)
             put_below(OTHER_BELOW, 1)
+    share = 1.0 / math.sqrt(wave.shape[0] * blocks)
+    base = 8 * (LEVELS - 1)
+    for source, kind in enumerate((WEIGHT, OTHER_WEIGHT)):
+        for k in range(tall):
+            coords[base + kind : base + kind + 1, k * LANES : (k + 1) * LANES] = (
+                lights[source, k : k + 1, :] * share
+            )
     for copy in late:
         copy.wait()
     mask[...] = (marks[...] > 0).astype(jnp.float32).astype(jnp.bfloat16)
 
 
-def prepare(blocks, wave, aperture, cell_x, depth, slowness):
+def prepare(blocks, wave, aperture, cell_x, depth, illumination, slowness):
     count, width = wave.shape
     levels = cell_x.shape[0]
     edge = jax.ShapeDtypeStruct((count, LANES), wave.dtype)
@@ -125,19 +134,20 @@
             jax.ShapeDtypeStruct((count, width), jnp.bfloat16),
             jax.ShapeDtypeStruct((8 * LEVELS, width), jnp.float32),
         ),
-        in_specs=[HBM] * 5,
+        in_specs=[HBM] * 6,
         out_specs=(VMEM,) * 4,
         scratch_shapes=[
             pltpu.VMEM((1 + LEVELS, levels, width), jnp.int32),
             pltpu.VMEM((2, width // LANES, LANES), jnp.int32),
+            pltpu.VMEM((2, width // LANES, LANES), jnp.float32),
             pltpu.SMEM((LEVELS,), jnp.float32),
             pltpu.VMEM((count, width), jnp.int32),
-            pltpu.SemaphoreType.DMA((11,)),
+            pltpu.SemaphoreType.DMA((13,)),
         ],
         compiler_params=pltpu.CompilerParams(vmem_limit_bytes=GRANT),
         cost_estimate=cost(24 * 2 * width * width * 15, count * width * 8),
         name="prepare",
-    )(wave, aperture, cell_x, depth, slowness)
+    )(wave, aperture, cell_x, depth, illumination, slowness)
 
 
 def tables_kernel(jobs, step, coords, *refs):
@@ -253,7 +263,8 @@
     )(mine, theirs, near, far, *after)
 
 
-def last_kernel(part, count, added, state, *refs):
+def last_kernel(part, weights, added, state, coords, *refs):
+    count = len(weights)
     tables, masks, sums = refs[:count], refs[count : 2 * count], refs[2 * count : 2 * count + added]
     width = tables[0].shape[1]
     scale = SCALE / math.sqrt(width)
@@ -265,35 +276,39 @@
             mixed = jnp.dot(state[...], tables[k][:, columns], preferred_element_type=jnp.float32)
             kept = jnp.where(masks[k][held, columns].astype(jnp.float32) > 0, mixed, 0.0)
             total = jnp.sum(kept, 0, keepdims=True) * scale
+            total = total * coords[weights[k] : weights[k] + 1, columns]
             if added:
                 total = total + sums[k][:, columns]
             out[:, columns] = total
 
 
-def last(part, state, tables, masks, sums, *after):
+def last(part, which, state, coords, tables, masks, sums, *after):
     width = state.shape[1]
-    count = len(tables)
+    count = len(which)
+    base = 8 * (LEVELS - 1)
+    weights = [base + (WEIGHT, OTHER_WEIGHT)[k] for k in which]
+    tables, masks = [tables[k] for k in which], [masks[k] for k in which]
     shape = jax.ShapeDtypeStruct((1, width), jnp.float32)
     return pl.pallas_call(
-        functools.partial(last_kernel, part, count, len(sums)),
+        functools.partial(last_kernel, part, weights, len(sums)),
         out_shape=(shape,) * count,
-        in_specs=[VMEM] * (1 + 2 * count + len(sums)) + [ANY] * len(after),
+        in_specs=[VMEM] * (2 + 2 * count + len(sums)) + [ANY] * len(after),
         out_specs=(VMEM,) * count,
         compiler_params=params(7),
         cost_estimate=cost(24 * count * width * width * 8, 2 * count * width * width),
-    )(state, *tables, *masks, *sums, *after)
+    )(state, coords, *tables, *masks, *sums, *after)
 
 
 def on_device(wavefield, redatum_taps, cell_x, cell_depth, slowness, illumination, aperture):
     index = lax.axis_index("space")
     blocks = lax.axis_size("space") // BOXES
     block_bits = blocks.bit_length() - 1
-    box = index // blocks
     block = index % blocks
     count, width = wavefield.shape
     depth = cell_depth.reshape(BOXES * width // LANES, LANES)
+    light = illumination.reshape(BOXES * width // LANES, LANES)
     near_edge, far_edge, mask, coords = prepare(
-        blocks, wavefield, aperture, cell_x, depth, slowness
+        blocks, wavefield, aperture, cell_x, depth, light, slowness
     )
     near_edge = partner(near_edge, "space", block_bits)
     far_edge = across(far_edge, "space", blocks)
@@ -318,11 +333,12 @@
             states[part] = mix(part, states[part], theirs[part], *table, ahead)
             ahead = states[part]
             if level + 2 == LEVELS and part + 1 < len(parts):
-                sums = last(part, states[part], later, both, sums)
+                sums = last(part, (0, 1), states[part], coords, later, both, sums)
                 ahead = sums[0]
             if level + 2 == LEVELS and part + 1 == len(parts):
-                (other,) = last(part, states[part], later[1:], both[1:], sums[1:])
-                (own,) = last(part, states[part], later[:1], both[:1], sums[:1], other)
+                final = (states[part], coords, later, both)
+                (other,) = last(part, (1,), *final, sums[1:])
+                (own,) = last(part, (0,), *final, sums[:1], other)
             if level + 2 < LEVELS:
                 theirs[part] = partner(states[part], "space", level + 1 + block_bits)
             if part == (0 if level == 1 else len(parts) - 1) and level < 2:
@@ -332,9 +348,7 @@
                 later = tables(level + 2, (0, 1), coords, ahead)
                 ahead = later[0]
         table = following
-    summed = own + partner(other, "space", LEVELS - 1 + block_bits)
-    weights = lax.dynamic_slice_in_dim(illumination, box * width, width)
-    image = summed * weights[None] / jnp.sqrt(jnp.float32(count * blocks))
+    image = own + partner(other, "space", LEVELS - 1 + block_bits)
     for level in range(block_bits):
         image = image + partner(image, "space", level)
     share = width // blocks

time: 64.4 us -> 60.6 us (0.941)
  local copies, waits for them, and re-layouts: 3.62 us -> 0.91 us
  Pallas kernels: 32.7 us -> 31.8 us
    unnamed x18 -> x10, local copies, waits for them, and re-layouts: 3.61 us -> 0.91 us
    pallas_call x6, Pallas kernels: 5.3 us -> 4.33 us  [mix(): pl.pallas_call(functools.partial(mix_kernel, held), out_shape=jax.ShapeDt...]
  transfers between devices with their start and end apart: 9 -> 9, of which waited for: 3 -> 3; matrix products, arithmetic and copies ran while one was open for 0% -> 0% of each run, Pallas kernels for 35% -> 36%
where the time goes in v6:
time: 60.6 us; the launch traced here: 60.4 us
  Pallas kernels  31.8 us (52%)
  waiting for transfers between devices  13.8 us (23%)
  starting transfers between devices  13.1 us (22%)
  local copies, waits for them, and re-layouts  0.91 us (2%)
    pallas_call x5, Pallas kernels, tables(): pl.pallas_call(functools.partial(tables_kernel, jobs, step), out_shape=(s...  17.3 us
    ppermute x8, waiting for transfers between devices, partner(): lax.ppermute(shard, axis, [(i, i ^ 1 << bit) for i in range(lax.axis_size...  13.8 us
    ppermute x8, starting transfers between devices, partner(): lax.ppermute(shard, axis, [(i, i ^ 1 << bit) for i in range(lax.axis_size...  12.5 us
    pallas_call x1, Pallas kernels, redatum(): pl.pallas_call(functools.partial(redatum_kernel, reach, blocks), out_shap...  5.95 us
    pallas_call x6, Pallas kernels, mix(): pl.pallas_call(functools.partial(mix_kernel, held), out_shape=jax.ShapeDt...  4.33 us
    pallas_call x1, Pallas kernels, prepare(): pl.pallas_call(functools.partial(prepare_kernel, blocks), out_shape=(edge...  2.49 us
    pallas_call x3, Pallas kernels, last(): pl.pallas_call(functools.partial(last_kernel, part, weights, len(sums)),...  1.72 us
  transfers between devices with their start and end apart: 9, of which 3 were waited for; matrix products, arithmetic and copies ran while one was open for 0% of the time, Pallas kernels for 36%

profile of v6, /device:TPU:0, one launch (start us, length us, event | category | flops | bytes accessed | tf_op | source)
XLA Modules:
  0.0 60.4 jit_solution(12344335994911913719)
XLA Ops:
  0.0 2.5 %prepare.1 = (bf16[256,128]{1,0:T(8,128)(2,1)}, bf16[256,128]{1,0:T(8,128)(2,1)}, bf16[256,1024]{1,0:T(8,128)(2,1)}, f32[32,1024]{1,0:T(8,128)}) custom-call(bf16[256,1024]{1,0:T(8,128)(2,1)} %wave.3, s32[256,1024]{1,0:T(8,128)} %aperture.1, s32[5,16384]{1,0:T(8,128)} %cell_x.1, s32[128,128]{1,0:T(8,128)} %bitcast.4, f32[128,128]{1,0:T(8,128)} %bitcast.5, ...), custom_call_target="tpu_custom_call" | custom-call | flops 754974720 | bytes 2097152 | tf_op jit(solution)/shard_map/prepare/pallas_call | solution.py:129
  2.5 0.6 collective-permute-start
  3.1 0.7 %collective-permute-start.1 = (bf16[256,128]{1,0:T(8,128)(2,1)}, bf16[256,128]{1,0:T(8,128)(2,1)S(1)}, u32[]{:S(2)}, u32[]{:S(2)}) collective-permute-start(bf16[256,128]{1,0:T(8,128)(2,1)} %get-tuple-element.21), channel_id=1, source_target_pairs={{1,2},{2,1},{3,4},{4,3},{5,6},{6,5},{7,8},{8,7},{9,10},{10,9},{11,... | collective-permute-start | bytes 196616 | tf_op jit(solution)/shard_map/ppermute | solution.py:38
  3.7 0.9 %copy-done.1 = f32[32,1024]{1,0:T(8,128)S(1)} copy-done((f32[32,1024]{1,0:T(8,128)S(1)}, f32[32,1024]{1,0:T(8,128)}, u32[]{:S(2)}) %copy-start.1) | copy-done | bytes 131096
  4.6 2.2 %shard_map.73.refs_0_.near = bf16[1024,1024]{1,0:T(8,128)(2,1)S(1)} custom-call(f32[32,1024]{1,0:T(8,128)S(1)} %copy-done.1), custom_call_target="tpu_custom_call" | custom-call | flops 1006632960 | bytes 2097152 | tf_op jit(solution)/shard_map/pallas_call | solution.py:188
  6.8 0.0 collective-permute-done.near_edge
  6.9 6.0 %redatum.1.refs_0_.mine = bf16[256,1024]{1,0:T(8,128)(2,1)S(1)} custom-call(bf16[256,128]{1,0:T(8,128)(2,1)S(1)} %collective-permute-done.near_edge, bf16[256,1024]{1,0:T(8,128)(2,1)S(1)} %copy-done.3, bf16[256,128]{1,0:T(8,128)(2,1)S(1)} %collective-permute-done.1.far_edge, f32[65,256]{1,0:T(8,128)S(1)} %bitcast.3, ...), custom_call_target="tpu_custom_call" | custom-call | flops 3019898880 | bytes 1048576 | tf_op jit(solution)/shard_map/redatum/pallas_call | solution.py:228
  12.8 3.9 %collective-permute-start.2 = (bf16[256,1024]{1,0:T(8,128)(2,1)S(1)}, bf16[256,1024]{1,0:T(8,128)(2,1)S(1)}, u32[]{:S(2)}, u32[]{:S(2)}) collective-permute-start(bf16[256,1024]{1,0:T(8,128)(2,1)S(1)} %redatum.1.refs_0_.mine), channel_id=1, source_target_pairs={{0,1},{1,0},{2,3},{3,2},{4,5},{5,4},{6,7},{7,6},{8,9},{9,8},{10,11... | collective-permute-start | bytes 1572872 | tf_op jit(solution)/shard_map/ppermute | solution.py:42
  16.7 2.2 %shard_map.74.far.refs_0_ = bf16[1024,1024]{1,0:T(8,128)(2,1)S(1)} custom-call(f32[32,1024]{1,0:T(8,128)S(1)} %copy-done.2, bf16[256,1024]{1,0:T(8,128)(2,1)S(1)} %redatum.1.refs_0_.mine), custom_call_target="tpu_custom_call" | custom-call | flops 1006632960 | bytes 2097152 | tf_op jit(solution)/shard_map/pallas_call | solution.py:188
  18.9 0.0 collective-permute-done.2.theirs
  18.9 0.7 %mix.6.refs_0_.mine = bf16[128,1024]{1,0:T(8,128)(2,1)S(1)} custom-call(bf16[256,1024]{1,0:T(8,128)(2,1)S(1)} %redatum.1.refs_0_.mine, bf16[256,1024]{1,0:T(8,128)(2,1)S(1)} %collective-permute-done.2.theirs, bf16[1024,1024]{1,0:T(8,128)(2,1)S(1)} %shard_map.73.refs_0_.near, bf16[1024,1024]{1,0:T(8,128)(2,1)S(1)} %shard_map.74.far.refs_0_, ...), custom_call_target="tpu_custom_call" | custom-call | flops 377487360 | bytes 4194304 | tf_op jit(solution)/shard_map/mix/pallas_call | solution.py:255
  19.7 2.1 %collective-permute-start.4 = (bf16[128,1024]{1,0:T(8,128)(2,1)S(1)}, bf16[128,1024]{1,0:T(8,128)(2,1)S(1)}, u32[]{:S(2)}, u32[]{:S(2)}) collective-permute-start(bf16[128,1024]{1,0:T(8,128)(2,1)S(1)} %mix.6.refs_0_.mine), channel_id=1, source_target_pairs={{0,2},{1,3},{2,0},{3,1},{4,6},{5,7},{6,4},{7,5},{8,10},{9,11},{10,... | collective-permute-start | bytes 786440 | tf_op jit(solution)/shard_map/ppermute | solution.py:42
  21.8 2.6 %collective-permute-start.7 = (bf16[256,1024]{1,0:T(8,128)(2,1)S(1)}, bf16[256,1024]{1,0:T(8,128)(2,1)S(1)}, u32[]{:S(2)}, u32[]{:S(2)}) collective-permute-start(bf16[256,1024]{1,0:T(8,128)(2,1)S(1)} %copy-done), channel_id=1, source_target_pairs={{0,8},{1,9},{2,10},{3,11},{4,12},{5,13},{6,14},{7,15},{8,0},{9,1},... | collective-permute-start | bytes 1572872 | tf_op jit(solution)/shard_map/ppermute | solution.py:42
  24.4 0.7 %mix.7.refs_0_.mine = bf16[128,1024]{1,0:T(8,128)(2,1)S(1)} custom-call(bf16[256,1024]{1,0:T(8,128)(2,1)S(1)} %redatum.1.refs_0_.mine, bf16[256,1024]{1,0:T(8,128)(2,1)S(1)} %collective-permute-done.2.theirs, bf16[1024,1024]{1,0:T(8,128)(2,1)S(1)} %shard_map.73.refs_0_.near, bf16[1024,1024]{1,0:T(8,128)(2,1)S(1)} %shard_map.74.far.refs_0_, ...), custom_call_target="tpu_custom_call" | custom-call | flops 377487360 | bytes 4194304 | tf_op jit(solution)/shard_map/mix/pallas_call | solution.py:255
  25.1 0.4 collective-permute-start.3
  25.5 4.3 %shard_map.75 = (bf16[1024,1024]{1,0:T(8,128)(2,1)S(1)}, bf16[1024,1024]{1,0:T(8,128)(2,1)S(1)}) custom-call(f32[32,1024]{1,0:T(8,128)S(1)} %copy-done.2, bf16[128,1024]{1,0:T(8,128)(2,1)S(1)} %mix.7.refs_0_.mine), custom_call_target="tpu_custom_call" | custom-call | flops 2013265920 | bytes 4194304 | tf_op jit(solution)/shard_map/pallas_call | solution.py:188
  29.8 0.7 %mix.8.refs_0_.mine = bf16[128,1024]{1,0:T(8,128)(2,1)S(1)} custom-call(bf16[128,1024]{1,0:T(8,128)(2,1)S(1)} %mix.6.refs_0_.mine, bf16[128,1024]{1,0:T(8,128)(2,1)S(1)} %collective-permute-done.4.theirs, bf16[1024,1024]{1,0:T(8,128)(2,1)S(1)} %get-tuple-element.26.near.refs_0_, bf16[1024,1024]{1,0:T(8,128)(2,1)S(1)} %get-tuple-element.27.far, ...), custom_call_target="tpu_custom_call" | custom-call | flops 377487360 | bytes 4194304 | tf_op jit(solution)/shard_map/mix/pallas_call | solution.py:255
  30.6 1.6 %collective-permute-start.6 = (bf16[128,1024]{1,0:T(8,128)(2,1)S(1)}, bf16[128,1024]{1,0:T(8,128)(2,1)S(1)}, u32[]{:S(2)}, u32[]{:S(2)}) collective-permute-start(bf16[128,1024]{1,0:T(8,128)(2,1)S(1)} %mix.8.refs_0_.mine), channel_id=1, source_target_pairs={{0,4},{1,5},{2,6},{3,7},{4,0},{5,1},{6,2},{7,3},{8,12},{9,13},{10,... | collective-permute-start | bytes 786440 | tf_op jit(solution)/shard_map/ppermute | solution.py:42
  32.2 4.3 %shard_map.76 = (bf16[1024,1024]{1,0:T(8,128)(2,1)S(1)}, bf16[1024,1024]{1,0:T(8,128)(2,1)S(1)}) custom-call(f32[32,1024]{1,0:T(8,128)S(1)} %copy-done.2, bf16[128,1024]{1,0:T(8,128)(2,1)S(1)} %mix.8.refs_0_.mine), custom_call_target="tpu_custom_call" | custom-call | flops 2013265920 | bytes 4194304 | tf_op jit(solution)/shard_map/pallas_call | solution.py:188
  36.6 0.7 %mix.9.refs_0_.mine = bf16[128,1024]{1,0:T(8,128)(2,1)S(1)} custom-call(bf16[128,1024]{1,0:T(8,128)(2,1)S(1)} %mix.7.refs_0_.mine, bf16[128,1024]{1,0:T(8,128)(2,1)S(1)} %collective-permute-done.3.theirs, bf16[1024,1024]{1,0:T(8,128)(2,1)S(1)} %get-tuple-element.26.near.refs_0_, bf16[1024,1024]{1,0:T(8,128)(2,1)S(1)} %get-tuple-element.27.far, ...), custom_call_target="tpu_custom_call" | custom-call | flops 377487360 | bytes 4194304 | tf_op jit(solution)/shard_map/mix/pallas_call | solution.py:255
  37.3 0.5 collective-permute-start.5
  37.8 4.3 %shard_map.77 = (bf16[1024,1024]{1,0:T(8,128)(2,1)S(1)}, bf16[1024,1024]{1,0:T(8,128)(2,1)S(1)}) custom-call(f32[32,1024]{1,0:T(8,128)S(1)} %copy-done.2, bf16[128,1024]{1,0:T(8,128)(2,1)S(1)} %mix.9.refs_0_.mine), custom_call_target="tpu_custom_call" | custom-call | flops 2013265920 | bytes 4194304 | tf_op jit(solution)/shard_map/pallas_call | solution.py:188
  42.1 7.2 %collective-permute-done.6.theirs = bf16[128,1024]{1,0:T(8,128)(2,1)S(1)} collective-permute-done((bf16[128,1024]{1,0:T(8,128)(2,1)S(1)}, bf16[128,1024]{1,0:T(8,128)(2,1)S(1)}, u32[]{:S(2)}, u32[]{:S(2)}) %collective-permute-start.6) | collective-permute-done | bytes 262176 | tf_op jit(solution)/shard_map/ppermute | solution.py:42
  49.3 0.7 %mix.10.state = bf16[128,1024]{1,0:T(8,128)(2,1)S(1)} custom-call(bf16[128,1024]{1,0:T(8,128)(2,1)S(1)} %mix.8.refs_0_.mine, bf16[128,1024]{1,0:T(8,128)(2,1)S(1)} %collective-permute-done.6.theirs, bf16[1024,1024]{1,0:T(8,128)(2,1)S(1)} %get-tuple-element.28.refs_0_.near, bf16[1024,1024]{1,0:T(8,128)(2,1)S(1)} %get-tuple-element.29.far, ...), custom_call_target="tpu_custom_call" | custom-call | flops 377487360 | bytes 4194304 | tf_op jit(solution)/shard_map/mix/pallas_call | solution.py:255
  50.1 0.8 %shard_map.78 = (f32[1,1024]{1,0:T(1,128)S(1)}, f32[1,1024]{1,0:T(1,128)S(1)}) custom-call(bf16[128,1024]{1,0:T(8,128)(2,1)S(1)} %mix.10.state, f32[32,1024]{1,0:T(8,128)S(1)} %copy-done.2, bf16[1024,1024]{1,0:T(8,128)(2,1)S(1)} %get-tuple-element.30.refs_0_, bf16[1024,1024]{1,0:T(8,128)(2,1)S(1)} %get-tuple-element.31.refs_1_.refs_0_, ...), custom_call_target="tpu_custom_call" | custom-call | flops 402653184 | bytes 4194304 | tf_op jit(solution)/shard_map/pallas_call | solution.py:292
  50.8 3.2 %collective-permute-done.5.theirs = bf16[128,1024]{1,0:T(8,128)(2,1)S(1)} collective-permute-done((bf16[128,1024]{1,0:T(8,128)(2,1)S(1)}, bf16[128,1024]{1,0:T(8,128)(2,1)S(1)}, u32[]{:S(2)}, u32[]{:S(2)}) %collective-permute-start.5) | collective-permute-done | bytes 262176 | tf_op jit(solution)/shard_map/ppermute | solution.py:42
  54.1 0.7 %mix.11.state = bf16[128,1024]{1,0:T(8,128)(2,1)S(1)} custom-call(bf16[128,1024]{1,0:T(8,128)(2,1)S(1)} %mix.9.refs_0_.mine, bf16[128,1024]{1,0:T(8,128)(2,1)S(1)} %collective-permute-done.5.theirs, bf16[1024,1024]{1,0:T(8,128)(2,1)S(1)} %get-tuple-element.28.refs_0_.near, bf16[1024,1024]{1,0:T(8,128)(2,1)S(1)} %get-tuple-element.29.far, ...), custom_call_target="tpu_custom_call" | custom-call | flops 377487360 | bytes 4194304 | tf_op jit(solution)/shard_map/mix/pallas_call | solution.py:255
  54.8 0.5 shard_map.79.refs_3_
  55.3 0.8 %collective-permute-start.8 = (f32[1,1024]{1,0:T(1,128)S(1)}, f32[1,1024]{1,0:T(1,128)S(1)}, u32[]{:S(2)}, u32[]{:S(2)}) collective-permute-start(f32[1,1024]{1,0:T(1,128)S(1)} %shard_map.79.refs_3_), channel_id=1, source_target_pairs={{0,8},{1,9},{2,10},{3,11},{4,12},{5,13},{6,14},{7,15},{8,0},{9,1},... | collective-permute-start | bytes 12296 | tf_op jit(solution)/shard_map/ppermute | solution.py:42
  56.0 0.5 shard_map.80
  56.5 3.3 %collective-permute-done.8 = f32[1,1024]{1,0:T(1,128)S(1)} collective-permute-done((f32[1,1024]{1,0:T(1,128)S(1)}, f32[1,1024]{1,0:T(1,128)S(1)}, u32[]{:S(2)}, u32[]{:S(2)}) %collective-permute-start.8) | collective-permute-done | bytes 4128 | tf_op jit(solution)/shard_map/ppermute | solution.py:42
  59.8 0.6 add.6
  (13 shorter events, 0.0 us)
Async XLA Ops:
  0.0 6.8 %copy-start.3 = (bf16[256,1024]{1,0:T(8,128)(2,1)S(1)}, bf16[256,1024]{1,0:T(8,128)(2,1)}, u32[]{:S(2)}) copy-start(bf16[256,1024]{1,0:T(8,128)(2,1)} %wave.3) | copy-start | bytes 1572868
  0.0 6.8 %copy-start.4 = (f32[256,65]{0,1:T(8,128)S(1)}, f32[256,65]{0,1:T(8,128)}, u32[]{:S(2)}) copy-start(f32[256,65]{0,1:T(8,128)} %param.8) | copy-start | bytes 199684
  2.5 4.3 %collective-permute-start = (bf16[256,128]{1,0:T(8,128)(2,1)}, bf16[256,128]{1,0:T(8,128)(2,1)S(1)}, u32[]{:S(2)}, u32[]{:S(2)}) collective-permute-start(bf16[256,128]{1,0:T(8,128)(2,1)} %get-tuple-element.20), channel_id=1, source_target_pairs={{0,1},{1,0},{2,3},{3,2},{4,5},{5,4},{6,7},{7,6},{8,9},{9,8},{10,11... | collective-permute-start | bytes 196616 | tf_op jit(solution)/shard_map/ppermute | solution.py:42
  3.1 3.8 %collective-permute-start.1 = (bf16[256,128]{1,0:T(8,128)(2,1)}, bf16[256,128]{1,0:T(8,128)(2,1)S(1)}, u32[]{:S(2)}, u32[]{:S(2)}) collective-permute-start(bf16[256,128]{1,0:T(8,128)(2,1)} %get-tuple-element.21), channel_id=1, source_target_pairs={{1,2},{2,1},{3,4},{4,3},{5,6},{6,5},{7,8},{8,7},{9,10},{10,9},{11,... | collective-permute-start | bytes 196616 | tf_op jit(solution)/shard_map/ppermute | solution.py:38
  3.7 0.9 %copy-start.1 = (f32[32,1024]{1,0:T(8,128)S(1)}, f32[32,1024]{1,0:T(8,128)}, u32[]{:S(2)}) copy-start(f32[32,1024]{1,0:T(8,128)} %get-tuple-element.25.coords) | copy-start | bytes 393220
  6.8 9.9 %copy-start.2 = (f32[32,1024]{1,0:T(8,128)S(1)}, f32[32,1024]{1,0:T(8,128)}, u32[]{:S(2)}) copy-start(f32[32,1024]{1,0:T(8,128)} %get-tuple-element.25.coords) | copy-start | bytes 393220
  12.8 6.1 %collective-permute-start.2 = (bf16[256,1024]{1,0:T(8,128)(2,1)S(1)}, bf16[256,1024]{1,0:T(8,128)(2,1)S(1)}, u32[]{:S(2)}, u32[]{:S(2)}) collective-permute-start(bf16[256,1024]{1,0:T(8,128)(2,1)S(1)} %redatum.1.refs_0_.mine), channel_id=1, source_target_pairs={{0,1},{1,0},{2,3},{3,2},{4,5},{5,4},{6,7},{7,6},{8,9},{9,8},{10,11... | collective-permute-start | bytes 1572872 | tf_op jit(solution)/shard_map/ppermute | solution.py:42
  18.9 2.8 %copy-start = (bf16[256,1024]{1,0:T(8,128)(2,1)S(1)}, bf16[256,1024]{1,0:T(8,128)(2,1)}, u32[]{:S(2)}) copy-start(bf16[256,1024]{1,0:T(8,128)(2,1)} %get-tuple-element.32.refs_2_.refs_1_) | copy-start | bytes 1572868
  19.7 10.2 %collective-permute-start.4 = (bf16[128,1024]{1,0:T(8,128)(2,1)S(1)}, bf16[128,1024]{1,0:T(8,128)(2,1)S(1)}, u32[]{:S(2)}, u32[]{:S(2)}) collective-permute-start(bf16[128,1024]{1,0:T(8,128)(2,1)S(1)} %mix.6.refs_0_.mine), channel_id=1, source_target_pairs={{0,2},{1,3},{2,0},{3,1},{4,6},{5,7},{6,4},{7,5},{8,10},{9,11},{10,... | collective-permute-start | bytes 786440 | tf_op jit(solution)/shard_map/ppermute | solution.py:42
  21.8 28.3 %collective-permute-start.7 = (bf16[256,1024]{1,0:T(8,128)(2,1)S(1)}, bf16[256,1024]{1,0:T(8,128)(2,1)S(1)}, u32[]{:S(2)}, u32[]{:S(2)}) collective-permute-start(bf16[256,1024]{1,0:T(8,128)(2,1)S(1)} %copy-done), channel_id=1, source_target_pairs={{0,8},{1,9},{2,10},{3,11},{4,12},{5,13},{6,14},{7,15},{8,0},{9,1},... | collective-permute-start | bytes 1572872 | tf_op jit(solution)/shard_map/ppermute | solution.py:42
  25.1 11.5 %collective-permute-start.3 = (bf16[128,1024]{1,0:T(8,128)(2,1)S(1)}, bf16[128,1024]{1,0:T(8,128)(2,1)S(1)}, u32[]{:S(2)}, u32[]{:S(2)}) collective-permute-start(bf16[128,1024]{1,0:T(8,128)(2,1)S(1)} %mix.7.refs_0_.mine), channel_id=1, source_target_pairs={{0,2},{1,3},{2,0},{3,1},{4,6},{5,7},{6,4},{7,5},{8,10},{9,11},{10,... | collective-permute-start | bytes 786440 | tf_op jit(solution)/shard_map/ppermute | solution.py:42
  30.6 18.7 %collective-permute-start.6 = (bf16[128,1024]{1,0:T(8,128)(2,1)S(1)}, bf16[128,1024]{1,0:T(8,128)(2,1)S(1)}, u32[]{:S(2)}, u32[]{:S(2)}) collective-permute-start(bf16[128,1024]{1,0:T(8,128)(2,1)S(1)} %mix.8.refs_0_.mine), channel_id=1, source_target_pairs={{0,4},{1,5},{2,6},{3,7},{4,0},{5,1},{6,2},{7,3},{8,12},{9,13},{10,... | collective-permute-start | bytes 786440 | tf_op jit(solution)/shard_map/ppermute | solution.py:42
  37.3 16.8 %collective-permute-start.5 = (bf16[128,1024]{1,0:T(8,128)(2,1)S(1)}, bf16[128,1024]{1,0:T(8,128)(2,1)S(1)}, u32[]{:S(2)}, u32[]{:S(2)}) collective-permute-start(bf16[128,1024]{1,0:T(8,128)(2,1)S(1)} %mix.9.refs_0_.mine), channel_id=1, source_target_pairs={{0,4},{1,5},{2,6},{3,7},{4,0},{5,1},{6,2},{7,3},{8,12},{9,13},{10,... | collective-permute-start | bytes 786440 | tf_op jit(solution)/shard_map/ppermute | solution.py:42
  55.3 4.6 %collective-permute-start.8 = (f32[1,1024]{1,0:T(1,128)S(1)}, f32[1,1024]{1,0:T(1,128)S(1)}, u32[]{:S(2)}, u32[]{:S(2)}) collective-permute-start(f32[1,1024]{1,0:T(1,128)S(1)} %shard_map.79.refs_3_), channel_id=1, source_target_pairs={{0,8},{1,9},{2,10},{3,11},{4,12},{5,13},{6,14},{7,15},{8,0},{9,1},... | collective-permute-start | bytes 12296 | tf_op jit(solution)/shard_map/ppermute | solution.py:42
